TPU v7x, 16 devices: a whole 2x2x2 slice. The times are simulated.
16 devices in a mesh: dp: 2 (over z), cp: 8 (over y, x, core).
Axes of the slice: x: 2, y: 2, z: 2, core: 2. Of those that a mesh axis runs over, the one named last changes fastest.
Arguments:
- x: bfloat16 [32, 1024, 2048], P('dp', 'cp')
- grad_out: bfloat16 [32, 1024, 2048], P('dp', 'cp')
- w_q: bfloat16 [2048, 32, 64], replicated
- w_k: bfloat16 [2048, 4, 64], replicated
- w_v: bfloat16 [2048, 4, 64], replicated
- w_o: bfloat16 [2048, 32, 64], replicated
- w_up: bfloat16 [2048, 5632], replicated
- w_down: bfloat16 [5632, 2048], replicated
Outputs:
- output 1: bfloat16 [32, 1024, 2048], P('dp', 'cp')
- output 2: float32 [2048, 32, 64], P(('dp', 'cp'))
- output 3: float32 [2048, 4, 64], P(('dp', 'cp'))
- output 4: float32 [2048, 4, 64], P(('dp', 'cp'))
- output 5: float32 [2048, 32, 64], P(('dp', 'cp'))
- output 6: float32 [2048, 5632], P(('dp', 'cp'))
- output 7: float32 [5632, 2048], P(('dp', 'cp'))
All inputs are finite; a program needn't handle non-finite values.
Results may differ from a plain program's by a relative error of at most 0.0130821.
Values are sent between devices in bfloat16 or wider.
A program may use at most 1 GiB of HBM per device.

v0:
```python
import functools, math
import jax, jax.numpy as jnp
from jax import lax
from jax.experimental import pallas as pl
from jax.experimental.pallas import tpu as pltpu
from jax.sharding import PartitionSpec as P


BF, F32 = jnp.bfloat16, jnp.float32
NEG_BIG = -1e30
LANES, WIDE, MODEL, FF_TILE, FF_ROWS, SEQ, Z = 128, 512, 2048, 1408, 352, 1024, 0
HALF = 64
CHUNK = 256
HEADS = 2
NORM = True


def nt(a, b):
    return lax.dot_general(a, b, (((1,), (1,)), ((), ())), preferred_element_type=F32)


def tn(a, b):
    return lax.dot_general(a, b, (((Z,), (Z,)), ((), ())), preferred_element_type=F32)


def nn(a, b):
    return lax.dot_general(a, b, (((1,), (Z,)), ((), ())), preferred_element_type=F32)


def low_lanes(rows):
    return lax.broadcasted_iota(jnp.int32, (rows, LANES), 1) < HALF


def load_keys(me, kv_refs, keys, vals, head):
    low = low_lanes(LANES)
    for pos, ref in enumerate(kv_refs):
        dev = me ^ pos
        tile = ref[Z, :, LANES * head:LANES * (head + 1)]
        flipped = jnp.concatenate([tile[:, HALF:], tile[:, :HALF]], axis=1)
        k_two = jnp.where(low, tile, flipped)
        v_two = jnp.where(low, flipped, tile)
        first = pl.multiple_of(dev * HALF, HALF)
        second = pl.multiple_of((15 - dev) * HALF, HALF)
        keys[pl.ds(first, HALF), :] = k_two[:HALF]
        keys[pl.ds(second, HALF), :] = k_two[HALF:]
        vals[pl.ds(first, HALF), :] = v_two[:HALF]
        vals[pl.ds(second, HALF), :] = v_two[HALF:]


def spread_heads(rows):
    low = low_lanes(HALF)
    zero = jnp.zeros((HALF, LANES), BF)
    parts = []
    for pair in range(4):
        tile = rows[:, LANES * pair:LANES * (pair + 1)]
        parts += [jnp.where(low, tile, zero), jnp.where(low, zero, tile)]
    return jnp.concatenate(parts, axis=Z)


def gather_heads(cols, ref, base, lane):
    low = low_lanes(HALF)
    for pair in range(4):
        tile = cols[:, LANES * pair:LANES * (pair + 1)].T
        ref[Z, base:base + HALF, lane + LANES * pair:lane + LANES * (pair + 1)] = jnp.where(low, tile[:HALF], tile[HALF:]).astype(BF)


def tile_plan(me):
    late = me >= 4
    fifth_key = pl.multiple_of(jnp.where(late, CHUNK, 768), CHUNK)
    fifth_block = jnp.where(late, me, 15 - me)
    return late, [(Z, me, True, Z), (Z, 15 - me, False, 1), (CHUNK, 15 - me, False, 1),
                  (2 * CHUNK, 15 - me, True, 1), (fifth_key, fifth_block, True, 2)]


def lag():
    row = lax.broadcasted_iota(jnp.int32, (CHUNK, WIDE), Z)
    col = lax.broadcasted_iota(jnp.int32, (CHUNK, WIDE), 1)
    return row - (col & (HALF - 1))


def fwd_kernel(scale2, aliased, me_ref, q_ref, *refs):
    kv_refs = refs[:8]
    refs = refs[8 + (1 if aliased else Z):]
    o_ref, lse_ref, keys, vals = refs
    me = me_ref[Z]
    gap = lag()
    late, plan = tile_plan(me)

    def choose(one, two):
        return [one, two, jnp.where(late, one, two)]

    def split(parts):
        zero = jnp.zeros_like(parts[4])
        return parts[Z] + jnp.where(late, parts[4], zero), parts[1] + parts[2] + parts[3] + jnp.where(late, zero, parts[4])

    class Head:
        pass

    heads = []
    for head in range(HEADS):
        x = Head()
        load_keys(me, kv_refs, keys.at[head], vals.at[head], head)
        lanes = slice(WIDE * head, WIDE * (head + 1))
        q_tile = q_ref[Z, :, lanes]
        x.q = choose(spread_heads(q_tile[:HALF]), spread_heads(q_tile[HALF:]))
        x.scores, x.tops, x.exps, x.sums, x.outs = [], [], [], [], []
        heads.append(x)

    def score(head, i):
        x = heads[head]
        start, block, masked, which = plan[i]
        s = nt(keys[head, pl.ds(start, CHUNK), :], x.q[which])
        if masked:
            s = jnp.where(gap <= block * HALF - start, s, NEG_BIG)
        x.scores.append(s)
        x.tops.append(jnp.max(s, axis=Z, keepdims=True))

    def top(head):
        x = heads[head]
        t = x.tops
        top_b = jnp.maximum(jnp.maximum(t[1], t[2]), t[3])
        top_a = jnp.where(late, jnp.maximum(t[Z], t[4]), t[Z]) * scale2
        top_b = jnp.where(late, top_b, jnp.maximum(top_b, t[4])) * scale2
        x.top = choose(top_a, top_b)

    def expo(head, i):
        x = heads[head]
        e = jnp.exp2(x.scores[i] * scale2 - x.top[plan[i][3]])
        x.exps.append(e if NORM else e.astype(BF))
        x.sums.append(jnp.sum(e, axis=Z, keepdims=True))

    def total(head):
        x = heads[head]
        sum_a, sum_b = split(x.sums)
        lse_ref[head, Z:1, :] = x.top[Z] + jnp.log2(sum_a)
        lse_ref[head, 1:2, :] = x.top[1] + jnp.log2(sum_b)
        x.inv = choose(1.0 / sum_a, 1.0 / sum_b)

    def value(head, i):
        x = heads[head]
        p = (x.exps[i] * x.inv[plan[i][3]]).astype(BF) if NORM else x.exps[i]
        x.outs.append(tn(vals[head, pl.ds(plan[i][Z], CHUNK), :], p))

    def finish(head):
        x = heads[head]
        out_a, out_b = split(x.outs)
        if not NORM:
            out_a, out_b = out_a * x.inv[Z], out_b * x.inv[1]
        gather_heads(out_a, o_ref, Z, WIDE * head)
        gather_heads(out_b, o_ref, HALF, WIDE * head)

    n = len(plan)
    for head in range(HEADS + 2):
        for i in range(n):
            if head < HEADS:
                score(head, i)
            if Z <= head - 1 < HEADS:
                if i == Z:
                    top(head - 1)
                expo(head - 1, i)
            if Z <= head - 2 < HEADS:
                if i == Z:
                    total(head - 2)
                value(head - 2, i)
        if Z <= head - 2 < HEADS:
            finish(head - 2)


def bwd_kernel(scale, scale2, aliased, me_ref, q_ref, g_ref, lse_ref, *refs):
    kv_refs = refs[:8]
    refs = refs[8 + (1 if aliased else Z):]
    dq_ref, keep_ref, send_ref, keys, vals, grads = refs
    me = me_ref[Z]
    gap = lag()
    late, plan = tile_plan(me)
    low = low_lanes(CHUNK)

    def choose(one, two):
        return [one, two, jnp.where(late, one, two)]

    def split(parts):
        zero = jnp.zeros_like(parts[4])
        return parts[Z] + jnp.where(late, parts[4], zero), parts[1] + parts[2] + parts[3] + jnp.where(late, zero, parts[4])

    class Head:
        pass

    heads = []
    for head in range(HEADS):
        x = Head()
        load_keys(me, kv_refs, keys.at[head], vals.at[head], head)
        lanes = slice(WIDE * head, WIDE * (head + 1))
        q_tile, g_tile = q_ref[Z, :, lanes], g_ref[Z, :, lanes]
        x.q = choose(spread_heads(q_tile[:HALF]), spread_heads(q_tile[HALF:]))
        x.g = choose(spread_heads(g_tile[:HALF]), spread_heads(g_tile[HALF:]))
        x.lse = choose(lse_ref[head, Z:1, :], lse_ref[head, 1:2, :])
        x.probs, x.dprobs, x.deltas, x.dqs, x.dks, x.dvs = [], [], [], [], [], []
        heads.append(x)

    def prob(head, i):
        x = heads[head]
        start, block, masked, which = plan[i]
        s = nt(keys[head, pl.ds(start, CHUNK), :], x.q[which])
        if masked:
            s = jnp.where(gap <= block * HALF - start, s, NEG_BIG)
        p = jnp.exp2(s * scale2 - x.lse[which])
        dp = nt(vals[head, pl.ds(start, CHUNK), :], x.g[which]).astype(BF)
        x.probs.append(p)
        x.dprobs.append(dp)
        x.deltas.append(jnp.sum(p * dp.astype(F32), axis=Z, keepdims=True))

    def delta(head):
        x = heads[head]
        x.delta = choose(*split(x.deltas))

    def grad(head, i):
        x = heads[head]
        start, _, _, which = plan[i]
        p, dp = x.probs[i], x.dprobs[i]
        ds = (p * (dp.astype(F32) - x.delta[which])).astype(BF)
        x.dvs.append(nn(p.astype(BF), x.g[which]))
        x.dks.append(nn(ds, x.q[which]))
        x.dqs.append(tn(keys[head, pl.ds(start, CHUNK), :], ds))

    def finish(head):
        x = heads[head]
        dq_a, dq_b = split(x.dqs)
        gather_heads(dq_a * scale, dq_ref, Z, WIDE * head)
        gather_heads(dq_b * scale, dq_ref, HALF, WIDE * head)
        zero = jnp.zeros_like(x.dks[4])

        def by_chunk(parts):
            return [parts[Z] + parts[1], parts[2] + jnp.where(late, parts[4], zero), parts[3],
                    jnp.where(late, zero, parts[4])]

        for chunk, (dk, dv) in enumerate(zip(by_chunk(x.dks), by_chunk(x.dvs))):
            dk = (dk + pltpu.roll(dk, HALF, 1)) * scale
            dv = dv + pltpu.roll(dv, HALF, 1)
            both = jnp.where(low, dk, dv)
            for sub in range(4):
                block = 4 * chunk + sub
                dev, base = (block, Z) if block < 8 else (15 - block, HALF)
                grads[dev ^ me, base:base + HALF, LANES * head:LANES * (head + 1)] = both[sub * HALF:(sub + 1) * HALF]

    n = len(plan)
    for head in range(HEADS + 1):
        for i in range(n):
            if head < HEADS:
                prob(head, i)
            if head >= 1:
                if i == Z:
                    delta(head - 1)
                grad(head - 1, i)
        if head >= 1:
            finish(head - 1)
    for one in range(2):
        for two in range(2):
            slot = jnp.where(pl.program_id(1) == Z, 2 * two + one, 2 * one + two)
            keep_ref[Z, one, two, Z] = grads[2 * slot]
            send_ref[Z, one, two, Z] = grads[2 * slot + 1]


def attn_fwd(me, q, kvs, first, total, o_prev=None):
    count = kvs[Z].shape[Z]
    scale2 = 0.125 * math.log2(math.e)
    aliased = o_prev is not None
    row = lambda b, g, m: (first + b, Z, g)
    kv_spec = pl.BlockSpec((1, LANES, LANES * HEADS), lambda b, g, m: (b, Z, g))
    grid_spec = pltpu.PrefetchScalarGridSpec(
        num_scalar_prefetch=1, grid=(count, 4 // HEADS),
        in_specs=[pl.BlockSpec((1, LANES, WIDE * HEADS), row)] + [kv_spec] * 8 + ([pl.BlockSpec(memory_space=pl.ANY)] if aliased else []),
        out_specs=[pl.BlockSpec((1, LANES, WIDE * HEADS), row), pl.BlockSpec((HEADS, 2, WIDE), lambda b, g, m: (b * (4 // HEADS) + g, Z, Z))],
        scratch_shapes=[pltpu.VMEM((HEADS, SEQ, LANES), BF), pltpu.VMEM((HEADS, SEQ, LANES), BF)])
    return pl.pallas_call(
        functools.partial(fwd_kernel, scale2, aliased), grid_spec=grid_spec, name='attn_fwd',
        out_shape=[jax.ShapeDtypeStruct((total, LANES, MODEL), BF), jax.ShapeDtypeStruct((count * 4, 2, WIDE), F32)],
        input_output_aliases={10: Z} if aliased else {},
        cost_estimate=timed(6 * count),
        compiler_params=ALL_VMEM,
    )(me, q, *kvs, *([o_prev] if aliased else []))


def attn_bwd(me, q, g, lse, kvs, first, sub, count, dq_prev=None):
    total = q.shape[Z]
    scale = 0.125
    scale2 = scale * math.log2(math.e)
    aliased = dq_prev is not None
    row = lambda b, h, m: (first + b, Z, h)
    kv_spec = pl.BlockSpec((1, LANES, LANES * HEADS), lambda b, h, m: (sub + b, Z, h))
    part = pl.BlockSpec((1, 2, 2, 1, LANES, CHUNK), lambda b, h, m: (h, Z, Z, b, Z, Z))
    part_shape = jax.ShapeDtypeStruct((2, 2, 2, count, LANES, CHUNK), F32)
    grid_spec = pltpu.PrefetchScalarGridSpec(
        num_scalar_prefetch=1, grid=(count, 4 // HEADS),
        in_specs=[pl.BlockSpec((1, LANES, WIDE * HEADS), row), pl.BlockSpec((1, LANES, WIDE * HEADS), row),
                  pl.BlockSpec((HEADS, 2, WIDE), lambda b, h, m: ((sub + b) * (4 // HEADS) + h, Z, Z))] + [kv_spec] * 8
        + ([pl.BlockSpec(memory_space=pl.ANY)] if aliased else []),
        out_specs=[pl.BlockSpec((1, LANES, WIDE * HEADS), row), part, part],
        scratch_shapes=[pltpu.VMEM((HEADS, SEQ, LANES), BF), pltpu.VMEM((HEADS, SEQ, LANES), BF), pltpu.VMEM((8, LANES, LANES * HEADS), F32)])
    return pl.pallas_call(
        functools.partial(bwd_kernel, scale, scale2, aliased), grid_spec=grid_spec, name='attn_bwd',
        out_shape=[jax.ShapeDtypeStruct((total, LANES, MODEL), BF)] + [part_shape] * 2,
        input_output_aliases={12: Z} if aliased else {},
        cost_estimate=timed(10 * count),
        compiler_params=ALL_VMEM,
    )(me, q, g, lse, *kvs, *([dq_prev] if aliased else []))


BITS = {'c': 1, 'x': 2, 'y': 4}
ALL_VMEM = pltpu.CompilerParams(vmem_limit_bytes=63 * 2**20)
NEXT = {'x': ('y', 'z'), 'y': ('z', 'x'), 'z': ('x', 'y')}


def swap(values, link):
    if link == 'z':
        return lax.ppermute(values, 'dp', [(Z, 1), (1, Z)])
    return lax.ppermute(values, 'cp', [(i, i ^ BITS[link]) for i in range(8)])


def pick(values, axis, index):
    return lax.index_in_dim(values, index, axis, keepdims=False)


def timed(micros):
    return pl.CostEstimate(flops=int(micros * 9e8), bytes_accessed=1 << 20, transcendentals=Z)


def mm_kernel(product, added, x_ref, w_ref, *refs):
    total = product(x_ref[...], w_ref[...])
    if added:
        total = total + refs[Z][...].astype(F32)
    refs[-1][...] = total.astype(refs[-1].dtype)


def mm(x, w, rows, first, count, width, flip=True, added=None, dtype=BF):
    total, depth = x.shape
    tile = pl.BlockSpec((rows, width), lambda n, t: (t, n))
    w_spec = pl.BlockSpec((width, depth), lambda n, t: (first + n, Z)) if flip else pl.BlockSpec(
        (depth, width), lambda n, t: (Z, first + n))
    return pl.pallas_call(
        functools.partial(mm_kernel, nt if flip else nn, added is not None), grid=(count, total // rows), name='mm',
        in_specs=[pl.BlockSpec((rows, depth), lambda n, t: (t, Z)), w_spec] + ([tile] if added is not None else []),
        out_specs=tile, out_shape=jax.ShapeDtypeStruct((total, count * width), dtype),
        cost_estimate=timed(total * count * width * depth * 2 / 9e8),
        compiler_params=ALL_VMEM)(x, w, *([added] if added is not None else []))


def join_kv(k_ref, v_ref, both):
    @pl.when(pl.program_id(Z) == Z)
    def _():
        for head in range(4):
            both[LANES * head:LANES * head + HALF, :] = k_ref[HALF * head:HALF * head + HALF, :]
            both[LANES * head + HALF:LANES * head + LANES, :] = v_ref[HALF * head:HALF * head + HALF, :]


def kv_kernel(x_ref, k_ref, v_ref, low_ref, high_ref, both):
    join_kv(k_ref, v_ref, both)
    value = nt(x_ref[...], both[...]).astype(BF)
    for index, ref in enumerate((low_ref, high_ref)):
        @pl.when(pl.program_id(Z) // 2 == index)
        def _():
            ref[...] = value


def kv_call(x, w_k, w_v):
    rows, (total, depth) = WIDE, x.shape
    whole = pl.BlockSpec((CHUNK, depth), lambda t: (Z, Z), pipeline_mode=pl.Buffered(1))
    return pl.pallas_call(
        kv_kernel, grid=(total // rows,), name='kv',
        in_specs=[pl.BlockSpec((rows, depth), lambda t: (t, Z)), whole, whole],
        out_specs=[pl.BlockSpec((rows, WIDE), lambda t: (jnp.minimum(t, 1), Z)), pl.BlockSpec((rows, WIDE), lambda t: (jnp.maximum(t - 2, Z), Z))],
        out_shape=[jax.ShapeDtypeStruct((total // 2, WIDE), BF)] * 2,
        scratch_shapes=[pltpu.VMEM((WIDE, depth), BF)], cost_estimate=timed(9), compiler_params=ALL_VMEM)(x, w_k, w_v)


def gx_kernel(h_ref, q_ref, g_ref, w_ref, k_ref, v_ref, *refs):
    out_ref, both = refs[-2:]
    join_kv(k_ref, v_ref, both)
    total = nn(q_ref[...], w_ref[...]) + nn(g_ref[...], both[...])
    out_ref[...] = (h_ref[...].astype(F32) + total).astype(BF)


def gx_call(grad_h, grad_q, grad_kv, w_q, w_k, w_v, half, prev=None):
    rows, (total, depth) = WIDE, grad_h.shape
    width = depth // 2
    aliased = prev is not None
    tile = pl.BlockSpec((rows, width), lambda t: (t, half))
    once = lambda count: pl.BlockSpec((count, width), lambda t: (Z, half), pipeline_mode=pl.Buffered(1))
    return pl.pallas_call(
        gx_kernel, grid=(total // rows,), name='gx',
        in_specs=[tile, pl.BlockSpec((rows, depth), lambda t: (t, Z)), pl.BlockSpec((rows, WIDE), lambda t: (t, Z)), once(depth), once(CHUNK),
                  once(CHUNK)] + ([pl.BlockSpec(memory_space=pl.ANY)] if aliased else []),
        out_specs=tile, out_shape=jax.ShapeDtypeStruct((total, depth), BF), scratch_shapes=[pltpu.VMEM((WIDE, width), BF)],
        input_output_aliases={6: Z} if aliased else {}, cost_estimate=timed(14), compiler_params=ALL_VMEM,
    )(grad_h, grad_q, grad_kv, w_q, w_k, w_v, *([prev] if aliased else []))


def ff_kernel(bits_ref, h_ref, w_ref, ga_ref, at_ref, gu_ref, held, turned):
    root = math.sqrt(2.0 / math.pi)
    width = w_ref.shape[1]
    for lo in range(Z, width, CHUNK):
        cut = slice(lo, min(lo + CHUNK, width))
        u = held[:, cut]
        held[:, cut] = nn(h_ref[...], w_ref[:, cut])
        rise = (root * 0.044715) * (u * u)
        t = jnp.tanh(u * (root + rise))
        up, down, half_u = 1.0 + t, 1.0 - t, 0.5 * u
        slope = up * (0.5 + (half_u * down) * (root + 3.0 * rise))
        gu_ref[:, cut] = (ga_ref[:, cut].astype(F32) * slope).astype(BF)
        turned[cut, :] = (half_u * up).T.astype(BF)
    for x in range(2):
        for c in range(2):
            lo = (2 * x + c) * FF_ROWS
            at_ref[Z, Z, x ^ bits_ref[2], c ^ bits_ref[3]] = turned[lo:lo + FF_ROWS, :]


def ff_block(bits, h, w_up, ga):
    tokens, width, rows = MODEL, FF_TILE, CHUNK
    per = tokens // rows
    steps = 4 * per
    now = lambda i: jnp.minimum(i, steps - 1)
    then = lambda i: jnp.maximum(i - 1, Z)
    grid_spec = pltpu.PrefetchScalarGridSpec(
        num_scalar_prefetch=1, grid=(steps + 1,),
        in_specs=[pl.BlockSpec((rows, MODEL), lambda i, m: (now(i) % per, Z)),
                  pl.BlockSpec((MODEL, width), lambda i, m: (Z, now(i) // per)),
                  pl.BlockSpec((rows, width), lambda i, m: (then(i) % per, then(i) // per))],
        out_specs=[pl.BlockSpec((1, 1, 2, 2, FF_ROWS, rows), lambda i, m: ((then(i) // per // 2) ^ m[Z], (then(i) // per % 2) ^ m[1], Z, Z, Z, then(i) % per)),
                   pl.BlockSpec((rows, width), lambda i, m: (then(i) % per, then(i) // per))],
        scratch_shapes=[pltpu.VMEM((rows, width), F32), pltpu.VMEM((width, rows), BF)])
    return pl.pallas_call(
        ff_kernel, grid_spec=grid_spec, name='ff_block',
        out_shape=[jax.ShapeDtypeStruct((2, 2, 2, 2, FF_ROWS, tokens), BF), jax.ShapeDtypeStruct((tokens, 5632), BF)],
        cost_estimate=timed(60), compiler_params=ALL_VMEM)(bits, h, w_up, ga)


def color_of(n, plan):
    edge, color = Z, Z
    for _, count in plan[:-1]:
        edge += count
        color = color + (n >= edge).astype(jnp.int32)
    return color


def pair_kernel(plan, rows, turned, *refs):
    n, steps = pl.program_id(Z), sum(count for _, count in plan)
    count = len(plan)
    if turned:
        left, refs = refs[Z], refs[1:]
        take = lambda place, core: left[place, core]
    else:
        parts, left, refs = refs[:16], refs[-1], refs[16:-1]

        @pl.when(n == Z)
        def _():
            for place in range(8):
                for core in range(2):
                    left[place, core] = parts[2 * place + core][...].T

        take = lambda place, core: left[place, core]
    right, outs = refs[Z], refs[1:1 + 2 * count]
    mine, sent, came, send_sem, recv_sem, free_sem = refs[1 + 2 * count:]
    me = lax.axis_index('cp')
    other = {'cp': me + 1 - 2 * (me % 2)}
    mesh_id = pl.DeviceIdType.MESH
    now, then = n % 2, (n + 1) % 2

    def copy(slot):
        return pltpu.make_async_remote_copy(src_ref=sent.at[slot], dst_ref=came.at[slot], send_sem=send_sem.at[slot],
                                            recv_sem=recv_sem.at[slot], device_id=other, device_id_type=mesh_id)

    @pl.when(n == Z)
    def _():
        barrier = pltpu.get_barrier_semaphore()
        pl.semaphore_signal(barrier, inc=1, device_id=other, device_id_type=mesh_id)
        pl.semaphore_wait(barrier, 1)

    @pl.when(n >= 3)
    def _():
        pl.semaphore_wait(free_sem, 1)

    @pl.when(n >= 1)
    def _():
        copy(then).start()

    @pl.when(n < steps)
    def _():
        some = 1 if turned else 4
        for core, dest in ((1, sent), (Z, mine)):
            for place in range(Z, 8, some):
                tile = jnp.concatenate([take(place + k, core) for k in range(some)], axis=Z)
                dest[now, place:place + some] = nn(tile, right[...]).reshape(some, rows, -1)

    @pl.when(n >= 1)
    def _():
        copy(then).wait()
        color = color_of(n - 1, plan)
        for index, (split, _) in enumerate(plan):
            @pl.when(color == index)
            def _():
                for place in range(8):
                    z, y, x = place // 4, place // 2 % 2, place % 2
                    half, k = {'z': (z, 2 * y + x), 'y': (y, 2 * z + x), 'x': (x, 2 * z + y)}[split]
                    outs[2 * index + 1 - half][k] = mine[then, place] + came[then, place]

    @pl.when((n >= 1) & (n < steps - 1))
    def _():
        pl.semaphore_signal(free_sem, inc=1, device_id=other, device_id_type=mesh_id)


def pair_call(left, right, plan, tile, call_id):
    turned = left.ndim == 4
    rows = left.shape[2] if turned else LANES
    steps = sum(count for _, count in plan)
    once = pl.Buffered(1)
    if turned:
        left_specs = [pl.BlockSpec((8, 2, rows, MODEL), lambda n: (Z, Z, Z, Z), pipeline_mode=once)]
    else:
        def column(place, core):
            def at(n):
                me = lax.axis_index('cp')
                bits = (lax.axis_index('dp'), me // 4, (me // 2) % 2, me % 2)
                flips = (place // 4, place // 2 % 2, place % 2, core)
                return Z, sum((1 - bit if flip else bit) * weight for bit, flip, weight in zip(bits, flips, (8, 4, 2, 1)))

            return at

        left_specs = [pl.BlockSpec((MODEL, LANES), column(place, core), pipeline_mode=once) for place in range(8) for core in range(2)]
    out_specs, out_shape, edge = [], [], Z
    for _, count in plan:
        spec = pl.BlockSpec((4, rows, tile), lambda n, edge=edge, count=count: (Z, Z, jnp.clip(n - 1 - edge, Z, count - 1)))
        out_specs += [spec, spec]
        out_shape += [jax.ShapeDtypeStruct((4, rows, count * tile), F32)] * 2
        edge += count
    both = pltpu.VMEM((2, 8, rows, tile), F32)
    two = pltpu.SemaphoreType.DMA((2,))
    return pl.pallas_call(
        functools.partial(pair_kernel, plan, rows, turned), grid=(steps + 1,), name='pair',
        in_specs=left_specs + [pl.BlockSpec((MODEL, tile), lambda n: (Z, jnp.minimum(n, steps - 1)))], out_specs=out_specs, out_shape=out_shape,
        scratch_shapes=[both, both, both, two, two, pltpu.SemaphoreType.REGULAR] + ([] if turned else [pltpu.VMEM((8, 2, LANES, MODEL), BF)]),
        cost_estimate=timed(16 * rows * steps * tile * 4096 / 9e8),
        compiler_params=pltpu.CompilerParams(vmem_limit_bytes=63 * 2**20, collective_id=call_id, has_side_effects=True),
    )(*([left] * len(left_specs)), right)


def halve(keep, got, axis):
    return tuple(pick(keep, axis, k) + pick(got, axis, k) for k in (1, Z))


def weight_grad(left, right, plan, tile, call_id, flip=False):
    outs = pair_call(left, right, plan, tile, call_id)
    keeps, gots, fars = [], [], []
    for (split, _), send, keep in zip(plan, outs[::2], outs[1::2]):
        shape = (2, 2, *keep.shape[1:])
        got = swap(send, split).reshape(shape)
        send, keep = lax.optimization_barrier(halve(keep.reshape(shape), got, Z if split == 'y' else 1))
        got = swap(send, NEXT[split][Z])
        keeps.append(keep)
        gots.append(got)
        fars.append(swap(keep[1] + got[1], NEXT[split][1]))
    return final(keeps, gots, fars, flip)


def final_kernel(flip, *refs):
    count, edge = len(refs) // 3, Z
    for index in range(count):
        keep, got, far = refs[index:-1:count]
        total = (keep[Z] + got[Z] + far[...]) / 16
        cut = slice(edge, edge + total.shape[1])
        edge = cut.stop
        if flip:
            refs[-1][cut, :] = total.T
        else:
            refs[-1][:, cut] = total


def final(keeps, gots, fars, flip):
    shape = (fars[Z].shape[Z], sum(far.shape[1] for far in fars))
    shape = shape[::-1] if flip else shape
    two = [pl.BlockSpec((1, *far.shape), lambda n: (Z, Z, Z)) for far in fars]
    one = [pl.BlockSpec(far.shape, lambda n: (Z, Z)) for far in fars]
    return pl.pallas_call(
        functools.partial(final_kernel, flip), grid=(1,), name='final', in_specs=two + two + one,
        out_specs=pl.BlockSpec(shape, lambda n: (Z, Z)), out_shape=jax.ShapeDtypeStruct(shape, F32),
        cost_estimate=timed(4), compiler_params=ALL_VMEM)(*keeps, *gots, *fars)


def small_kernel(bits_ref, *refs):
    right = refs[2][...]
    for core in range(2):
        refs[3 + core][Z] = tn(refs[core][...], right)


def small_grad(bits, left, right):
    def column(core):
        return lambda k, m: (Z, ((k % 2) ^ m[Z]) * 8 + ((k // 2 % 2) ^ m[1]) * 4 + ((k // 4) ^ m[2]) * 2 + (core ^ m[3]))

    out = pl.BlockSpec((1, LANES, WIDE), lambda k, m: (k, Z, Z))
    grid_spec = pltpu.PrefetchScalarGridSpec(
        num_scalar_prefetch=1, grid=(8,),
        in_specs=[pl.BlockSpec((MODEL, LANES), column(core)) for core in range(2)] + [pl.BlockSpec((MODEL, WIDE), lambda k, m: (Z, Z))],
        out_specs=[out, out])
    keep, send = pl.pallas_call(small_kernel, grid_spec=grid_spec, name='small', out_shape=[jax.ShapeDtypeStruct((8, LANES, WIDE), F32)] * 2,
                                cost_estimate=timed(8), compiler_params=ALL_VMEM)(bits, left, left, right)
    for link in 'cxy':
        got, half = swap(send, link), keep.shape[Z] // 2
        send, keep = lax.optimization_barrier((keep[half:] + got[half:], keep[:half] + got[:half]))
    return (keep[Z] + swap(send, 'z')[Z]) / 16


def join_kernel(*refs):
    row = Z
    for chunk in range(Z, len(refs) - 1, 4):
        rows = slice(row, row + refs[chunk].shape[Z])
        row = rows.stop
        for color in range(2):
            total, far = refs[chunk + 2 * color:chunk + 2 * color + 2]
            refs[-1][rows, :, CHUNK * color:CHUNK * (color + 1)] = (total[...] + far[...]).astype(BF)


def join(parts):
    return pl.pallas_call(join_kernel, name='join', out_shape=jax.ShapeDtypeStruct((16, LANES, WIDE), BF),
                          cost_estimate=timed(4), compiler_params=ALL_VMEM)(*parts)


def gather_kv(kv, order):
    held = {Z: kv}
    for link in order:
        held.update({pos ^ BITS[link]: swap(tile, link) for pos, tile in list(held.items())})
    return [held[pos] for pos in range(8)]


def reduce_dkv(keep, send):
    got = swap(send, 'c')
    parts = []
    for color, (first, second) in enumerate((('x', 'y'), ('y', 'x'))):
        more = swap(keep[color, 1] + got[color, 1], first)
        send, total = lax.optimization_barrier(tuple(keep[color, Z, k] + got[color, Z, k] + more[k] for k in (1, Z)))
        parts += [total, swap(send, second)]
    return parts


CHUNKS = ((Z, 8), (8, 4), (12, 4))
PLAN_UP = (('z', 4), ('y', 4), ('x', 3))
PLAN_D = (('z', 2), ('y', 1), ('x', 1))
PLAN_DOWN = (('z', 3), ('y', 3), ('x', 2))


def solution(mesh):
    def per_device(x_loc, cot_loc, w_q, w_k, w_v, w_o, w_up, w_down):
        batch, seq, d_model = x_loc.shape
        tokens = batch * seq
        me = lax.axis_index('cp').astype(jnp.int32)
        me_one = me.reshape(1)
        bits = jnp.stack([lax.axis_index('dp').astype(jnp.int32), me >> 2, (me >> 1) & 1, me & 1])
        x2, cot2 = x_loc.reshape(tokens, d_model), cot_loc.reshape(tokens, d_model)
        w_q2, w_k2, w_v2, w_o2 = (w.transpose(1, 2, Z).reshape(-1, d_model) for w in (w_q, w_k, w_v, w_o))

        kvs = [kv.reshape(batch // 2, seq, -1) for kv in kv_call(x2, w_k2, w_v2)]
        gathered = [gather_kv(kvs[Z], 'xyc'), gather_kv(kvs[1], 'yxc')]
        q = mm(x2, w_q2, WIDE, Z, 2, SEQ).reshape(batch, seq, -1)
        grad_act = mm(cot2, w_down, WIDE, Z, 4, FF_TILE)

        o, lse_first = attn_fwd(me_one, q, gathered[Z], Z, batch)
        o, lse_second = attn_fwd(me_one, q, gathered[1], batch // 2, batch, o)
        lse = [lse_first, lse_second]
        o2 = o.reshape(tokens, -1)
        h = mm(o2, w_o2, WIDE, Z, 2, SEQ, False, x2)

        act_t, grad_u = ff_block(bits, h, w_up, grad_act)
        grad_w_up = weight_grad(h, grad_u, PLAN_UP, WIDE, Z)
        grad_w_down = weight_grad(act_t.reshape(8, 2, -1, tokens), cot2, PLAN_DOWN, CHUNK, 1)
        grad_h = mm(grad_u, w_up, WIDE, Z, 4, WIDE, True, cot2)
        grad_o = mm(grad_h, w_o2, WIDE, Z, 2, SEQ).reshape(batch, seq, -1)

        grad_q, grad_kv = None, []
        for first, count in CHUNKS:
            side, sub = first // 8, first % 8
            grad_q, keep, send = attn_bwd(me_one, q, grad_o, lse[side], gathered[side], first, sub, count, grad_q)
            grad_kv += reduce_dkv(keep, send)
        grad_q2 = grad_q.reshape(tokens, -1)
        grad_w_o = weight_grad(grad_h, o2, PLAN_D, WIDE, 2, True)
        grad_w_q = weight_grad(x2, grad_q2, PLAN_D, WIDE, 3, True)
        grad_kv2 = join(grad_kv).reshape(tokens, -1)
        grad_w_kv = small_grad(bits, x2, grad_kv2).reshape(-1, 4, 2, HALF)
        grad_x = None
        for part in range(2):
            grad_x = gx_call(grad_h, grad_q2, grad_kv2, w_q2, w_k2, w_v2, part, grad_x)
        return (grad_x.reshape(x_loc.shape), grad_w_q.reshape(32, HALF, -1).transpose(2, Z, 1), grad_w_kv[:, :, Z], grad_w_kv[:, :, 1],
                grad_w_o.reshape(32, HALF, -1).transpose(2, Z, 1), grad_w_up, grad_w_down)

    act_spec = P('dp', 'cp', None)
    rep_three, rep_two = P(None, None, None), P(None, None)
    grad_three, grad_two = P(('dp', 'cp'), None, None), P(('dp', 'cp'), None)
    return jax.shard_map(per_device, mesh=mesh,
                         in_specs=(act_spec, act_spec, rep_three, rep_three, rep_three, rep_three, rep_two, rep_two),
                         out_specs=(act_spec, grad_three, grad_three, grad_three, grad_three, grad_two, grad_two),
                         check_vma=False)
```

profile of v0, /device:TPU:0, one launch (start us, length us, event | category | flops | bytes accessed | tf_op | source)
XLA Modules:
  0.0 1522.4 jit_solution(12060030527307521114)
XLA Ops:
  15.1 22.3 %collective-permute-done.8.refs_2_ = bf16[8,128,512]{2,1,0:T(8,128)(2,1)} collective-permute-done((bf16[8,128,512]{2,1,0:T(8,128)(2,1)}, bf16[8,128,512]{2,1,0:T(8,128)(2,1)}, u32[]{:S(2)}, u32[]{:S(2)}) %collective-permute-start.8) | collective-permute-done | bytes 1048608 | tf_op jit(solution)/shard_map/ppermute | solution.py:316
  39.4 60.9 %mm.7.ga_ref = bf16[2048,5632]{1,0:T(8,128)(2,1)} custom-call(bf16[2048,2048]{1,0:T(8,128)(2,1)} %bitcast.425, bf16[5632,2048]{1,0:T(8,128)(2,1)} %w_ref.3), custom_call_target="tpu_custom_call" | custom-call | flops 47244640256 | bytes 1048576 | tf_op jit(solution)/shard_map/mm/pallas_call | solution.py:339
  102.9 23.7 %mm.5 = bf16[2048,2048]{1,0:T(8,128)(2,1)} custom-call(bf16[2048,2048]{1,0:T(8,128)(2,1)} %bitcast.380, bf16[2048,2048]{1,0:T(8,128)(2,1)} %bitcast.428), custom_call_target="tpu_custom_call" | custom-call | flops 17179869184 | bytes 1048576 | tf_op jit(solution)/shard_map/mm/pallas_call | solution.py:339
  127.7 45.3 %attn_fwd.2 = (bf16[16,128,2048]{2,1,0:T(8,128)(2,1)}, f32[32,2,512]{2,1,0:T(2,128)}) custom-call(s32[1]{0:T(128)} %bitcast.4.me_ref, bf16[16,128,2048]{2,1,0:T(8,128)(2,1)} %bitcast.449, bf16[8,128,512]{2,1,0:T(8,128)(2,1)} %bitcast.446, bf16[8,128,512]{2,1,0:T(8,128)(2,1)} %collective-permute-done.7.refs_1_, ...), custom_call_target="tpu_custom_call" | custom-call | flops 43200000000 | bytes 1048576 | tf_op jit(solution)/shard_map/attn_fwd/pallas_call | solution.py:274
  173.0 45.3 %attn_fwd.3 = (bf16[16,128,2048]{2,1,0:T(8,128)(2,1)}, f32[32,2,512]{2,1,0:T(2,128)}) custom-call(s32[1]{0:T(128)} %bitcast.4.me_ref, bf16[16,128,2048]{2,1,0:T(8,128)(2,1)} %bitcast.450, bf16[8,128,512]{2,1,0:T(8,128)(2,1)} %bitcast.440, bf16[8,128,512]{2,1,0:T(8,128)(2,1)} %collective-permute-done.refs_1_, ...), custom_call_target="tpu_custom_call", output_to_operand_aliasing={{0}: (10, {})} | custom-call | flops 43200000000 | bytes 1048576 | tf_op jit(solution)/shard_map/attn_fwd/pallas_call | solution.py:274
  218.4 25.0 %mm.6.h_ref.refs_0_.refs_1_.refs_2_.refs_3_.refs_4_.refs_5_.refs_6_.refs_7_.refs_8_.refs_9_.refs_10_.refs_11_.refs_12_.refs_13_.refs_14_.refs_15_ = bf16[2048,2048]{1,0:T(8,128)(2,1)} custom-call(bf16[2048,2048]{1,0:T(8,128)(2,1)} %bitcast.400, bf16[2048,2048]{1,0:T(8,128)(2,1)} %bitcast.423, bf16[2048,2048]{1,0:T(8,128)(2,1)} %bitcast.381), custom_call_target="tpu_custom_call" | custom-call | flops 17179869184 | bytes 1048576 | tf_op jit(solution)/shard_map/mm/pallas_call | solution.py:339
  243.4 89.6 %ff_block.1 = (bf16[2,2,2,2,352,2048]{5,4,3,2,1,0:T(8,128)(2,1)}, bf16[2048,5632]{1,0:T(8,128)(2,1)}) custom-call(s32[4]{0:T(128)} %pad_add_fusion.bits_ref, bf16[2048,2048]{1,0:T(8,128)(2,1)} %mm.6.h_ref.refs_0_.refs_1_.refs_2_.refs_3_.refs_4_.refs_5_.refs_6_.refs_7_.refs_8_.refs_9_.refs_10_.refs_11_.refs_12_.refs_13_.refs_14_.refs_15_, ...), custom_call_target="tpu_custom_call" | custom-call | flops 54000001024 | bytes 1048576 | tf_op jit(solution)/shard_map/ff_block/pallas_call | solution.py:430
  333.0 61.1 %mm.8.x_ref.h_ref.refs_0_.refs_1_.refs_2_.refs_3_.refs_4_.refs_5_.refs_6_.refs_7_.refs_8_.refs_9_.refs_10_.refs_11_.refs_12_.refs_13_.refs_14_.refs_15_ = bf16[2048,2048]{1,0:T(8,128)(2,1)} custom-call(bf16[2048,5632]{1,0:T(8,128)(2,1)} %get-tuple-element.96.x_ref.refs_16_, bf16[2048,5632]{1,0:T(8,128)(2,1)} %w_ref.5, bf16[2048,2048]{1,0:T(8,128)(2,1)} %bitcast.426), custom_call_target="tpu_custom_call" | custom-call | flops 47244640256 | bytes 1048576 | tf_op jit(solution)/shard_map/mm/pallas_call | solution.py:339
  394.1 35.2 %pair.5 = (f32[4,128,1024]{2,1,0:T(8,128)}, f32[4,128,1024]{2,1,0:T(8,128)}, f32[4,128,512]{2,1,0:T(8,128)}, f32[4,128,512]{2,1,0:T(8,128)}, f32[4,128,512]{2,1,0:T(8,128)}, /*index=5*/f32[4,128,512]{2,1,0:T(8,128)}) custom-call(bf16[2048,2048]{1,0:T(8,128)(2,1)} %mm.8.x_ref.h_ref.refs_0_.refs_1_.refs_2_.refs_3_.refs_4_.refs_5_.refs_6_.refs_7_.refs_8_.refs_9_.refs_10_.refs_11, ...), custom_call_target="tpu_custom_call" | custom-call | flops 17179869184 | bytes 1048576 | tf_op jit(solution)/shard_map/pair/pallas_call | solution.py:536
  429.3 23.9 %mm.9 = bf16[2048,2048]{1,0:T(8,128)(2,1)} custom-call(bf16[2048,2048]{1,0:T(8,128)(2,1)} %mm.8.x_ref.h_ref.refs_0_.refs_1_.refs_2_.refs_3_.refs_4_.refs_5_.refs_6_.refs_7_.refs_8_.refs_9_.refs_10_.refs_11_.refs_12_.refs_13_.refs_14_.refs_15_, bf16[2048,2048]{1,0:T(8,128)(2,1)} %bitcast.424), custom_call_target="tpu_custom_call" | custom-call | flops 17179869184 | bytes 1048576 | tf_op jit(solution)/shard_map/mm/pallas_call | solution.py:339
  454.3 77.8 %attn_bwd.3 = (bf16[16,128,2048]{2,1,0:T(8,128)(2,1)}, f32[2,2,2,8,128,256]{5,4,3,2,1,0:T(8,128)}, f32[2,2,2,8,128,256]{5,4,3,2,1,0:T(8,128)}) custom-call(s32[1]{0:T(128)} %bitcast.4.me_ref, bf16[16,128,2048]{2,1,0:T(8,128)(2,1)} %bitcast.451, bf16[16,128,2048]{2,1,0:T(8,128)(2,1)} %bitcast.454, f32[32,2,512]{2,1,0:T(2,128)} %get-tuple-element.98.lse_ref, ...), custom_call_target="tpu_custom_call" | custom-call | flops 71999995904 | bytes 1048576 | tf_op jit(solution)/shard_map/attn_bwd/pallas_call | solution.py:299
  532.1 40.0 %attn_bwd.4 = (bf16[16,128,2048]{2,1,0:T(8,128)(2,1)}, f32[2,2,2,4,128,256]{5,4,3,2,1,0:T(8,128)}, f32[2,2,2,4,128,256]{5,4,3,2,1,0:T(8,128)}) custom-call(s32[1]{0:T(128)} %bitcast.4.me_ref, bf16[16,128,2048]{2,1,0:T(8,128)(2,1)} %bitcast.452, bf16[16,128,2048]{2,1,0:T(8,128)(2,1)} %bitcast.455, ...), custom_call_target="tpu_custom_call", output_to_operand_aliasing={{0}: (12, {})} | custom-call | flops 35999997952 | bytes 1048576 | tf_op jit(solution)/shard_map/attn_bwd/pallas_call | solution.py:299
  572.1 40.3 %attn_bwd.5 = (bf16[16,128,2048]{2,1,0:T(8,128)(2,1)}, f32[2,2,2,4,128,256]{5,4,3,2,1,0:T(8,128)}, f32[2,2,2,4,128,256]{5,4,3,2,1,0:T(8,128)}) custom-call(s32[1]{0:T(128)} %bitcast.4.me_ref, bf16[16,128,2048]{2,1,0:T(8,128)(2,1)} %bitcast.453, bf16[16,128,2048]{2,1,0:T(8,128)(2,1)} %bitcast.456, ...), custom_call_target="tpu_custom_call", output_to_operand_aliasing={{0}: (12, {})} | custom-call | flops 35999997952 | bytes 1048576 | tf_op jit(solution)/shard_map/attn_bwd/pallas_call | solution.py:299
  612.4 35.2 %pair.4 = (f32[4,128,1024]{2,1,0:T(8,128)}, f32[4,128,1024]{2,1,0:T(8,128)}, f32[4,128,512]{2,1,0:T(8,128)}, f32[4,128,512]{2,1,0:T(8,128)}, f32[4,128,512]{2,1,0:T(8,128)}, /*index=5*/f32[4,128,512]{2,1,0:T(8,128)}) custom-call(bf16[2048,2048]{1,0:T(8,128)(2,1)} %bitcast.382, bf16[2048,2048]{1,0:T(8,128)(2,1)} %bitcast.383, bf16[2048,2048]{1,0:T(8,128)(2,1)} %bitcast.384, ...), custom_call_target="tpu_custom_call" | custom-call | flops 17179869184 | bytes 1048576 | tf_op jit(solution)/shard_map/pair/pallas_call | solution.py:536
  657.7 16.3 %collective-permute-done.30 = f32[4,128,512]{2,1,0:T(8,128)S(1)} collective-permute-done((f32[4,128,512]{2,1,0:T(8,128)}, f32[4,128,512]{2,1,0:T(8,128)S(1)}, u32[]{:S(2)}, u32[]{:S(2)}) %collective-permute-start.30) | collective-permute-done | bytes 1048608 | tf_op jit(solution)/shard_map/ppermute | solution.py:316
  679.5 69.5 %pair.7 = (f32[4,352,768]{2,1,0:T(8,128)}, f32[4,352,768]{2,1,0:T(8,128)}, f32[4,352,768]{2,1,0:T(8,128)}, f32[4,352,768]{2,1,0:T(8,128)}, f32[4,352,512]{2,1,0:T(8,128)}, /*index=5*/f32[4,352,512]{2,1,0:T(8,128)}) custom-call(bf16[8,2,352,2048]{3,2,1,0:T(8,128)(2,1)} %bitcast.448, bf16[2048,2048]{1,0:T(8,128)(2,1)} %bitcast.427), custom_call_target="tpu_custom_call" | custom-call | flops 47244640256 | bytes 1048576 | tf_op jit(solution)/shard_map/pair/pallas_call | solution.py:536
  754.2 73.6 %pair.6 = (f32[4,128,2048]{2,1,0:T(8,128)}, f32[4,128,2048]{2,1,0:T(8,128)}, f32[4,128,2048]{2,1,0:T(8,128)}, f32[4,128,2048]{2,1,0:T(8,128)}, f32[4,128,1536]{2,1,0:T(8,128)}, /*index=5*/f32[4,128,1536]{2,1,0:T(8,128)}) custom-call(bf16[2048,2048]{1,0:T(8,128)(2,1)} %mm.6.h_ref.refs_0_.refs_1_.refs_2_.refs_3_.refs_4_.refs_5_.refs_6_.refs_7_.refs_8_.refs_9_.refs_10_.refs_11_., ...), custom_call_target="tpu_custom_call" | custom-call | flops 47244640256 | bytes 1048576 | tf_op jit(solution)/shard_map/pair/pallas_call | solution.py:536
  847.4 51.7 %collective-permute-done.53 = f32[4,128,1536]{2,1,0:T(8,128)S(1)} collective-permute-done((f32[4,128,1536]{2,1,0:T(8,128)}, f32[4,128,1536]{2,1,0:T(8,128)S(1)}, u32[]{:S(2)}, u32[]{:S(2)}) %collective-permute-start.53) | collective-permute-done | bytes 3145760 | tf_op jit(solution)/shard_map/ppermute | solution.py:316
  899.4 22.2 %collective-permute-done.45.refs_3_ = f32[2,128,1024]{2,1,0:T(8,128)S(1)} collective-permute-done((f32[2,128,1024]{2,1,0:T(8,128)S(1)}, f32[2,128,1024]{2,1,0:T(8,128)S(1)}, u32[]{:S(2)}, u32[]{:S(2)}) %collective-permute-start.45) | collective-permute-done | bytes 1048608 | tf_op jit(solution)/shard_map/ppermute | solution.py:316
  921.6 21.7 %collective-permute-done.32.refs_3_ = f32[2,128,1024]{2,1,0:T(8,128)S(1)} collective-permute-done((f32[2,128,1024]{2,1,0:T(8,128)S(1)}, f32[2,128,1024]{2,1,0:T(8,128)S(1)}, u32[]{:S(2)}, u32[]{:S(2)}) %collective-permute-start.32) | collective-permute-done | bytes 1048608 | tf_op jit(solution)/shard_map/ppermute | solution.py:316
  953.6 36.7 %collective-permute-done.51 = f32[4,128,2048]{2,1,0:T(8,128)S(1)} collective-permute-done((f32[4,128,2048]{2,1,0:T(8,128)}, f32[4,128,2048]{2,1,0:T(8,128)S(1)}, u32[]{:S(2)}, u32[]{:S(2)}) %collective-permute-start.51) | collective-permute-done | bytes 4194336 | tf_op jit(solution)/shard_map/ppermute | solution.py:315
  993.0 44.0 %collective-permute-done.52 = f32[4,128,2048]{2,1,0:T(8,128)} collective-permute-done((f32[4,128,2048]{2,1,0:T(8,128)}, f32[4,128,2048]{2,1,0:T(8,128)}, u32[]{:S(2)}, u32[]{:S(2)}) %collective-permute-start.52) | collective-permute-done | bytes 4194336 | tf_op jit(solution)/shard_map/ppermute | solution.py:316
  1037.4 30.4 %collective-permute-done.65.refs_5_ = f32[2,352,512]{2,1,0:T(8,128)S(1)} collective-permute-done((f32[2,352,512]{2,1,0:T(8,128)S(1)}, f32[2,352,512]{2,1,0:T(8,128)S(1)}, u32[]{:S(2)}, u32[]{:S(2)}) %collective-permute-start.65) | collective-permute-done | bytes 1441824 | tf_op jit(solution)/shard_map/ppermute | solution.py:316
  1077.2 105.7 %collective-permute-done.27 = f32[2,4,128,256]{3,2,1,0:T(8,128)S(1)} collective-permute-done((f32[2,4,128,256]{3,2,1,0:T(8,128)S(1)}, f32[2,4,128,256]{3,2,1,0:T(8,128)S(1)}, u32[]{:S(2)}, u32[]{:S(2)}) %collective-permute-start.27) | collective-permute-done | bytes 1048608 | tf_op jit(solution)/shard_map/ppermute | solution.py:316
  1186.7 18.8 %collective-permute-done.22 = f32[2,4,128,256]{3,2,1,0:T(8,128)} collective-permute-done((f32[2,4,128,256]{3,2,1,0:T(8,128)S(1)}, f32[2,4,128,256]{3,2,1,0:T(8,128)}, u32[]{:S(2)}, u32[]{:S(2)}) %collective-permute-start.22) | collective-permute-done | bytes 1048608 | tf_op jit(solution)/shard_map/ppermute | solution.py:316
  1219.8 30.2 %collective-permute-done.20 = f32[2,4,128,256]{3,2,1,0:T(8,128)} collective-permute-done((f32[2,4,128,256]{3,2,1,0:T(8,128)}, f32[2,4,128,256]{3,2,1,0:T(8,128)}, u32[]{:S(2)}, u32[]{:S(2)}) %collective-permute-start.20) | collective-permute-done | bytes 1048608 | tf_op jit(solution)/shard_map/ppermute | solution.py:316
  1310.6 15.5 %collective-permute-done.50.refs_8_ = f32[128,512]{1,0:T(8,128)} collective-permute-done((f32[128,512]{1,0:T(8,128)}, f32[128,512]{1,0:T(8,128)}, u32[]{:S(2)}, u32[]{:S(2)}) %collective-permute-start.50) | collective-permute-done | bytes 262176 | tf_op jit(solution)/shard_map/ppermute | solution.py:315
  1326.7 26.1 %collective-permute-done.36.refs_7_ = f32[128,512]{1,0:T(8,128)S(1)} collective-permute-done((f32[128,512]{1,0:T(8,128)}, f32[128,512]{1,0:T(8,128)S(1)}, u32[]{:S(2)}, u32[]{:S(2)}) %collective-permute-start.36) | collective-permute-done | bytes 262176 | tf_op jit(solution)/shard_map/ppermute | solution.py:316
  1369.5 29.8 %collective-permute-done.37.refs_8_ = f32[128,512]{1,0:T(8,128)S(1)} collective-permute-done((f32[128,512]{1,0:T(8,128)S(1)}, f32[128,512]{1,0:T(8,128)S(1)}, u32[]{:S(2)}, u32[]{:S(2)}) %collective-permute-start.37) | collective-permute-done | bytes 262176 | tf_op jit(solution)/shard_map/ppermute | solution.py:315
  1421.4 23.1 %collective-permute-done.35.refs_6_ = f32[128,1024]{1,0:T(8,128)S(1)} collective-permute-done((f32[128,1024]{1,0:T(8,128)}, f32[128,1024]{1,0:T(8,128)S(1)}, u32[]{:S(2)}, u32[]{:S(2)}) %collective-permute-start.35) | collective-permute-done | bytes 524320 | tf_op jit(solution)/shard_map/ppermute | solution.py:316
  1484.9 16.9 %gx.2.refs_0_ = bf16[2048,2048]{1,0:T(8,128)(2,1)} custom-call(bf16[2048,2048]{1,0:T(8,128)(2,1)} %mm.8.x_ref.h_ref.refs_0_.refs_1_.refs_2_.refs_3_.refs_4_.refs_5_.refs_6_.refs_7_.refs_8_.refs_9_.refs_10_.refs_11_.refs_12_.refs_13_.refs_14_.refs_15_, bf16[2048,2048]{1,0:T(8,128)(2,1)} %bitcast.403, bf16[2048,512]{1,0:T(8,128)(2,1)} %bitcast.459, ...), custom_call_target="tpu_custom_call" | custom-call | flops 12600000512 | bytes 1048576 | tf_op jit(solution)/shard_map/gx/pallas_call | solution.py:388
  1504.3 16.9 %gx.3 = bf16[2048,2048]{1,0:T(8,128)(2,1)} custom-call(bf16[2048,2048]{1,0:T(8,128)(2,1)} %mm.8.x_ref.h_ref.refs_0_.refs_1_.refs_2_.refs_3_.refs_4_.refs_5_.refs_6_.refs_7_.refs_8_.refs_9_.refs_10_.refs_11_.refs_12_.refs_13_.refs_14_.refs_15_, bf16[2048,2048]{1,0:T(8,128)(2,1)} %bitcast.404, ...), custom_call_target="tpu_custom_call", output_to_operand_aliasing={{}: (6, {})} | custom-call | flops 12600000512 | bytes 1048576 | tf_op jit(solution)/shard_map/gx/pallas_call | solution.py:388
  (268 shorter events, 246.3 us)
Async XLA Ops:
  13.0 87.9 %collective-permute-start.10 = (bf16[8,128,512]{2,1,0:T(8,128)(2,1)}, bf16[8,128,512]{2,1,0:T(8,128)(2,1)}, u32[]{:S(2)}, u32[]{:S(2)}) collective-permute-start(bf16[8,128,512]{2,1,0:T(8,128)(2,1)} %bitcast.444), channel_id=1, source_target_pairs={{0,4},{1,5},{2,6},{3,7},{4,0},{5,1},{6,2},{7,3},{8,12},{9,13},{10,... | collective-permute-start | bytes 3145736 | tf_op jit(solution)/shard_map/ppermute | solution.py:316
  14.5 86.4 %collective-permute-start.7 = (bf16[8,128,512]{2,1,0:T(8,128)(2,1)}, bf16[8,128,512]{2,1,0:T(8,128)(2,1)}, u32[]{:S(2)}, u32[]{:S(2)}) collective-permute-start(bf16[8,128,512]{2,1,0:T(8,128)(2,1)} %bitcast.445), channel_id=1, source_target_pairs={{0,1},{1,0},{2,3},{3,2},{4,5},{5,4},{6,7},{7,6},{8,9},{9,8},{10,11... | collective-permute-start | bytes 3145736 | tf_op jit(solution)/shard_map/ppermute | solution.py:316
  14.5 86.9 %collective-permute-start.3 = (bf16[8,128,512]{2,1,0:T(8,128)(2,1)}, bf16[8,128,512]{2,1,0:T(8,128)(2,1)}, u32[]{:S(2)}, u32[]{:S(2)}) collective-permute-start(bf16[8,128,512]{2,1,0:T(8,128)(2,1)} %bitcast.437), channel_id=1, source_target_pairs={{0,4},{1,5},{2,6},{3,7},{4,0},{5,1},{6,2},{7,3},{8,12},{9,13},{10,... | collective-permute-start | bytes 3145736 | tf_op jit(solution)/shard_map/ppermute | solution.py:316
  15.0 111.6 %collective-permute-start.1 = (bf16[8,128,512]{2,1,0:T(8,128)(2,1)}, bf16[8,128,512]{2,1,0:T(8,128)(2,1)}, u32[]{:S(2)}, u32[]{:S(2)}) collective-permute-start(bf16[8,128,512]{2,1,0:T(8,128)(2,1)} %bitcast.438), channel_id=1, source_target_pairs={{0,2},{1,3},{2,0},{3,1},{4,6},{5,7},{6,4},{7,5},{8,10},{9,11},{10,... | collective-permute-start | bytes 3145736 | tf_op jit(solution)/shard_map/ppermute | solution.py:316
  453.2 197.4 %collective-permute-start.43 = (f32[4,128,512]{2,1,0:T(8,128)}, f32[4,128,512]{2,1,0:T(8,128)}, u32[]{:S(2)}, u32[]{:S(2)}) collective-permute-start(f32[4,128,512]{2,1,0:T(8,128)} %get-tuple-element.144), channel_id=1, source_target_pairs={{0,4},{1,5},{2,6},{3,7},{4,0},{5,1},{6,2},{7,3},{8,12},{9,13},{10,... | collective-permute-start | bytes 3145736 | tf_op jit(solution)/shard_map/ppermute | solution.py:316
  453.7 201.1 %collective-permute-start.44 = (f32[4,128,512]{2,1,0:T(8,128)}, f32[4,128,512]{2,1,0:T(8,128)}, u32[]{:S(2)}, u32[]{:S(2)}) collective-permute-start(f32[4,128,512]{2,1,0:T(8,128)} %get-tuple-element.147), channel_id=1, source_target_pairs={{0,2},{1,3},{2,0},{3,1},{4,6},{5,7},{6,4},{7,5},{8,10},{9,11},{10,... | collective-permute-start | bytes 3145736 | tf_op jit(solution)/shard_map/ppermute | solution.py:316
  653.2 97.4 %collective-permute-start.46 = (f32[2,128,512]{2,1,0:T(8,128)}, f32[2,128,512]{2,1,0:T(8,128)}, u32[]{:S(2)}, u32[]{:S(2)}) collective-permute-start(f32[2,128,512]{2,1,0:T(8,128)} %get-tuple-element.150), channel_id=1, source_target_pairs={{0,8},{8,0},{1,9},{9,1},{2,10},{10,2},{3,11},{11,3},{4,12},{12,4},... | collective-permute-start | bytes 1572872 | tf_op jit(solution)/shard_map/ppermute | solution.py:315
  657.3 94.6 %collective-permute-start.47 = (f32[2,128,512]{2,1,0:T(8,128)}, f32[2,128,512]{2,1,0:T(8,128)}, u32[]{:S(2)}, u32[]{:S(2)}) collective-permute-start(f32[2,128,512]{2,1,0:T(8,128)} %get-tuple-element.151), channel_id=1, source_target_pairs={{0,4},{1,5},{2,6},{3,7},{4,0},{5,1},{6,2},{7,3},{8,12},{9,13},{10,... | collective-permute-start | bytes 1572872 | tf_op jit(solution)/shard_map/ppermute | solution.py:316
  675.1 78.5 %collective-permute-start.33 = (f32[2,128,512]{2,1,0:T(8,128)}, f32[2,128,512]{2,1,0:T(8,128)}, u32[]{:S(2)}, u32[]{:S(2)}) collective-permute-start(f32[2,128,512]{2,1,0:T(8,128)} %get-tuple-element.130), channel_id=1, source_target_pairs={{0,8},{8,0},{1,9},{9,1},{2,10},{10,2},{3,11},{11,3},{4,12},{12,4},... | collective-permute-start | bytes 1572872 | tf_op jit(solution)/shard_map/ppermute | solution.py:315
  677.9 75.8 %collective-permute-start.34 = (f32[2,128,512]{2,1,0:T(8,128)}, f32[2,128,512]{2,1,0:T(8,128)}, u32[]{:S(2)}, u32[]{:S(2)}) collective-permute-start(f32[2,128,512]{2,1,0:T(8,128)} %get-tuple-element.131), channel_id=1, source_target_pairs={{0,4},{1,5},{2,6},{3,7},{4,0},{5,1},{6,2},{7,3},{8,12},{9,13},{10,... | collective-permute-start | bytes 1572872 | tf_op jit(solution)/shard_map/ppermute | solution.py:316
  749.0 96.8 %collective-permute-start.62 = (f32[4,352,512]{2,1,0:T(8,128)}, f32[4,352,512]{2,1,0:T(8,128)}, u32[]{:S(2)}, u32[]{:S(2)}) collective-permute-start(f32[4,352,512]{2,1,0:T(8,128)} %get-tuple-element.172), channel_id=1, source_target_pairs={{0,2},{1,3},{2,0},{3,1},{4,6},{5,7},{6,4},{7,5},{8,10},{9,11},{10,... | collective-permute-start | bytes 8650760 | tf_op jit(solution)/shard_map/ppermute | solution.py:316
  750.6 78.8 %collective-permute-start.42 = (f32[4,128,1024]{2,1,0:T(8,128)}, f32[4,128,1024]{2,1,0:T(8,128)}, u32[]{:S(2)}, u32[]{:S(2)}) collective-permute-start(f32[4,128,1024]{2,1,0:T(8,128)} %get-tuple-element.141), channel_id=1, source_target_pairs={{0,8},{8,0},{1,9},{9,1},{2,10},{10,2},{3,11},{11,3},{4,12},{12,4},... | collective-permute-start | bytes 6291464 | tf_op jit(solution)/shard_map/ppermute | solution.py:315
  751.9 91.3 %collective-permute-start.29 = (f32[4,128,1024]{2,1,0:T(8,128)}, f32[4,128,1024]{2,1,0:T(8,128)}, u32[]{:S(2)}, u32[]{:S(2)}) collective-permute-start(f32[4,128,1024]{2,1,0:T(8,128)} %get-tuple-element.121), channel_id=1, source_target_pairs={{0,8},{8,0},{1,9},{9,1},{2,10},{10,2},{3,11},{11,3},{4,12},{12,4},... | collective-permute-start | bytes 6291464 | tf_op jit(solution)/shard_map/ppermute | solution.py:315
  753.6 315.6 %collective-permute-start.14 = (f32[2,2,2,8,128,256]{5,4,3,2,1,0:T(8,128)}, f32[2,2,2,8,128,256]{5,4,3,2,1,0:T(8,128)}, u32[]{:S(2)}, u32[]{:S(2)}) collective-permute-start(f32[2,2,2,8,128,256]{5,4,3,2,1,0:T(8,128)} %get-tuple-element.103), channel_id=1, source_target_pairs={{0,1},{1,0},{2,3},{3,2},{4,5},{5,4},{6,7},{7,6},{8,9},{9,8},{10,11... | collective-permute-start | bytes 25165832 | tf_op jit(solution)/shard_map/ppermute | solution.py:316
  753.6 74.2 %collective-permute-start.49 = (f32[128,512]{1,0:T(8,128)S(1)}, f32[128,512]{1,0:T(8,128)S(1)}, u32[]{:S(2)}, u32[]{:S(2)}) collective-permute-start(f32[128,512]{1,0:T(8,128)S(1)} %fusion.71), channel_id=1, source_target_pairs={{0,2},{1,3},{2,0},{3,1},{4,6},{5,7},{6,4},{7,5},{8,10},{9,11},{10,... | collective-permute-start | bytes 786440 | tf_op jit(solution)/shard_map/ppermute | solution.py:316
  829.4 117.6 %collective-permute-start.24 = (f32[2,2,2,4,128,256]{5,4,3,2,1,0:T(8,128)}, f32[2,2,2,4,128,256]{5,4,3,2,1,0:T(8,128)S(1)}, u32[]{:S(2)}, u32[]{:S(2)}) collective-permute-start(f32[2,2,2,4,128,256]{5,4,3,2,1,0:T(8,128)} %get-tuple-element.115), channel_id=1, source_target_pairs={{0,1},{1,0},{2,3},{3,2},{4,5},{5,4},{6,7},{7,6},{8,9},{9,8},{10,11... | collective-permute-start | bytes 12582920 | tf_op jit(solution)/shard_map/ppermute | solution.py:316
  843.2 78.3 %collective-permute-start.45 = (f32[2,128,1024]{2,1,0:T(8,128)S(1)}, f32[2,128,1024]{2,1,0:T(8,128)S(1)}, u32[]{:S(2)}, u32[]{:S(2)}) collective-permute-start(f32[2,128,1024]{2,1,0:T(8,128)S(1)} %get-tuple-element.149), channel_id=1, source_target_pairs={{0,2},{1,3},{2,0},{3,1},{4,6},{5,7},{6,4},{7,5},{8,10},{9,11},{10,... | collective-permute-start | bytes 3145736 | tf_op jit(solution)/shard_map/ppermute | solution.py:316
  845.9 97.4 %collective-permute-start.32 = (f32[2,128,1024]{2,1,0:T(8,128)S(1)}, f32[2,128,1024]{2,1,0:T(8,128)S(1)}, u32[]{:S(2)}, u32[]{:S(2)}) collective-permute-start(f32[2,128,1024]{2,1,0:T(8,128)S(1)} %get-tuple-element.129), channel_id=1, source_target_pairs={{0,2},{1,3},{2,0},{3,1},{4,6},{5,7},{6,4},{7,5},{8,10},{9,11},{10,... | collective-permute-start | bytes 3145736 | tf_op jit(solution)/shard_map/ppermute | solution.py:316
  899.1 91.2 %collective-permute-start.51 = (f32[4,128,2048]{2,1,0:T(8,128)}, f32[4,128,2048]{2,1,0:T(8,128)S(1)}, u32[]{:S(2)}, u32[]{:S(2)}) collective-permute-start(f32[4,128,2048]{2,1,0:T(8,128)} %get-tuple-element.153), channel_id=1, source_target_pairs={{0,8},{8,0},{1,9},{9,1},{2,10},{10,2},{3,11},{11,3},{4,12},{12,4},... | collective-permute-start | bytes 12582920 | tf_op jit(solution)/shard_map/ppermute | solution.py:315
  943.2 93.8 %collective-permute-start.52 = (f32[4,128,2048]{2,1,0:T(8,128)}, f32[4,128,2048]{2,1,0:T(8,128)}, u32[]{:S(2)}, u32[]{:S(2)}) collective-permute-start(f32[4,128,2048]{2,1,0:T(8,128)} %get-tuple-element.156), channel_id=1, source_target_pairs={{0,4},{1,5},{2,6},{3,7},{4,0},{5,1},{6,2},{7,3},{8,12},{9,13},{10,... | collective-permute-start | bytes 12582920 | tf_op jit(solution)/shard_map/ppermute | solution.py:316
  947.0 120.8 %collective-permute-start.65 = (f32[2,352,512]{2,1,0:T(8,128)S(1)}, f32[2,352,512]{2,1,0:T(8,128)S(1)}, u32[]{:S(2)}, u32[]{:S(2)}) collective-permute-start(f32[2,352,512]{2,1,0:T(8,128)S(1)} %get-tuple-element.176), channel_id=1, source_target_pairs={{0,4},{1,5},{2,6},{3,7},{4,0},{5,1},{6,2},{7,3},{8,12},{9,13},{10,... | collective-permute-start | bytes 4325384 | tf_op jit(solution)/shard_map/ppermute | solution.py:316
  990.3 272.0 %collective-permute-start.60 = (f32[4,352,768]{2,1,0:T(8,128)}, f32[4,352,768]{2,1,0:T(8,128)}, u32[]{:S(2)}, u32[]{:S(2)}) collective-permute-start(f32[4,352,768]{2,1,0:T(8,128)} %get-tuple-element.166), channel_id=1, source_target_pairs={{0,8},{8,0},{1,9},{9,1},{2,10},{10,2},{3,11},{11,3},{4,12},{12,4},... | collective-permute-start | bytes 12976136 | tf_op jit(solution)/shard_map/ppermute | solution.py:315
  990.6 272.6 %collective-permute-start.61 = (f32[4,352,768]{2,1,0:T(8,128)}, f32[4,352,768]{2,1,0:T(8,128)S(1)}, u32[]{:S(2)}, u32[]{:S(2)}) collective-permute-start(f32[4,352,768]{2,1,0:T(8,128)} %get-tuple-element.169), channel_id=1, source_target_pairs={{0,4},{1,5},{2,6},{3,7},{4,0},{5,1},{6,2},{7,3},{8,12},{9,13},{10,... | collective-permute-start | bytes 12976136 | tf_op jit(solution)/shard_map/ppermute | solution.py:316
  1037.0 146.0 %collective-permute-start.27 = (f32[2,4,128,256]{3,2,1,0:T(8,128)S(1)}, f32[2,4,128,256]{3,2,1,0:T(8,128)S(1)}, u32[]{:S(2)}, u32[]{:S(2)}) collective-permute-start(f32[2,4,128,256]{3,2,1,0:T(8,128)S(1)} %get-tuple-element.203), channel_id=1, source_target_pairs={{0,4},{1,5},{2,6},{3,7},{4,0},{5,1},{6,2},{7,3},{8,12},{9,13},{10,... | collective-permute-start | bytes 3145736 | tf_op jit(solution)/shard_map/ppermute | solution.py:316
  1067.8 115.5 %collective-permute-start.25 = (f32[2,4,128,256]{3,2,1,0:T(8,128)S(1)}, f32[2,4,128,256]{3,2,1,0:T(8,128)}, u32[]{:S(2)}, u32[]{:S(2)}) collective-permute-start(f32[2,4,128,256]{3,2,1,0:T(8,128)S(1)} %get-tuple-element.204), channel_id=1, source_target_pairs={{0,2},{1,3},{2,0},{3,1},{4,6},{5,7},{6,4},{7,5},{8,10},{9,11},{10,... | collective-permute-start | bytes 3145736 | tf_op jit(solution)/shard_map/ppermute | solution.py:316
  1069.3 136.3 %collective-permute-start.22 = (f32[2,4,128,256]{3,2,1,0:T(8,128)S(1)}, f32[2,4,128,256]{3,2,1,0:T(8,128)}, u32[]{:S(2)}, u32[]{:S(2)}) collective-permute-start(f32[2,4,128,256]{3,2,1,0:T(8,128)S(1)} %get-tuple-element.207), channel_id=1, source_target_pairs={{0,4},{1,5},{2,6},{3,7},{4,0},{5,1},{6,2},{7,3},{8,12},{9,13},{10,... | collective-permute-start | bytes 3145736 | tf_op jit(solution)/shard_map/ppermute | solution.py:316
  1183.3 72.9 %collective-permute-start.15 = (f32[2,8,128,256]{3,2,1,0:T(8,128)S(1)}, f32[2,8,128,256]{3,2,1,0:T(8,128)}, u32[]{:S(2)}, u32[]{:S(2)}) collective-permute-start(f32[2,8,128,256]{3,2,1,0:T(8,128)S(1)} %get-tuple-element.184), channel_id=1, source_target_pairs={{0,2},{1,3},{2,0},{3,1},{4,6},{5,7},{6,4},{7,5},{8,10},{9,11},{10,... | collective-permute-start | bytes 6291464 | tf_op jit(solution)/shard_map/ppermute | solution.py:316
  1268.6 95.8 %collective-permute-start.56 = (f32[2,128,1536]{2,1,0:T(8,128)}, f32[2,128,1536]{2,1,0:T(8,128)}, u32[]{:S(2)}, u32[]{:S(2)}) collective-permute-start(f32[2,128,1536]{2,1,0:T(8,128)} %get-tuple-element.163), channel_id=1, source_target_pairs={{0,4},{1,5},{2,6},{3,7},{4,0},{5,1},{6,2},{7,3},{8,12},{9,13},{10,... | collective-permute-start | bytes 4718600 | tf_op jit(solution)/shard_map/ppermute | solution.py:316
  1276.4 89.8 %collective-permute-start.54 = (f32[2,128,2048]{2,1,0:T(8,128)}, f32[2,128,2048]{2,1,0:T(8,128)}, u32[]{:S(2)}, u32[]{:S(2)}) collective-permute-start(f32[2,128,2048]{2,1,0:T(8,128)} %get-tuple-element.161), channel_id=1, source_target_pairs={{0,2},{1,3},{2,0},{3,1},{4,6},{5,7},{6,4},{7,5},{8,10},{9,11},{10,... | collective-permute-start | bytes 6291464 | tf_op jit(solution)/shard_map/ppermute | solution.py:316
  1282.9 117.8 %collective-permute-start.55 = (f32[2,128,2048]{2,1,0:T(8,128)}, f32[2,128,2048]{2,1,0:T(8,128)}, u32[]{:S(2)}, u32[]{:S(2)}) collective-permute-start(f32[2,128,2048]{2,1,0:T(8,128)} %get-tuple-element.162), channel_id=1, source_target_pairs={{0,8},{8,0},{1,9},{9,1},{2,10},{10,2},{3,11},{11,3},{4,12},{12,4},... | collective-permute-start | bytes 6291464 | tf_op jit(solution)/shard_map/ppermute | solution.py:315
  1326.1 89.4 %collective-permute-start.63 = (f32[2,352,768]{2,1,0:T(8,128)}, f32[2,352,768]{2,1,0:T(8,128)}, u32[]{:S(2)}, u32[]{:S(2)}) collective-permute-start(f32[2,352,768]{2,1,0:T(8,128)} %get-tuple-element.174), channel_id=1, source_target_pairs={{0,2},{1,3},{2,0},{3,1},{4,6},{5,7},{6,4},{7,5},{8,10},{9,11},{10,... | collective-permute-start | bytes 6488072 | tf_op jit(solution)/shard_map/ppermute | solution.py:316
  1364.5 81.7 %collective-permute-start.38 = (f32[8,128,512]{2,1,0:T(8,128)}, f32[8,128,512]{2,1,0:T(8,128)S(1)}, u32[]{:S(2)}, u32[]{:S(2)}) collective-permute-start(f32[8,128,512]{2,1,0:T(8,128)} %get-tuple-element.133), channel_id=1, source_target_pairs={{0,1},{1,0},{2,3},{3,2},{4,5},{5,4},{6,7},{7,6},{8,9},{9,8},{10,11... | collective-permute-start | bytes 6291464 | tf_op jit(solution)/shard_map/ppermute | solution.py:316
  (86 other events, 3613.8 us)
where the time goes:
time: 1530 us; the launch traced here: 1520 us
  Pallas kernels  823 us (54%)
  waiting for transfers between devices  555 us (36%)
  other arithmetic  77 us (5%)
  starting transfers between devices  60.4 us (4%)
    ppermute x56, waiting for transfers between devices, swap(): return lax.ppermute(values, 'cp', [(i, i ^ BITS[link]) for i in range(8)])  462 us
    pallas_call x4, Pallas kernels, pair_call(): pl.pallas_call(functools.partial(pair_kernel, plan, rows, turned), grid=(...  214 us
    pallas_call x5, Pallas kernels, mm(): pl.pallas_call(functools.partial(mm_kernel, nt if flip else nn, added is...  195 us
    pallas_call x3, Pallas kernels, attn_bwd(): pl.pallas_call(functools.partial(bwd_kernel, scale, scale2, aliased), gri...  158 us
    ppermute x13, waiting for transfers between devices, swap(): return lax.ppermute(values, 'dp', [(Z, 1), (1, Z)])  93 us
    pallas_call x2, Pallas kernels, attn_fwd(): pl.pallas_call(functools.partial(fwd_kernel, scale2, aliased), grid_spec=...  90.6 us
    pallas_call x1, Pallas kernels, ff_block(): pl.pallas_call(ff_kernel, grid_spec=grid_spec, name='ff_block', out_shape...  89.6 us
    ppermute x56, starting transfers between devices, swap(): return lax.ppermute(values, 'cp', [(i, i ^ BITS[link]) for i in range(8)])  50 us
  transfers between devices with their start and end apart: 69, of which 25 were waited for; matrix products, arithmetic and copies ran while one was open for 5% of the time, Pallas kernels for 35%

commit v1 on v0

--- a/solution.py
+++ b/solution.py
@@ -414,7 +414,7 @@
 
 
 def ff_block(bits, h, w_up, ga):
-    tokens, width, rows = MODEL, FF_TILE, CHUNK
+    tokens, width, rows = MODEL, FF_TILE, WIDE
     per = tokens // rows
     steps = 4 * per
     now = lambda i: jnp.minimum(i, steps - 1)
@@ -641,8 +641,7 @@
 
 CHUNKS = ((Z, 8), (8, 4), (12, 4))
 PLAN_UP = (('z', 4), ('y', 4), ('x', 3))
-PLAN_D = (('z', 2), ('y', 1), ('x', 1))
-PLAN_DOWN = (('z', 3), ('y', 3), ('x', 2))
+PLAN_D = (('z', 3), ('y', 3), ('x', 2))
 
 
 def solution(mesh):
@@ -668,18 +667,19 @@
 
         act_t, grad_u = ff_block(bits, h, w_up, grad_act)
         grad_w_up = weight_grad(h, grad_u, PLAN_UP, WIDE, Z)
-        grad_w_down = weight_grad(act_t.reshape(8, 2, -1, tokens), cot2, PLAN_DOWN, CHUNK, 1)
+        grad_w_down = weight_grad(act_t.reshape(8, 2, -1, tokens), cot2, PLAN_D, CHUNK, 1)
         grad_h = mm(grad_u, w_up, WIDE, Z, 4, WIDE, True, cot2)
         grad_o = mm(grad_h, w_o2, WIDE, Z, 2, SEQ).reshape(batch, seq, -1)
 
         grad_q, grad_kv = None, []
-        for first, count in CHUNKS:
+        for part, (first, count) in enumerate(CHUNKS):
             side, sub = first // 8, first % 8
             grad_q, keep, send = attn_bwd(me_one, q, grad_o, lse[side], gathered[side], first, sub, count, grad_q)
             grad_kv += reduce_dkv(keep, send)
+            if part == Z:
+                grad_w_o = weight_grad(grad_h, o2, PLAN_D, CHUNK, 2, True)
         grad_q2 = grad_q.reshape(tokens, -1)
-        grad_w_o = weight_grad(grad_h, o2, PLAN_D, WIDE, 2, True)
-        grad_w_q = weight_grad(x2, grad_q2, PLAN_D, WIDE, 3, True)
+        grad_w_q = weight_grad(x2, grad_q2, PLAN_D, CHUNK, 3, True)
         grad_kv2 = join(grad_kv).reshape(tokens, -1)
         grad_w_kv = small_grad(bits, x2, grad_kv2).reshape(-1, 4, 2, HALF)
         grad_x = None

time: 1530 us -> 1600 us (1.046)
  waiting for transfers between devices: 555 us -> 618 us
    ppermute x56, waiting for transfers between devices: 462 us -> 540 us  [swap(): return lax.ppermute(values, 'cp', [(i, i ^ BITS[link]) for i in range(8)])]
  transfers between devices with their start and end apart: 69 -> 69, of which waited for: 25 -> 22; matrix products, arithmetic and copies ran while one was open for 5% -> 5% of each run, Pallas kernels for 35% -> 34%
where the time goes in v1:
time: 1600 us; the launch traced here: 1590 us
  Pallas kernels  822 us (51%)
  waiting for transfers between devices  618 us (39%)
  other arithmetic  82.1 us (5%)
  starting transfers between devices  64.2 us (4%)
    ppermute x56, waiting for transfers between devices, swap(): return lax.ppermute(values, 'cp', [(i, i ^ BITS[link]) for i in range(8)])  540 us
    pallas_call x4, Pallas kernels, pair_call(): pl.pallas_call(functools.partial(pair_kernel, plan, rows, turned), grid=(...  216 us
    pallas_call x5, Pallas kernels, mm(): pl.pallas_call(functools.partial(mm_kernel, nt if flip else nn, added is...  195 us
    pallas_call x3, Pallas kernels, attn_bwd(): pl.pallas_call(functools.partial(bwd_kernel, scale, scale2, aliased), gri...  158 us
    pallas_call x2, Pallas kernels, attn_fwd(): pl.pallas_call(functools.partial(fwd_kernel, scale2, aliased), grid_spec=...  90.5 us
    pallas_call x1, Pallas kernels, ff_block(): pl.pallas_call(ff_kernel, grid_spec=grid_spec, name='ff_block', out_shape...  85.5 us
    ppermute x13, waiting for transfers between devices, swap(): return lax.ppermute(values, 'dp', [(Z, 1), (1, Z)])  77.8 us
    ppermute x56, starting transfers between devices, swap(): return lax.ppermute(values, 'cp', [(i, i ^ BITS[link]) for i in range(8)])  48 us
  transfers between devices with their start and end apart: 69, of which 22 were waited for; matrix products, arithmetic and copies ran while one was open for 5% of the time, Pallas kernels for 34%

profile of v1, /device:TPU:0, one launch (start us, length us, event | category | flops | bytes accessed | tf_op | source)
XLA Modules:
  0.0 1594.1 jit_solution(6553623801391327815)
XLA Ops:
  0.6 9.1 kv.1
  15.1 22.3 %collective-permute-done.8.refs_2_ = bf16[8,128,512]{2,1,0:T(8,128)(2,1)} collective-permute-done((bf16[8,128,512]{2,1,0:T(8,128)(2,1)}, bf16[8,128,512]{2,1,0:T(8,128)(2,1)}, u32[]{:S(2)}, u32[]{:S(2)}) %collective-permute-start.8) | collective-permute-done | bytes 1048608 | tf_op jit(solution)/shard_map/ppermute | solution.py:316
  39.4 60.8 %mm.7.ga_ref = bf16[2048,5632]{1,0:T(8,128)(2,1)} custom-call(bf16[2048,2048]{1,0:T(8,128)(2,1)} %bitcast.427, bf16[5632,2048]{1,0:T(8,128)(2,1)} %w_ref.3), custom_call_target="tpu_custom_call" | custom-call | flops 47244640256 | bytes 1048576 | tf_op jit(solution)/shard_map/mm/pallas_call | solution.py:339
  102.9 23.7 %mm.5 = bf16[2048,2048]{1,0:T(8,128)(2,1)} custom-call(bf16[2048,2048]{1,0:T(8,128)(2,1)} %bitcast.380, bf16[2048,2048]{1,0:T(8,128)(2,1)} %bitcast.430), custom_call_target="tpu_custom_call" | custom-call | flops 17179869184 | bytes 1048576 | tf_op jit(solution)/shard_map/mm/pallas_call | solution.py:339
  127.6 45.2 %attn_fwd.2 = (bf16[16,128,2048]{2,1,0:T(8,128)(2,1)}, f32[32,2,512]{2,1,0:T(2,128)}) custom-call(s32[1]{0:T(128)} %bitcast.4.me_ref, bf16[16,128,2048]{2,1,0:T(8,128)(2,1)} %bitcast.451, bf16[8,128,512]{2,1,0:T(8,128)(2,1)} %bitcast.448, bf16[8,128,512]{2,1,0:T(8,128)(2,1)} %collective-permute-done.7.refs_1_, ...), custom_call_target="tpu_custom_call" | custom-call | flops 43200000000 | bytes 1048576 | tf_op jit(solution)/shard_map/attn_fwd/pallas_call | solution.py:274
  172.8 45.3 %attn_fwd.3 = (bf16[16,128,2048]{2,1,0:T(8,128)(2,1)}, f32[32,2,512]{2,1,0:T(2,128)}) custom-call(s32[1]{0:T(128)} %bitcast.4.me_ref, bf16[16,128,2048]{2,1,0:T(8,128)(2,1)} %bitcast.452, bf16[8,128,512]{2,1,0:T(8,128)(2,1)} %bitcast.442, bf16[8,128,512]{2,1,0:T(8,128)(2,1)} %collective-permute-done.refs_1_, ...), custom_call_target="tpu_custom_call", output_to_operand_aliasing={{0}: (10, {})} | custom-call | flops 43200000000 | bytes 1048576 | tf_op jit(solution)/shard_map/attn_fwd/pallas_call | solution.py:274
  218.2 25.0 %mm.6.h_ref.refs_0_.refs_1_.refs_2_.refs_3_.refs_4_.refs_5_.refs_6_.refs_7_.refs_8_.refs_9_.refs_10_.refs_11_.refs_12_.refs_13_.refs_14_.refs_15_ = bf16[2048,2048]{1,0:T(8,128)(2,1)} custom-call(bf16[2048,2048]{1,0:T(8,128)(2,1)} %bitcast.400, bf16[2048,2048]{1,0:T(8,128)(2,1)} %bitcast.425, bf16[2048,2048]{1,0:T(8,128)(2,1)} %bitcast.381), custom_call_target="tpu_custom_call" | custom-call | flops 17179869184 | bytes 1048576 | tf_op jit(solution)/shard_map/mm/pallas_call | solution.py:339
  243.2 85.5 %ff_block.1 = (bf16[2,2,2,2,352,2048]{5,4,3,2,1,0:T(8,128)(2,1)}, bf16[2048,5632]{1,0:T(8,128)(2,1)}) custom-call(s32[4]{0:T(128)} %pad_add_fusion.bits_ref, bf16[2048,2048]{1,0:T(8,128)(2,1)} %mm.6.h_ref.refs_0_.refs_1_.refs_2_.refs_3_.refs_4_.refs_5_.refs_6_.refs_7_.refs_8_.refs_9_.refs_10_.refs_11_.refs_12_.refs_13_.refs_14_.refs_15_, ...), custom_call_target="tpu_custom_call" | custom-call | flops 54000001024 | bytes 1048576 | tf_op jit(solution)/shard_map/ff_block/pallas_call | solution.py:430
  328.6 61.0 %mm.8.x_ref.h_ref.refs_0_.refs_1_.refs_2_.refs_3_.refs_4_.refs_5_.refs_6_.refs_7_.refs_8_.refs_9_.refs_10_.refs_11_.refs_12_.refs_13_.refs_14_.refs_15_ = bf16[2048,2048]{1,0:T(8,128)(2,1)} custom-call(bf16[2048,5632]{1,0:T(8,128)(2,1)} %get-tuple-element.96.x_ref.refs_16_, bf16[2048,5632]{1,0:T(8,128)(2,1)} %w_ref.5, bf16[2048,2048]{1,0:T(8,128)(2,1)} %bitcast.428), custom_call_target="tpu_custom_call" | custom-call | flops 47244640256 | bytes 1048576 | tf_op jit(solution)/shard_map/mm/pallas_call | solution.py:339
  389.7 36.9 %pair.5 = (f32[4,128,768]{2,1,0:T(8,128)}, f32[4,128,768]{2,1,0:T(8,128)}, f32[4,128,768]{2,1,0:T(8,128)}, f32[4,128,768]{2,1,0:T(8,128)}, f32[4,128,512]{2,1,0:T(8,128)}, /*index=5*/f32[4,128,512]{2,1,0:T(8,128)}) custom-call(bf16[2048,2048]{1,0:T(8,128)(2,1)} %mm.8.x_ref.h_ref.refs_0_.refs_1_.refs_2_.refs_3_.refs_4_.refs_5_.refs_6_.refs_7_.refs_8_.refs_9_.refs_10_.refs_11_., ...), custom_call_target="tpu_custom_call" | custom-call | flops 17179869184 | bytes 1048576 | tf_op jit(solution)/shard_map/pair/pallas_call | solution.py:536
  426.6 23.9 %mm.9 = bf16[2048,2048]{1,0:T(8,128)(2,1)} custom-call(bf16[2048,2048]{1,0:T(8,128)(2,1)} %mm.8.x_ref.h_ref.refs_0_.refs_1_.refs_2_.refs_3_.refs_4_.refs_5_.refs_6_.refs_7_.refs_8_.refs_9_.refs_10_.refs_11_.refs_12_.refs_13_.refs_14_.refs_15_, bf16[2048,2048]{1,0:T(8,128)(2,1)} %bitcast.426), custom_call_target="tpu_custom_call" | custom-call | flops 17179869184 | bytes 1048576 | tf_op jit(solution)/shard_map/mm/pallas_call | solution.py:339
  452.7 77.8 %attn_bwd.3 = (bf16[16,128,2048]{2,1,0:T(8,128)(2,1)}, f32[2,2,2,8,128,256]{5,4,3,2,1,0:T(8,128)}, f32[2,2,2,8,128,256]{5,4,3,2,1,0:T(8,128)}) custom-call(s32[1]{0:T(128)} %bitcast.4.me_ref, bf16[16,128,2048]{2,1,0:T(8,128)(2,1)} %bitcast.453, bf16[16,128,2048]{2,1,0:T(8,128)(2,1)} %bitcast.456, f32[32,2,512]{2,1,0:T(2,128)} %get-tuple-element.98.lse_ref, ...), custom_call_target="tpu_custom_call" | custom-call | flops 71999995904 | bytes 1048576 | tf_op jit(solution)/shard_map/attn_bwd/pallas_call | solution.py:299
  530.5 40.1 %attn_bwd.4 = (bf16[16,128,2048]{2,1,0:T(8,128)(2,1)}, f32[2,2,2,4,128,256]{5,4,3,2,1,0:T(8,128)}, f32[2,2,2,4,128,256]{5,4,3,2,1,0:T(8,128)}) custom-call(s32[1]{0:T(128)} %bitcast.4.me_ref, bf16[16,128,2048]{2,1,0:T(8,128)(2,1)} %bitcast.454, bf16[16,128,2048]{2,1,0:T(8,128)(2,1)} %bitcast.457, ...), custom_call_target="tpu_custom_call", output_to_operand_aliasing={{0}: (12, {})} | custom-call | flops 35999997952 | bytes 1048576 | tf_op jit(solution)/shard_map/attn_bwd/pallas_call | solution.py:299
  570.6 40.4 %attn_bwd.5 = (bf16[16,128,2048]{2,1,0:T(8,128)(2,1)}, f32[2,2,2,4,128,256]{5,4,3,2,1,0:T(8,128)}, f32[2,2,2,4,128,256]{5,4,3,2,1,0:T(8,128)}) custom-call(s32[1]{0:T(128)} %bitcast.4.me_ref, bf16[16,128,2048]{2,1,0:T(8,128)(2,1)} %bitcast.455, bf16[16,128,2048]{2,1,0:T(8,128)(2,1)} %bitcast.458, ...), custom_call_target="tpu_custom_call", output_to_operand_aliasing={{0}: (12, {})} | custom-call | flops 35999997952 | bytes 1048576 | tf_op jit(solution)/shard_map/attn_bwd/pallas_call | solution.py:299
  610.9 36.7 %pair.4 = (f32[4,128,768]{2,1,0:T(8,128)}, f32[4,128,768]{2,1,0:T(8,128)}, f32[4,128,768]{2,1,0:T(8,128)}, f32[4,128,768]{2,1,0:T(8,128)}, f32[4,128,512]{2,1,0:T(8,128)}, /*index=5*/f32[4,128,512]{2,1,0:T(8,128)}) custom-call(bf16[2048,2048]{1,0:T(8,128)(2,1)} %bitcast.382, bf16[2048,2048]{1,0:T(8,128)(2,1)} %bitcast.383, bf16[2048,2048]{1,0:T(8,128)(2,1)} %bitcast.384, ...), custom_call_target="tpu_custom_call" | custom-call | flops 17179869184 | bytes 1048576 | tf_op jit(solution)/shard_map/pair/pallas_call | solution.py:536
  653.2 20.0 %collective-permute-done.31 = f32[4,128,512]{2,1,0:T(8,128)S(1)} collective-permute-done((f32[4,128,512]{2,1,0:T(8,128)}, f32[4,128,512]{2,1,0:T(8,128)S(1)}, u32[]{:S(2)}, u32[]{:S(2)}) %collective-permute-start.31) | collective-permute-done | bytes 1048608 | tf_op jit(solution)/shard_map/ppermute | solution.py:316
  690.4 41.0 %collective-permute-done.47.refs_5_ = f32[2,128,512]{2,1,0:T(8,128)S(1)} collective-permute-done((f32[2,128,512]{2,1,0:T(8,128)S(1)}, f32[2,128,512]{2,1,0:T(8,128)S(1)}, u32[]{:S(2)}, u32[]{:S(2)}) %collective-permute-start.47) | collective-permute-done | bytes 524320 | tf_op jit(solution)/shard_map/ppermute | solution.py:316
  733.4 73.8 %pair.6 = (f32[4,128,2048]{2,1,0:T(8,128)}, f32[4,128,2048]{2,1,0:T(8,128)}, f32[4,128,2048]{2,1,0:T(8,128)}, f32[4,128,2048]{2,1,0:T(8,128)}, f32[4,128,1536]{2,1,0:T(8,128)}, /*index=5*/f32[4,128,1536]{2,1,0:T(8,128)}) custom-call(bf16[2048,2048]{1,0:T(8,128)(2,1)} %mm.6.h_ref.refs_0_.refs_1_.refs_2_.refs_3_.refs_4_.refs_5_.refs_6_.refs_7_.refs_8_.refs_9_.refs_10_.refs_11_., ...), custom_call_target="tpu_custom_call" | custom-call | flops 47244640256 | bytes 1048576 | tf_op jit(solution)/shard_map/pair/pallas_call | solution.py:536
  812.9 69.1 %pair.7 = (f32[4,352,768]{2,1,0:T(8,128)}, f32[4,352,768]{2,1,0:T(8,128)}, f32[4,352,768]{2,1,0:T(8,128)}, f32[4,352,768]{2,1,0:T(8,128)}, f32[4,352,512]{2,1,0:T(8,128)}, /*index=5*/f32[4,352,512]{2,1,0:T(8,128)}) custom-call(bf16[8,2,352,2048]{3,2,1,0:T(8,128)(2,1)} %bitcast.450, bf16[2048,2048]{1,0:T(8,128)(2,1)} %bitcast.429), custom_call_target="tpu_custom_call" | custom-call | flops 47244640256 | bytes 1048576 | tf_op jit(solution)/shard_map/pair/pallas_call | solution.py:536
  882.0 38.2 %collective-permute-done.33.refs_4_ = f32[2,128,768]{2,1,0:T(8,128)} collective-permute-done((f32[2,128,768]{2,1,0:T(8,128)}, f32[2,128,768]{2,1,0:T(8,128)}, u32[]{:S(2)}, u32[]{:S(2)}) %collective-permute-start.33) | collective-permute-done | bytes 786464 | tf_op jit(solution)/shard_map/ppermute | solution.py:315
  924.8 60.9 %collective-permute-done.62 = f32[4,352,512]{2,1,0:T(8,128)S(1)} collective-permute-done((f32[4,352,512]{2,1,0:T(8,128)}, f32[4,352,512]{2,1,0:T(8,128)S(1)}, u32[]{:S(2)}, u32[]{:S(2)}) %collective-permute-start.62) | collective-permute-done | bytes 2883616 | tf_op jit(solution)/shard_map/ppermute | solution.py:316
  989.7 63.4 %collective-permute-done.53 = f32[4,128,1536]{2,1,0:T(8,128)S(1)} collective-permute-done((f32[4,128,1536]{2,1,0:T(8,128)}, f32[4,128,1536]{2,1,0:T(8,128)S(1)}, u32[]{:S(2)}, u32[]{:S(2)}) %collective-permute-start.53) | collective-permute-done | bytes 3145760 | tf_op jit(solution)/shard_map/ppermute | solution.py:316
  1063.0 12.6 collective-permute-done.25
  1102.4 111.6 %collective-permute-done.17 = f32[2,8,128,256]{3,2,1,0:T(8,128)S(1)} collective-permute-done((f32[2,8,128,256]{3,2,1,0:T(8,128)S(1)}, f32[2,8,128,256]{3,2,1,0:T(8,128)S(1)}, u32[]{:S(2)}, u32[]{:S(2)}) %collective-permute-start.17) | collective-permute-done | bytes 2097184 | tf_op jit(solution)/shard_map/ppermute | solution.py:316
  1236.7 100.9 %collective-permute-done.65.refs_5_ = f32[2,352,512]{2,1,0:T(8,128)S(1)} collective-permute-done((f32[2,352,512]{2,1,0:T(8,128)}, f32[2,352,512]{2,1,0:T(8,128)S(1)}, u32[]{:S(2)}, u32[]{:S(2)}) %collective-permute-start.65) | collective-permute-done | bytes 1441824 | tf_op jit(solution)/shard_map/ppermute | solution.py:316
  1365.0 17.5 %collective-permute-done.16.refs_1_ = f32[8,128,256]{2,1,0:T(8,128)S(1)} collective-permute-done((f32[8,128,256]{2,1,0:T(8,128)S(1)}, f32[8,128,256]{2,1,0:T(8,128)S(1)}, u32[]{:S(2)}, u32[]{:S(2)}) %collective-permute-start.16) | collective-permute-done | bytes 1048608 | tf_op jit(solution)/shard_map/ppermute | solution.py:316
  1393.2 39.6 %collective-permute-done.37.refs_8_ = f32[128,512]{1,0:T(8,128)} collective-permute-done((f32[128,512]{1,0:T(8,128)S(1)}, f32[128,512]{1,0:T(8,128)}, u32[]{:S(2)}, u32[]{:S(2)}) %collective-permute-start.37) | collective-permute-done | bytes 262176 | tf_op jit(solution)/shard_map/ppermute | solution.py:315
  1436.4 11.7 small.1
  1451.7 29.3 %collective-permute-done.49.refs_7_ = f32[128,768]{1,0:T(8,128)S(1)} collective-permute-done((f32[128,768]{1,0:T(8,128)S(1)}, f32[128,768]{1,0:T(8,128)S(1)}, u32[]{:S(2)}, u32[]{:S(2)}) %collective-permute-start.49) | collective-permute-done | bytes 393248 | tf_op jit(solution)/shard_map/ppermute | solution.py:316
  1517.9 10.1 collective-permute-done.58.refs_7_
  1555.8 16.9 %gx.2.refs_0_ = bf16[2048,2048]{1,0:T(8,128)(2,1)} custom-call(bf16[2048,2048]{1,0:T(8,128)(2,1)} %mm.8.x_ref.h_ref.refs_0_.refs_1_.refs_2_.refs_3_.refs_4_.refs_5_.refs_6_.refs_7_.refs_8_.refs_9_.refs_10_.refs_11_.refs_12_.refs_13_.refs_14_.refs_15_, bf16[2048,2048]{1,0:T(8,128)(2,1)} %bitcast.403, bf16[2048,512]{1,0:T(8,128)(2,1)} %bitcast.461, ...), custom_call_target="tpu_custom_call" | custom-call | flops 12600000512 | bytes 1048576 | tf_op jit(solution)/shard_map/gx/pallas_call | solution.py:388
  1576.1 16.9 %gx.3 = bf16[2048,2048]{1,0:T(8,128)(2,1)} custom-call(bf16[2048,2048]{1,0:T(8,128)(2,1)} %mm.8.x_ref.h_ref.refs_0_.refs_1_.refs_2_.refs_3_.refs_4_.refs_5_.refs_6_.refs_7_.refs_8_.refs_9_.refs_10_.refs_11_.refs_12_.refs_13_.refs_14_.refs_15_, bf16[2048,2048]{1,0:T(8,128)(2,1)} %bitcast.404, ...), custom_call_target="tpu_custom_call", output_to_operand_aliasing={{}: (6, {})} | custom-call | flops 12600000512 | bytes 1048576 | tf_op jit(solution)/shard_map/gx/pallas_call | solution.py:388
  (276 shorter events, 225.8 us)
Async XLA Ops:
  13.0 87.9 %collective-permute-start.10 = (bf16[8,128,512]{2,1,0:T(8,128)(2,1)}, bf16[8,128,512]{2,1,0:T(8,128)(2,1)}, u32[]{:S(2)}, u32[]{:S(2)}) collective-permute-start(bf16[8,128,512]{2,1,0:T(8,128)(2,1)} %bitcast.446), channel_id=1, source_target_pairs={{0,4},{1,5},{2,6},{3,7},{4,0},{5,1},{6,2},{7,3},{8,12},{9,13},{10,... | collective-permute-start | bytes 3145736 | tf_op jit(solution)/shard_map/ppermute | solution.py:316
  14.5 86.4 %collective-permute-start.7 = (bf16[8,128,512]{2,1,0:T(8,128)(2,1)}, bf16[8,128,512]{2,1,0:T(8,128)(2,1)}, u32[]{:S(2)}, u32[]{:S(2)}) collective-permute-start(bf16[8,128,512]{2,1,0:T(8,128)(2,1)} %bitcast.447), channel_id=1, source_target_pairs={{0,1},{1,0},{2,3},{3,2},{4,5},{5,4},{6,7},{7,6},{8,9},{9,8},{10,11... | collective-permute-start | bytes 3145736 | tf_op jit(solution)/shard_map/ppermute | solution.py:316
  14.5 86.9 %collective-permute-start.3 = (bf16[8,128,512]{2,1,0:T(8,128)(2,1)}, bf16[8,128,512]{2,1,0:T(8,128)(2,1)}, u32[]{:S(2)}, u32[]{:S(2)}) collective-permute-start(bf16[8,128,512]{2,1,0:T(8,128)(2,1)} %bitcast.439), channel_id=1, source_target_pairs={{0,4},{1,5},{2,6},{3,7},{4,0},{5,1},{6,2},{7,3},{8,12},{9,13},{10,... | collective-permute-start | bytes 3145736 | tf_op jit(solution)/shard_map/ppermute | solution.py:316
  15.0 111.5 %collective-permute-start.1 = (bf16[8,128,512]{2,1,0:T(8,128)(2,1)}, bf16[8,128,512]{2,1,0:T(8,128)(2,1)}, u32[]{:S(2)}, u32[]{:S(2)}) collective-permute-start(bf16[8,128,512]{2,1,0:T(8,128)(2,1)} %bitcast.440), channel_id=1, source_target_pairs={{0,2},{1,3},{2,0},{3,1},{4,6},{5,7},{6,4},{7,5},{8,10},{9,11},{10,... | collective-permute-start | bytes 3145736 | tf_op jit(solution)/shard_map/ppermute | solution.py:316
  450.5 199.6 %collective-permute-start.44 = (f32[4,128,512]{2,1,0:T(8,128)}, f32[4,128,512]{2,1,0:T(8,128)}, u32[]{:S(2)}, u32[]{:S(2)}) collective-permute-start(f32[4,128,512]{2,1,0:T(8,128)} %get-tuple-element.147), channel_id=1, source_target_pairs={{0,2},{1,3},{2,0},{3,1},{4,6},{5,7},{6,4},{7,5},{8,10},{9,11},{10,... | collective-permute-start | bytes 3145736 | tf_op jit(solution)/shard_map/ppermute | solution.py:316
  451.2 223.2 %collective-permute-start.42 = (f32[4,128,768]{2,1,0:T(8,128)}, f32[4,128,768]{2,1,0:T(8,128)}, u32[]{:S(2)}, u32[]{:S(2)}) collective-permute-start(f32[4,128,768]{2,1,0:T(8,128)} %get-tuple-element.141), channel_id=1, source_target_pairs={{0,8},{8,0},{1,9},{9,1},{2,10},{10,2},{3,11},{11,3},{4,12},{12,4},... | collective-permute-start | bytes 4718600 | tf_op jit(solution)/shard_map/ppermute | solution.py:315
  650.1 82.6 %collective-permute-start.30 = (f32[4,128,768]{2,1,0:T(8,128)}, f32[4,128,768]{2,1,0:T(8,128)}, u32[]{:S(2)}, u32[]{:S(2)}) collective-permute-start(f32[4,128,768]{2,1,0:T(8,128)} %get-tuple-element.124), channel_id=1, source_target_pairs={{0,4},{1,5},{2,6},{3,7},{4,0},{5,1},{6,2},{7,3},{8,12},{9,13},{10,... | collective-permute-start | bytes 4718600 | tf_op jit(solution)/shard_map/ppermute | solution.py:316
  673.2 382.9 %collective-permute-start.14 = (f32[2,2,2,8,128,256]{5,4,3,2,1,0:T(8,128)}, f32[2,2,2,8,128,256]{5,4,3,2,1,0:T(8,128)}, u32[]{:S(2)}, u32[]{:S(2)}) collective-permute-start(f32[2,2,2,8,128,256]{5,4,3,2,1,0:T(8,128)} %get-tuple-element.103), channel_id=1, source_target_pairs={{0,1},{1,0},{2,3},{3,2},{4,5},{5,4},{6,7},{7,6},{8,9},{9,8},{10,11... | collective-permute-start | bytes 25165832 | tf_op jit(solution)/shard_map/ppermute | solution.py:316
  686.4 123.9 %collective-permute-start.34 = (f32[2,128,512]{2,1,0:T(8,128)}, f32[2,128,512]{2,1,0:T(8,128)}, u32[]{:S(2)}, u32[]{:S(2)}) collective-permute-start(f32[2,128,512]{2,1,0:T(8,128)} %get-tuple-element.131), channel_id=1, source_target_pairs={{0,4},{1,5},{2,6},{3,7},{4,0},{5,1},{6,2},{7,3},{8,12},{9,13},{10,... | collective-permute-start | bytes 1572872 | tf_op jit(solution)/shard_map/ppermute | solution.py:316
  688.4 123.5 %collective-permute-start.45 = (f32[2,128,768]{2,1,0:T(8,128)}, f32[2,128,768]{2,1,0:T(8,128)}, u32[]{:S(2)}, u32[]{:S(2)}) collective-permute-start(f32[2,128,768]{2,1,0:T(8,128)} %get-tuple-element.149), channel_id=1, source_target_pairs={{0,2},{1,3},{2,0},{3,1},{4,6},{5,7},{6,4},{7,5},{8,10},{9,11},{10,... | collective-permute-start | bytes 2359304 | tf_op jit(solution)/shard_map/ppermute | solution.py:316
  732.2 79.7 %collective-permute-start.46 = (f32[2,128,768]{2,1,0:T(8,128)}, f32[2,128,768]{2,1,0:T(8,128)}, u32[]{:S(2)}, u32[]{:S(2)}) collective-permute-start(f32[2,128,768]{2,1,0:T(8,128)} %get-tuple-element.150), channel_id=1, source_target_pairs={{0,8},{8,0},{1,9},{9,1},{2,10},{10,2},{3,11},{11,3},{4,12},{12,4},... | collective-permute-start | bytes 2359304 | tf_op jit(solution)/shard_map/ppermute | solution.py:315
  732.7 79.8 %collective-permute-start.32 = (f32[2,128,768]{2,1,0:T(8,128)}, f32[2,128,768]{2,1,0:T(8,128)}, u32[]{:S(2)}, u32[]{:S(2)}) collective-permute-start(f32[2,128,768]{2,1,0:T(8,128)} %get-tuple-element.129), channel_id=1, source_target_pairs={{0,2},{1,3},{2,0},{3,1},{4,6},{5,7},{6,4},{7,5},{8,10},{9,11},{10,... | collective-permute-start | bytes 2359304 | tf_op jit(solution)/shard_map/ppermute | solution.py:316
  810.4 244.2 %collective-permute-start.51 = (f32[4,128,2048]{2,1,0:T(8,128)}, f32[4,128,2048]{2,1,0:T(8,128)}, u32[]{:S(2)}, u32[]{:S(2)}) collective-permute-start(f32[4,128,2048]{2,1,0:T(8,128)} %get-tuple-element.153), channel_id=1, source_target_pairs={{0,8},{8,0},{1,9},{9,1},{2,10},{10,2},{3,11},{11,3},{4,12},{12,4},... | collective-permute-start | bytes 12582920 | tf_op jit(solution)/shard_map/ppermute | solution.py:315
  811.9 109.6 %collective-permute-start.24 = (f32[2,2,2,4,128,256]{5,4,3,2,1,0:T(8,128)}, f32[2,2,2,4,128,256]{5,4,3,2,1,0:T(8,128)}, u32[]{:S(2)}, u32[]{:S(2)}) collective-permute-start(f32[2,2,2,4,128,256]{5,4,3,2,1,0:T(8,128)} %get-tuple-element.115), channel_id=1, source_target_pairs={{0,1},{1,0},{2,3},{3,2},{4,5},{5,4},{6,7},{7,6},{8,9},{9,8},{10,11... | collective-permute-start | bytes 12582920 | tf_op jit(solution)/shard_map/ppermute | solution.py:316
  811.9 174.4 %collective-permute-start.19 = (f32[2,2,2,4,128,256]{5,4,3,2,1,0:T(8,128)}, f32[2,2,2,4,128,256]{5,4,3,2,1,0:T(8,128)}, u32[]{:S(2)}, u32[]{:S(2)}) collective-permute-start(f32[2,2,2,4,128,256]{5,4,3,2,1,0:T(8,128)} %get-tuple-element.109), channel_id=1, source_target_pairs={{0,1},{1,0},{2,3},{3,2},{4,5},{5,4},{6,7},{7,6},{8,9},{9,8},{10,11... | collective-permute-start | bytes 12582920 | tf_op jit(solution)/shard_map/ppermute | solution.py:316
  812.4 107.7 %collective-permute-start.33 = (f32[2,128,768]{2,1,0:T(8,128)}, f32[2,128,768]{2,1,0:T(8,128)}, u32[]{:S(2)}, u32[]{:S(2)}) collective-permute-start(f32[2,128,768]{2,1,0:T(8,128)} %get-tuple-element.130), channel_id=1, source_target_pairs={{0,8},{8,0},{1,9},{9,1},{2,10},{10,2},{3,11},{11,3},{4,12},{12,4},... | collective-permute-start | bytes 2359304 | tf_op jit(solution)/shard_map/ppermute | solution.py:315
  920.2 65.6 %collective-permute-start.62 = (f32[4,352,512]{2,1,0:T(8,128)}, f32[4,352,512]{2,1,0:T(8,128)S(1)}, u32[]{:S(2)}, u32[]{:S(2)}) collective-permute-start(f32[4,352,512]{2,1,0:T(8,128)} %get-tuple-element.172), channel_id=1, source_target_pairs={{0,2},{1,3},{2,0},{3,1},{4,6},{5,7},{6,4},{7,5},{8,10},{9,11},{10,... | collective-permute-start | bytes 8650760 | tf_op jit(solution)/shard_map/ppermute | solution.py:316
  921.5 131.6 %collective-permute-start.53 = (f32[4,128,1536]{2,1,0:T(8,128)}, f32[4,128,1536]{2,1,0:T(8,128)S(1)}, u32[]{:S(2)}, u32[]{:S(2)}) collective-permute-start(f32[4,128,1536]{2,1,0:T(8,128)} %get-tuple-element.159), channel_id=1, source_target_pairs={{0,2},{1,3},{2,0},{3,1},{4,6},{5,7},{6,4},{7,5},{8,10},{9,11},{10,... | collective-permute-start | bytes 9437192 | tf_op jit(solution)/shard_map/ppermute | solution.py:316
  985.7 75.9 %collective-permute-start.27 = (f32[2,4,128,256]{3,2,1,0:T(8,128)S(1)}, f32[2,4,128,256]{3,2,1,0:T(8,128)S(1)}, u32[]{:S(2)}, u32[]{:S(2)}) collective-permute-start(f32[2,4,128,256]{3,2,1,0:T(8,128)S(1)} %get-tuple-element.203), channel_id=1, source_target_pairs={{0,4},{1,5},{2,6},{3,7},{4,0},{5,1},{6,2},{7,3},{8,12},{9,13},{10,... | collective-permute-start | bytes 3145736 | tf_op jit(solution)/shard_map/ppermute | solution.py:316
  986.4 89.2 %collective-permute-start.25 = (f32[2,4,128,256]{3,2,1,0:T(8,128)S(1)}, f32[2,4,128,256]{3,2,1,0:T(8,128)S(1)}, u32[]{:S(2)}, u32[]{:S(2)}) collective-permute-start(f32[2,4,128,256]{3,2,1,0:T(8,128)S(1)} %get-tuple-element.204), channel_id=1, source_target_pairs={{0,2},{1,3},{2,0},{3,1},{4,6},{5,7},{6,4},{7,5},{8,10},{9,11},{10,... | collective-permute-start | bytes 3145736 | tf_op jit(solution)/shard_map/ppermute | solution.py:316
  1054.5 283.7 %collective-permute-start.60 = (f32[4,352,768]{2,1,0:T(8,128)}, f32[4,352,768]{2,1,0:T(8,128)S(1)}, u32[]{:S(2)}, u32[]{:S(2)}) collective-permute-start(f32[4,352,768]{2,1,0:T(8,128)} %get-tuple-element.166), channel_id=1, source_target_pairs={{0,8},{8,0},{1,9},{9,1},{2,10},{10,2},{3,11},{11,3},{4,12},{12,4},... | collective-permute-start | bytes 12976136 | tf_op jit(solution)/shard_map/ppermute | solution.py:315
  1056.1 179.3 %collective-permute-start.52 = (f32[4,128,2048]{2,1,0:T(8,128)}, f32[4,128,2048]{2,1,0:T(8,128)}, u32[]{:S(2)}, u32[]{:S(2)}) collective-permute-start(f32[4,128,2048]{2,1,0:T(8,128)} %get-tuple-element.156), channel_id=1, source_target_pairs={{0,4},{1,5},{2,6},{3,7},{4,0},{5,1},{6,2},{7,3},{8,12},{9,13},{10,... | collective-permute-start | bytes 12582920 | tf_op jit(solution)/shard_map/ppermute | solution.py:316
  1076.6 137.4 %collective-permute-start.17 = (f32[2,8,128,256]{3,2,1,0:T(8,128)S(1)}, f32[2,8,128,256]{3,2,1,0:T(8,128)S(1)}, u32[]{:S(2)}, u32[]{:S(2)}) collective-permute-start(f32[2,8,128,256]{3,2,1,0:T(8,128)S(1)} %get-tuple-element.183), channel_id=1, source_target_pairs={{0,4},{1,5},{2,6},{3,7},{4,0},{5,1},{6,2},{7,3},{8,12},{9,13},{10,... | collective-permute-start | bytes 6291464 | tf_op jit(solution)/shard_map/ppermute | solution.py:316
  1080.1 266.2 %collective-permute-start.61 = (f32[4,352,768]{2,1,0:T(8,128)}, f32[4,352,768]{2,1,0:T(8,128)S(1)}, u32[]{:S(2)}, u32[]{:S(2)}) collective-permute-start(f32[4,352,768]{2,1,0:T(8,128)} %get-tuple-element.169), channel_id=1, source_target_pairs={{0,4},{1,5},{2,6},{3,7},{4,0},{5,1},{6,2},{7,3},{8,12},{9,13},{10,... | collective-permute-start | bytes 12976136 | tf_op jit(solution)/shard_map/ppermute | solution.py:316
  1096.4 131.0 %collective-permute-start.15 = (f32[2,8,128,256]{3,2,1,0:T(8,128)S(1)}, f32[2,8,128,256]{3,2,1,0:T(8,128)}, u32[]{:S(2)}, u32[]{:S(2)}) collective-permute-start(f32[2,8,128,256]{3,2,1,0:T(8,128)S(1)} %get-tuple-element.184), channel_id=1, source_target_pairs={{0,2},{1,3},{2,0},{3,1},{4,6},{5,7},{6,4},{7,5},{8,10},{9,11},{10,... | collective-permute-start | bytes 6291464 | tf_op jit(solution)/shard_map/ppermute | solution.py:316
  1214.0 123.6 %collective-permute-start.65 = (f32[2,352,512]{2,1,0:T(8,128)}, f32[2,352,512]{2,1,0:T(8,128)S(1)}, u32[]{:S(2)}, u32[]{:S(2)}) collective-permute-start(f32[2,352,512]{2,1,0:T(8,128)} %get-tuple-element.176), channel_id=1, source_target_pairs={{0,4},{1,5},{2,6},{3,7},{4,0},{5,1},{6,2},{7,3},{8,12},{9,13},{10,... | collective-permute-start | bytes 4325384 | tf_op jit(solution)/shard_map/ppermute | solution.py:316
  1234.6 114.2 %collective-permute-start.26 = (f32[4,128,256]{2,1,0:T(8,128)}, f32[4,128,256]{2,1,0:T(8,128)S(1)}, u32[]{:S(2)}, u32[]{:S(2)}) collective-permute-start(f32[4,128,256]{2,1,0:T(8,128)} %get-tuple-element.117), channel_id=1, source_target_pairs={{0,4},{1,5},{2,6},{3,7},{4,0},{5,1},{6,2},{7,3},{8,12},{9,13},{10,... | collective-permute-start | bytes 1572872 | tf_op jit(solution)/shard_map/ppermute | solution.py:316
  1235.4 115.8 %collective-permute-start.28 = (f32[4,128,256]{2,1,0:T(8,128)}, f32[4,128,256]{2,1,0:T(8,128)S(1)}, u32[]{:S(2)}, u32[]{:S(2)}) collective-permute-start(f32[4,128,256]{2,1,0:T(8,128)} %get-tuple-element.119), channel_id=1, source_target_pairs={{0,2},{1,3},{2,0},{3,1},{4,6},{5,7},{6,4},{7,5},{8,10},{9,11},{10,... | collective-permute-start | bytes 1572872 | tf_op jit(solution)/shard_map/ppermute | solution.py:316
  1351.2 96.9 %collective-permute-start.56 = (f32[2,128,1536]{2,1,0:T(8,128)}, f32[2,128,1536]{2,1,0:T(8,128)}, u32[]{:S(2)}, u32[]{:S(2)}) collective-permute-start(f32[2,128,1536]{2,1,0:T(8,128)} %get-tuple-element.163), channel_id=1, source_target_pairs={{0,4},{1,5},{2,6},{3,7},{4,0},{5,1},{6,2},{7,3},{8,12},{9,13},{10,... | collective-permute-start | bytes 4718600 | tf_op jit(solution)/shard_map/ppermute | solution.py:316
  1360.0 89.7 %collective-permute-start.54 = (f32[2,128,2048]{2,1,0:T(8,128)}, f32[2,128,2048]{2,1,0:T(8,128)}, u32[]{:S(2)}, u32[]{:S(2)}) collective-permute-start(f32[2,128,2048]{2,1,0:T(8,128)} %get-tuple-element.161), channel_id=1, source_target_pairs={{0,2},{1,3},{2,0},{3,1},{4,6},{5,7},{6,4},{7,5},{8,10},{9,11},{10,... | collective-permute-start | bytes 6291464 | tf_op jit(solution)/shard_map/ppermute | solution.py:316
  1364.4 70.5 %collective-permute-start.48 = (f32[128,768]{1,0:T(8,128)}, f32[128,768]{1,0:T(8,128)S(1)}, u32[]{:S(2)}, u32[]{:S(2)}) collective-permute-start(f32[128,768]{1,0:T(8,128)} %fusion.69), channel_id=1, source_target_pairs={{0,4},{1,5},{2,6},{3,7},{4,0},{5,1},{6,2},{7,3},{8,12},{9,13},{10,... | collective-permute-start | bytes 1179656 | tf_op jit(solution)/shard_map/ppermute | solution.py:316
  1382.5 99.1 %collective-permute-start.55 = (f32[2,128,2048]{2,1,0:T(8,128)}, f32[2,128,2048]{2,1,0:T(8,128)}, u32[]{:S(2)}, u32[]{:S(2)}) collective-permute-start(f32[2,128,2048]{2,1,0:T(8,128)} %get-tuple-element.162), channel_id=1, source_target_pairs={{0,8},{8,0},{1,9},{9,1},{2,10},{10,2},{3,11},{11,3},{4,12},{12,4},... | collective-permute-start | bytes 6291464 | tf_op jit(solution)/shard_map/ppermute | solution.py:315
  (90 other events, 2770.6 us)

commit v2 on v1

--- a/solution.py
+++ b/solution.py
@@ -307,6 +307,7 @@
 
 BITS = {'c': 1, 'x': 2, 'y': 4}
 ALL_VMEM = pltpu.CompilerParams(vmem_limit_bytes=63 * 2**20)
+FF_PARAMS = pltpu.CompilerParams(vmem_limit_bytes=63 * 2**20)
 NEXT = {'x': ('y', 'z'), 'y': ('z', 'x'), 'z': ('x', 'y')}
 
 
@@ -430,7 +431,7 @@
     return pl.pallas_call(
         ff_kernel, grid_spec=grid_spec, name='ff_block',
         out_shape=[jax.ShapeDtypeStruct((2, 2, 2, 2, FF_ROWS, tokens), BF), jax.ShapeDtypeStruct((tokens, 5632), BF)],
-        cost_estimate=timed(60), compiler_params=ALL_VMEM)(bits, h, w_up, ga)
+        cost_estimate=timed(60), compiler_params=FF_PARAMS)(bits, h, w_up, ga)
 
 
 def color_of(n, plan):
@@ -444,22 +445,22 @@
 def pair_kernel(plan, rows, turned, *refs):
     n, steps = pl.program_id(Z), sum(count for _, count in plan)
     count = len(plan)
-    if turned:
-        left, refs = refs[Z], refs[1:]
-        take = lambda place, core: left[place, core]
-    else:
-        parts, left, refs = refs[:16], refs[-1], refs[16:-1]
-
-        @pl.when(n == Z)
-        def _():
-            for place in range(8):
-                for core in range(2):
-                    left[place, core] = parts[2 * place + core][...].T
-
-        take = lambda place, core: left[place, core]
+    source, left, load_sem = refs[Z], refs[-2], refs[-1]
+    parts, refs = (None, refs[1:-2]) if turned else (refs[-3], refs[1:-3])
+    me = lax.axis_index('cp')
+    bits = (lax.axis_index('dp'), me // 4, (me // 2) % 2, me % 2)
+
+    def load(place, core):
+        if turned:
+            from_ref, to_ref = source.at[place, core], left.at[place, core]
+        else:
+            flips = (place // 4, place // 2 % 2, place % 2, core)
+            block = sum((1 - bit if flip else bit) * weight for bit, flip, weight in zip(bits, flips, (8, 4, 2, 1)))
+            from_ref, to_ref = source.at[:, pl.ds(pl.multiple_of(block * LANES, LANES), LANES)], parts.at[place, core]
+        return pltpu.make_async_copy(from_ref, to_ref, load_sem.at[place, core])
+
     right, outs = refs[Z], refs[1:1 + 2 * count]
     mine, sent, came, send_sem, recv_sem, free_sem = refs[1 + 2 * count:]
-    me = lax.axis_index('cp')
     other = {'cp': me + 1 - 2 * (me % 2)}
     mesh_id = pl.DeviceIdType.MESH
     now, then = n % 2, (n + 1) % 2
@@ -470,6 +471,9 @@
 
     @pl.when(n == Z)
     def _():
+        for core in (1, Z):
+            for place in range(8):
+                load(place, core).start()
         barrier = pltpu.get_barrier_semaphore()
         pl.semaphore_signal(barrier, inc=1, device_id=other, device_id_type=mesh_id)
         pl.semaphore_wait(barrier, 1)
@@ -482,13 +486,26 @@
     def _():
         copy(then).start()
 
-    @pl.when(n < steps)
-    def _():
+    def products(first):
         some = 1 if turned else 4
         for core, dest in ((1, sent), (Z, mine)):
             for place in range(Z, 8, some):
-                tile = jnp.concatenate([take(place + k, core) for k in range(some)], axis=Z)
+                group = range(place, place + some)
+                if first:
+                    for k in group:
+                        load(k, core).wait()
+                        if not turned:
+                            left[k, core] = parts[k, core].T
+                tile = jnp.concatenate([left[k, core] for k in group], axis=Z)
                 dest[now, place:place + some] = nn(tile, right[...]).reshape(some, rows, -1)
+
+    @pl.when(n == Z)
+    def _():
+        products(True)
+
+    @pl.when((n >= 1) & (n < steps))
+    def _():
+        products(False)
 
     @pl.when(n >= 1)
     def _():
@@ -511,20 +528,6 @@
     turned = left.ndim == 4
     rows = left.shape[2] if turned else LANES
     steps = sum(count for _, count in plan)
-    once = pl.Buffered(1)
-    if turned:
-        left_specs = [pl.BlockSpec((8, 2, rows, MODEL), lambda n: (Z, Z, Z, Z), pipeline_mode=once)]
-    else:
-        def column(place, core):
-            def at(n):
-                me = lax.axis_index('cp')
-                bits = (lax.axis_index('dp'), me // 4, (me // 2) % 2, me % 2)
-                flips = (place // 4, place // 2 % 2, place % 2, core)
-                return Z, sum((1 - bit if flip else bit) * weight for bit, flip, weight in zip(bits, flips, (8, 4, 2, 1)))
-
-            return at
-
-        left_specs = [pl.BlockSpec((MODEL, LANES), column(place, core), pipeline_mode=once) for place in range(8) for core in range(2)]
     out_specs, out_shape, edge = [], [], Z
     for _, count in plan:
         spec = pl.BlockSpec((4, rows, tile), lambda n, edge=edge, count=count: (Z, Z, jnp.clip(n - 1 - edge, Z, count - 1)))
@@ -533,13 +536,16 @@
         edge += count
     both = pltpu.VMEM((2, 8, rows, tile), F32)
     two = pltpu.SemaphoreType.DMA((2,))
+    staging = [] if turned else [pltpu.VMEM((8, 2, MODEL, LANES), BF)]
     return pl.pallas_call(
         functools.partial(pair_kernel, plan, rows, turned), grid=(steps + 1,), name='pair',
-        in_specs=left_specs + [pl.BlockSpec((MODEL, tile), lambda n: (Z, jnp.minimum(n, steps - 1)))], out_specs=out_specs, out_shape=out_shape,
-        scratch_shapes=[both, both, both, two, two, pltpu.SemaphoreType.REGULAR] + ([] if turned else [pltpu.VMEM((8, 2, LANES, MODEL), BF)]),
+        in_specs=[pl.BlockSpec(memory_space=pl.ANY), pl.BlockSpec((MODEL, tile), lambda n: (Z, jnp.minimum(n, steps - 1)))],
+        out_specs=out_specs, out_shape=out_shape,
+        scratch_shapes=[both, both, both, two, two, pltpu.SemaphoreType.REGULAR, *staging, pltpu.VMEM((8, 2, rows, MODEL), BF),
+                        pltpu.SemaphoreType.DMA((8, 2))],
         cost_estimate=timed(16 * rows * steps * tile * 4096 / 9e8),
         compiler_params=pltpu.CompilerParams(vmem_limit_bytes=63 * 2**20, collective_id=call_id, has_side_effects=True),
-    )(*([left] * len(left_specs)), right)
+    )(left, right)
 
 
 def halve(keep, got, axis):
@@ -640,8 +646,8 @@
 
 
 CHUNKS = ((Z, 8), (8, 4), (12, 4))
-PLAN_UP = (('z', 4), ('y', 4), ('x', 3))
-PLAN_D = (('z', 3), ('y', 3), ('x', 2))
+PLAN_UP = (('z', 5), ('y', 3), ('x', 3))
+PLAN_D = (('z', 4), ('y', 2), ('x', 2))
 
 
 def solution(mesh):

time: 1600 us -> 1580 us (0.988)
  waiting for transfers between devices: 618 us -> 585 us
    ppermute x56, waiting for transfers between devices: 540 us -> 388 us  [swap(): return lax.ppermute(values, 'cp', [(i, i ^ BITS[link]) for i in range(8)])]
    ppermute x13, waiting for transfers between devices: 77.8 us -> 197 us  [swap(): return lax.ppermute(values, 'dp', [(Z, 1), (1, Z)])]
  transfers between devices with their start and end apart: 69 -> 69, of which waited for: 22 -> 21; matrix products, arithmetic and copies ran while one was open for 5% -> 5% of each run, Pallas kernels for 34% -> 34%
where the time goes in v2:
time: 1580 us; the launch traced here: 1570 us
  Pallas kernels  823 us (52%)
  waiting for transfers between devices  585 us (37%)
  other arithmetic  85.5 us (5%)
  starting transfers between devices  68 us (4%)
    ppermute x56, waiting for transfers between devices, swap(): return lax.ppermute(values, 'cp', [(i, i ^ BITS[link]) for i in range(8)])  388 us
    pallas_call x4, Pallas kernels, pair_call(): pl.pallas_call(functools.partial(pair_kernel, plan, rows, turned), grid=(...  217 us
    ppermute x13, waiting for transfers between devices, swap(): return lax.ppermute(values, 'dp', [(Z, 1), (1, Z)])  197 us
    pallas_call x5, Pallas kernels, mm(): pl.pallas_call(functools.partial(mm_kernel, nt if flip else nn, added is...  194 us
    pallas_call x3, Pallas kernels, attn_bwd(): pl.pallas_call(functools.partial(bwd_kernel, scale, scale2, aliased), gri...  158 us
    pallas_call x2, Pallas kernels, attn_fwd(): pl.pallas_call(functools.partial(fwd_kernel, scale2, aliased), grid_spec=...  90.6 us
    pallas_call x1, Pallas kernels, ff_block(): pl.pallas_call(ff_kernel, grid_spec=grid_spec, name='ff_block', out_shape...  85.4 us
    ppermute x56, starting transfers between devices, swap(): return lax.ppermute(values, 'cp', [(i, i ^ BITS[link]) for i in range(8)])  51.6 us
  transfers between devices with their start and end apart: 69, of which 21 were waited for; matrix products, arithmetic and copies ran while one was open for 5% of the time, Pallas kernels for 34%

profile of v2, /device:TPU:0, one launch (start us, length us, event | category | flops | bytes accessed | tf_op | source)
XLA Modules:
  0.0 1568.4 jit_solution(13009160530209742488)
XLA Ops:
  15.1 22.2 %collective-permute-done.8.refs_2_ = bf16[8,128,512]{2,1,0:T(8,128)(2,1)} collective-permute-done((bf16[8,128,512]{2,1,0:T(8,128)(2,1)}, bf16[8,128,512]{2,1,0:T(8,128)(2,1)}, u32[]{:S(2)}, u32[]{:S(2)}) %collective-permute-start.8) | collective-permute-done | bytes 1048608 | tf_op jit(solution)/shard_map/ppermute | solution.py:317
  39.4 60.9 %mm.7.ga_ref = bf16[2048,5632]{1,0:T(8,128)(2,1)} custom-call(bf16[2048,2048]{1,0:T(8,128)(2,1)} %bitcast.399, bf16[5632,2048]{1,0:T(8,128)(2,1)} %w_ref.3), custom_call_target="tpu_custom_call" | custom-call | flops 47244640256 | bytes 1048576 | tf_op jit(solution)/shard_map/mm/pallas_call | solution.py:340
  102.9 23.7 %mm.5 = bf16[2048,2048]{1,0:T(8,128)(2,1)} custom-call(bf16[2048,2048]{1,0:T(8,128)(2,1)} %bitcast.403, bf16[2048,2048]{1,0:T(8,128)(2,1)} %bitcast.408), custom_call_target="tpu_custom_call" | custom-call | flops 17179869184 | bytes 1048576 | tf_op jit(solution)/shard_map/mm/pallas_call | solution.py:340
  127.7 45.3 %attn_fwd.2 = (bf16[16,128,2048]{2,1,0:T(8,128)(2,1)}, f32[32,2,512]{2,1,0:T(2,128)}) custom-call(s32[1]{0:T(128)} %bitcast.4.me_ref, bf16[16,128,2048]{2,1,0:T(8,128)(2,1)} %bitcast.429, bf16[8,128,512]{2,1,0:T(8,128)(2,1)} %bitcast.426, bf16[8,128,512]{2,1,0:T(8,128)(2,1)} %collective-permute-done.7.refs_1_, ...), custom_call_target="tpu_custom_call" | custom-call | flops 43200000000 | bytes 1048576 | tf_op jit(solution)/shard_map/attn_fwd/pallas_call | solution.py:274
  173.0 45.3 %attn_fwd.3 = (bf16[16,128,2048]{2,1,0:T(8,128)(2,1)}, f32[32,2,512]{2,1,0:T(2,128)}) custom-call(s32[1]{0:T(128)} %bitcast.4.me_ref, bf16[16,128,2048]{2,1,0:T(8,128)(2,1)} %bitcast.430, bf16[8,128,512]{2,1,0:T(8,128)(2,1)} %bitcast.420, bf16[8,128,512]{2,1,0:T(8,128)(2,1)} %collective-permute-done.refs_1_, ...), custom_call_target="tpu_custom_call", output_to_operand_aliasing={{0}: (10, {})} | custom-call | flops 43200000000 | bytes 1048576 | tf_op jit(solution)/shard_map/attn_fwd/pallas_call | solution.py:274
  218.4 24.8 %mm.6.h_ref.refs_0_ = bf16[2048,2048]{1,0:T(8,128)(2,1)} custom-call(bf16[2048,2048]{1,0:T(8,128)(2,1)} %bitcast.438, bf16[2048,2048]{1,0:T(8,128)(2,1)} %bitcast.397, bf16[2048,2048]{1,0:T(8,128)(2,1)} %bitcast.404), custom_call_target="tpu_custom_call" | custom-call | flops 17179869184 | bytes 1048576 | tf_op jit(solution)/shard_map/mm/pallas_call | solution.py:340
  243.2 85.4 %ff_block.1 = (bf16[2,2,2,2,352,2048]{5,4,3,2,1,0:T(8,128)(2,1)}, bf16[2048,5632]{1,0:T(8,128)(2,1)}) custom-call(s32[4]{0:T(128)} %pad_add_fusion.bits_ref, bf16[2048,2048]{1,0:T(8,128)(2,1)} %mm.6.h_ref.refs_0_, bf16[2048,5632]{1,0:T(8,128)(2,1)} %w_ref.5, bf16[2048,5632]{1,0:T(8,128)(2,1)} %mm.7.ga_ref), custom_call_target="tpu_custom_call" | custom-call | flops 54000001024 | bytes 1048576 | tf_op jit(solution)/shard_map/ff_block/pallas_call | solution.py:431
  328.6 61.1 %mm.8.x_ref.h_ref.refs_0_ = bf16[2048,2048]{1,0:T(8,128)(2,1)} custom-call(bf16[2048,5632]{1,0:T(8,128)(2,1)} %get-tuple-element.96.x_ref.refs_1_, bf16[2048,5632]{1,0:T(8,128)(2,1)} %w_ref.5, bf16[2048,2048]{1,0:T(8,128)(2,1)} %bitcast.400), custom_call_target="tpu_custom_call" | custom-call | flops 47244640256 | bytes 1048576 | tf_op jit(solution)/shard_map/mm/pallas_call | solution.py:340
  389.6 33.3 %pair.5 = (f32[4,128,1024]{2,1,0:T(8,128)}, f32[4,128,1024]{2,1,0:T(8,128)}, f32[4,128,512]{2,1,0:T(8,128)}, f32[4,128,512]{2,1,0:T(8,128)}, f32[4,128,512]{2,1,0:T(8,128)}, /*index=5*/f32[4,128,512]{2,1,0:T(8,128)}) custom-call(bf16[2048,2048]{1,0:T(8,128)(2,1)} %mm.8.x_ref.h_ref.refs_0_, bf16[2048,2048]{1,0:T(8,128)(2,1)} %bitcast.439), custom_call_target="tpu_custom_call" | custom-call | flops 17179869184 | bytes 1048576 | tf_op jit(solution)/shard_map/pair/pallas_call | solution.py:540
  422.9 23.7 %mm.9 = bf16[2048,2048]{1,0:T(8,128)(2,1)} custom-call(bf16[2048,2048]{1,0:T(8,128)(2,1)} %mm.8.x_ref.h_ref.refs_0_, bf16[2048,2048]{1,0:T(8,128)(2,1)} %bitcast.398), custom_call_target="tpu_custom_call" | custom-call | flops 17179869184 | bytes 1048576 | tf_op jit(solution)/shard_map/mm/pallas_call | solution.py:340
  447.8 78.0 %attn_bwd.3 = (bf16[16,128,2048]{2,1,0:T(8,128)(2,1)}, f32[2,2,2,8,128,256]{5,4,3,2,1,0:T(8,128)}, f32[2,2,2,8,128,256]{5,4,3,2,1,0:T(8,128)}) custom-call(s32[1]{0:T(128)} %bitcast.4.me_ref, bf16[16,128,2048]{2,1,0:T(8,128)(2,1)} %bitcast.431, bf16[16,128,2048]{2,1,0:T(8,128)(2,1)} %bitcast.434, f32[32,2,512]{2,1,0:T(2,128)} %get-tuple-element.98.lse_ref, ...), custom_call_target="tpu_custom_call" | custom-call | flops 71999995904 | bytes 1048576 | tf_op jit(solution)/shard_map/attn_bwd/pallas_call | solution.py:299
  525.8 40.1 %attn_bwd.4 = (bf16[16,128,2048]{2,1,0:T(8,128)(2,1)}, f32[2,2,2,4,128,256]{5,4,3,2,1,0:T(8,128)}, f32[2,2,2,4,128,256]{5,4,3,2,1,0:T(8,128)}) custom-call(s32[1]{0:T(128)} %bitcast.4.me_ref, bf16[16,128,2048]{2,1,0:T(8,128)(2,1)} %bitcast.432, bf16[16,128,2048]{2,1,0:T(8,128)(2,1)} %bitcast.435, ...), custom_call_target="tpu_custom_call", output_to_operand_aliasing={{0}: (12, {})} | custom-call | flops 35999997952 | bytes 1048576 | tf_op jit(solution)/shard_map/attn_bwd/pallas_call | solution.py:299
  565.8 40.4 %attn_bwd.5 = (bf16[16,128,2048]{2,1,0:T(8,128)(2,1)}, f32[2,2,2,4,128,256]{5,4,3,2,1,0:T(8,128)}, f32[2,2,2,4,128,256]{5,4,3,2,1,0:T(8,128)}) custom-call(s32[1]{0:T(128)} %bitcast.4.me_ref, bf16[16,128,2048]{2,1,0:T(8,128)(2,1)} %bitcast.433, bf16[16,128,2048]{2,1,0:T(8,128)(2,1)} %bitcast.436, ...), custom_call_target="tpu_custom_call", output_to_operand_aliasing={{0}: (12, {})} | custom-call | flops 35999997952 | bytes 1048576 | tf_op jit(solution)/shard_map/attn_bwd/pallas_call | solution.py:299
  606.3 32.8 %pair.4 = (f32[4,128,1024]{2,1,0:T(8,128)}, f32[4,128,1024]{2,1,0:T(8,128)}, f32[4,128,512]{2,1,0:T(8,128)}, f32[4,128,512]{2,1,0:T(8,128)}, f32[4,128,512]{2,1,0:T(8,128)}, /*index=5*/f32[4,128,512]{2,1,0:T(8,128)}) custom-call(bf16[2048,2048]{1,0:T(8,128)(2,1)} %bitcast.405, bf16[2048,2048]{1,0:T(8,128)(2,1)} %bitcast.440), custom_call_target="tpu_custom_call" | custom-call | flops 17179869184 | bytes 1048576 | tf_op jit(solution)/shard_map/pair/pallas_call | solution.py:540
  650.0 14.5 collective-permute-done.30
  670.0 76.9 %collective-permute-done.46.refs_4_ = f32[2,128,512]{2,1,0:T(8,128)S(1)} collective-permute-done((f32[2,128,512]{2,1,0:T(8,128)S(1)}, f32[2,128,512]{2,1,0:T(8,128)S(1)}, u32[]{:S(2)}, u32[]{:S(2)}) %collective-permute-start.46) | collective-permute-done | bytes 524320 | tf_op jit(solution)/shard_map/ppermute | solution.py:316
  748.3 72.2 %pair.7 = (f32[4,352,1024]{2,1,0:T(8,128)}, f32[4,352,1024]{2,1,0:T(8,128)}, f32[4,352,512]{2,1,0:T(8,128)}, f32[4,352,512]{2,1,0:T(8,128)}, f32[4,352,512]{2,1,0:T(8,128)}, /*index=5*/f32[4,352,512]{2,1,0:T(8,128)}) custom-call(bf16[8,2,352,2048]{3,2,1,0:T(8,128)(2,1)} %bitcast.428, bf16[2048,2048]{1,0:T(8,128)(2,1)} %bitcast.401), custom_call_target="tpu_custom_call" | custom-call | flops 47244640256 | bytes 1048576 | tf_op jit(solution)/shard_map/pair/pallas_call | solution.py:540
  823.2 79.1 %pair.6 = (f32[4,128,2560]{2,1,0:T(8,128)}, f32[4,128,2560]{2,1,0:T(8,128)}, f32[4,128,1536]{2,1,0:T(8,128)}, f32[4,128,1536]{2,1,0:T(8,128)}, f32[4,128,1536]{2,1,0:T(8,128)}, /*index=5*/f32[4,128,1536]{2,1,0:T(8,128)}) custom-call(bf16[2048,2048]{1,0:T(8,128)(2,1)} %mm.6.h_ref.refs_0_, bf16[2048,5632]{1,0:T(8,128)(2,1)} %get-tuple-element.96.x_ref.refs_1_), custom_call_target="tpu_custom_call" | custom-call | flops 47244640256 | bytes 1048576 | tf_op jit(solution)/shard_map/pair/pallas_call | solution.py:540
  907.1 65.8 %collective-permute-done.52 = f32[4,128,1536]{2,1,0:T(8,128)S(1)} collective-permute-done((f32[4,128,1536]{2,1,0:T(8,128)}, f32[4,128,1536]{2,1,0:T(8,128)S(1)}, u32[]{:S(2)}, u32[]{:S(2)}) %collective-permute-start.52) | collective-permute-done | bytes 3145760 | tf_op jit(solution)/shard_map/ppermute | solution.py:317
  993.3 13.6 collective-permute-done.45.refs_3_
  1007.5 19.9 %collective-permute-done.32.refs_3_ = f32[2,128,1024]{2,1,0:T(8,128)S(1)} collective-permute-done((f32[2,128,1024]{2,1,0:T(8,128)S(1)}, f32[2,128,1024]{2,1,0:T(8,128)S(1)}, u32[]{:S(2)}, u32[]{:S(2)}) %collective-permute-start.32) | collective-permute-done | bytes 1048608 | tf_op jit(solution)/shard_map/ppermute | solution.py:317
  1061.9 14.3 collective-permute-done.20
  1083.4 16.1 %collective-permute-done.17 = f32[2,8,128,256]{3,2,1,0:T(8,128)} collective-permute-done((f32[2,8,128,256]{3,2,1,0:T(8,128)}, f32[2,8,128,256]{3,2,1,0:T(8,128)}, u32[]{:S(2)}, u32[]{:S(2)}) %collective-permute-start.17) | collective-permute-done | bytes 2097184 | tf_op jit(solution)/shard_map/ppermute | solution.py:317
  1103.9 14.5 collective-permute-done.15
  1125.7 116.3 %collective-permute-done.64.refs_4_ = f32[2,352,512]{2,1,0:T(8,128)S(1)} collective-permute-done((f32[2,352,512]{2,1,0:T(8,128)}, f32[2,352,512]{2,1,0:T(8,128)S(1)}, u32[]{:S(2)}, u32[]{:S(2)}) %collective-permute-start.64) | collective-permute-done | bytes 1441824 | tf_op jit(solution)/shard_map/ppermute | solution.py:316
  1262.9 16.6 %collective-permute-done.16.refs_1_ = f32[8,128,256]{2,1,0:T(8,128)S(1)} collective-permute-done((f32[8,128,256]{2,1,0:T(8,128)}, f32[8,128,256]{2,1,0:T(8,128)S(1)}, u32[]{:S(2)}, u32[]{:S(2)}) %collective-permute-start.16) | collective-permute-done | bytes 1048608 | tf_op jit(solution)/shard_map/ppermute | solution.py:317
  1288.7 11.7 small.1
  1300.5 100.6 %collective-permute-done.49.refs_7_ = f32[128,512]{1,0:T(8,128)S(1)} collective-permute-done((f32[128,512]{1,0:T(8,128)}, f32[128,512]{1,0:T(8,128)S(1)}, u32[]{:S(2)}, u32[]{:S(2)}) %collective-permute-start.49) | collective-permute-done | bytes 262176 | tf_op jit(solution)/shard_map/ppermute | solution.py:317
  1421.7 29.4 %collective-permute-done.48.refs_6_ = f32[128,1024]{1,0:T(8,128)S(1)} collective-permute-done((f32[128,1024]{1,0:T(8,128)S(1)}, f32[128,1024]{1,0:T(8,128)S(1)}, u32[]{:S(2)}, u32[]{:S(2)}) %collective-permute-start.48) | collective-permute-done | bytes 524320 | tf_op jit(solution)/shard_map/ppermute | solution.py:317
  1461.0 34.0 %collective-permute-done.35.refs_6_ = f32[128,1024]{1,0:T(8,128)S(1)} collective-permute-done((f32[128,1024]{1,0:T(8,128)S(1)}, f32[128,1024]{1,0:T(8,128)S(1)}, u32[]{:S(2)}, u32[]{:S(2)}) %collective-permute-start.35) | collective-permute-done | bytes 524320 | tf_op jit(solution)/shard_map/ppermute | solution.py:317
  1530.7 16.9 %gx.2.refs_0_ = bf16[2048,2048]{1,0:T(8,128)(2,1)} custom-call(bf16[2048,2048]{1,0:T(8,128)(2,1)} %mm.8.x_ref.h_ref.refs_0_, bf16[2048,2048]{1,0:T(8,128)(2,1)} %bitcast.441, bf16[2048,512]{1,0:T(8,128)(2,1)} %bitcast.444, bf16[2048,2048]{1,0:T(8,128)(2,1)} %bitcast.409, bf16[256,2048]{1,0:T(8,128)(2,1)} %bitcast.412, bf16[256,2048]{1,0:T(8,128)(2,1)} %bitcast.415), custom_call_target="tpu_custom_call" | custom-call | flops 12600000512 | bytes 1048576 | tf_op jit(solution)/shard_map/gx/pallas_call | solution.py:389
  1550.2 16.9 %gx.3 = bf16[2048,2048]{1,0:T(8,128)(2,1)} custom-call(bf16[2048,2048]{1,0:T(8,128)(2,1)} %mm.8.x_ref.h_ref.refs_0_, bf16[2048,2048]{1,0:T(8,128)(2,1)} %bitcast.442, bf16[2048,512]{1,0:T(8,128)(2,1)} %bitcast.445, bf16[2048,2048]{1,0:T(8,128)(2,1)} %bitcast.410, bf16[256,2048]{1,0:T(8,128)(2,1)} %bitcast.413, ...), custom_call_target="tpu_custom_call", output_to_operand_aliasing={{}: (6, {})} | custom-call | flops 12600000512 | bytes 1048576 | tf_op jit(solution)/shard_map/gx/pallas_call | solution.py:389
  (268 shorter events, 220.7 us)
Async XLA Ops:
  13.0 88.0 %collective-permute-start.10 = (bf16[8,128,512]{2,1,0:T(8,128)(2,1)}, bf16[8,128,512]{2,1,0:T(8,128)(2,1)}, u32[]{:S(2)}, u32[]{:S(2)}) collective-permute-start(bf16[8,128,512]{2,1,0:T(8,128)(2,1)} %bitcast.424), channel_id=1, source_target_pairs={{0,4},{1,5},{2,6},{3,7},{4,0},{5,1},{6,2},{7,3},{8,12},{9,13},{10,... | collective-permute-start | bytes 3145736 | tf_op jit(solution)/shard_map/ppermute | solution.py:317
  14.5 86.4 %collective-permute-start.7 = (bf16[8,128,512]{2,1,0:T(8,128)(2,1)}, bf16[8,128,512]{2,1,0:T(8,128)(2,1)}, u32[]{:S(2)}, u32[]{:S(2)}) collective-permute-start(bf16[8,128,512]{2,1,0:T(8,128)(2,1)} %bitcast.425), channel_id=1, source_target_pairs={{0,1},{1,0},{2,3},{3,2},{4,5},{5,4},{6,7},{7,6},{8,9},{9,8},{10,11... | collective-permute-start | bytes 3145736 | tf_op jit(solution)/shard_map/ppermute | solution.py:317
  14.5 86.9 %collective-permute-start.3 = (bf16[8,128,512]{2,1,0:T(8,128)(2,1)}, bf16[8,128,512]{2,1,0:T(8,128)(2,1)}, u32[]{:S(2)}, u32[]{:S(2)}) collective-permute-start(bf16[8,128,512]{2,1,0:T(8,128)(2,1)} %bitcast.417), channel_id=1, source_target_pairs={{0,4},{1,5},{2,6},{3,7},{4,0},{5,1},{6,2},{7,3},{8,12},{9,13},{10,... | collective-permute-start | bytes 3145736 | tf_op jit(solution)/shard_map/ppermute | solution.py:317
  15.0 111.6 %collective-permute-start.1 = (bf16[8,128,512]{2,1,0:T(8,128)(2,1)}, bf16[8,128,512]{2,1,0:T(8,128)(2,1)}, u32[]{:S(2)}, u32[]{:S(2)}) collective-permute-start(bf16[8,128,512]{2,1,0:T(8,128)(2,1)} %bitcast.418), channel_id=1, source_target_pairs={{0,2},{1,3},{2,0},{3,1},{4,6},{5,7},{6,4},{7,5},{8,10},{9,11},{10,... | collective-permute-start | bytes 3145736 | tf_op jit(solution)/shard_map/ppermute | solution.py:317
  37.3 65.6 %collective-permute-start.12 = (bf16[8,128,512]{2,1,0:T(8,128)(2,1)}, bf16[8,128,512]{2,1,0:T(8,128)(2,1)}, u32[]{:S(2)}, u32[]{:S(2)}) collective-permute-start(bf16[8,128,512]{2,1,0:T(8,128)(2,1)} %collective-permute-done.8.refs_2_), channel_id=1, source_target_pairs={{0,4},{1,5},{2,6},{3,7},{4,0},{5,1},{6,2},{7,3},{8,12},{9,13},{10,... | collective-permute-start | bytes 3145736 | tf_op jit(solution)/shard_map/ppermute | solution.py:317
  446.7 197.0 %collective-permute-start.43 = (f32[4,128,512]{2,1,0:T(8,128)}, f32[4,128,512]{2,1,0:T(8,128)}, u32[]{:S(2)}, u32[]{:S(2)}) collective-permute-start(f32[4,128,512]{2,1,0:T(8,128)} %get-tuple-element.144), channel_id=1, source_target_pairs={{0,4},{1,5},{2,6},{3,7},{4,0},{5,1},{6,2},{7,3},{8,12},{9,13},{10,... | collective-permute-start | bytes 3145736 | tf_op jit(solution)/shard_map/ppermute | solution.py:317
  447.2 198.6 %collective-permute-start.44 = (f32[4,128,512]{2,1,0:T(8,128)}, f32[4,128,512]{2,1,0:T(8,128)}, u32[]{:S(2)}, u32[]{:S(2)}) collective-permute-start(f32[4,128,512]{2,1,0:T(8,128)} %get-tuple-element.147), channel_id=1, source_target_pairs={{0,2},{1,3},{2,0},{3,1},{4,6},{5,7},{6,4},{7,5},{8,10},{9,11},{10,... | collective-permute-start | bytes 3145736 | tf_op jit(solution)/shard_map/ppermute | solution.py:317
  642.0 180.6 %collective-permute-start.42 = (f32[4,128,1024]{2,1,0:T(8,128)}, f32[4,128,1024]{2,1,0:T(8,128)}, u32[]{:S(2)}, u32[]{:S(2)}) collective-permute-start(f32[4,128,1024]{2,1,0:T(8,128)} %get-tuple-element.141), channel_id=1, source_target_pairs={{0,8},{8,0},{1,9},{9,1},{2,10},{10,2},{3,11},{11,3},{4,12},{12,4},... | collective-permute-start | bytes 6291464 | tf_op jit(solution)/shard_map/ppermute | solution.py:316
  643.7 179.4 %collective-permute-start.29 = (f32[4,128,1024]{2,1,0:T(8,128)}, f32[4,128,1024]{2,1,0:T(8,128)}, u32[]{:S(2)}, u32[]{:S(2)}) collective-permute-start(f32[4,128,1024]{2,1,0:T(8,128)} %get-tuple-element.121), channel_id=1, source_target_pairs={{0,8},{8,0},{1,9},{9,1},{2,10},{10,2},{3,11},{11,3},{4,12},{12,4},... | collective-permute-start | bytes 6291464 | tf_op jit(solution)/shard_map/ppermute | solution.py:316
  645.9 101.0 %collective-permute-start.46 = (f32[2,128,512]{2,1,0:T(8,128)S(1)}, f32[2,128,512]{2,1,0:T(8,128)S(1)}, u32[]{:S(2)}, u32[]{:S(2)}) collective-permute-start(f32[2,128,512]{2,1,0:T(8,128)S(1)} %get-tuple-element.150), channel_id=1, source_target_pairs={{0,8},{8,0},{1,9},{9,1},{2,10},{10,2},{3,11},{11,3},{4,12},{12,4},... | collective-permute-start | bytes 1572872 | tf_op jit(solution)/shard_map/ppermute | solution.py:316
  664.6 156.0 %collective-permute-start.47 = (f32[2,128,512]{2,1,0:T(8,128)}, f32[2,128,512]{2,1,0:T(8,128)}, u32[]{:S(2)}, u32[]{:S(2)}) collective-permute-start(f32[2,128,512]{2,1,0:T(8,128)} %get-tuple-element.151), channel_id=1, source_target_pairs={{0,4},{1,5},{2,6},{3,7},{4,0},{5,1},{6,2},{7,3},{8,12},{9,13},{10,... | collective-permute-start | bytes 1572872 | tf_op jit(solution)/shard_map/ppermute | solution.py:317
  667.2 154.8 %collective-permute-start.33 = (f32[2,128,512]{2,1,0:T(8,128)}, f32[2,128,512]{2,1,0:T(8,128)}, u32[]{:S(2)}, u32[]{:S(2)}) collective-permute-start(f32[2,128,512]{2,1,0:T(8,128)} %get-tuple-element.130), channel_id=1, source_target_pairs={{0,8},{8,0},{1,9},{9,1},{2,10},{10,2},{3,11},{11,3},{4,12},{12,4},... | collective-permute-start | bytes 1572872 | tf_op jit(solution)/shard_map/ppermute | solution.py:316
  747.7 74.9 %collective-permute-start.34 = (f32[2,128,512]{2,1,0:T(8,128)}, f32[2,128,512]{2,1,0:T(8,128)}, u32[]{:S(2)}, u32[]{:S(2)}) collective-permute-start(f32[2,128,512]{2,1,0:T(8,128)} %get-tuple-element.131), channel_id=1, source_target_pairs={{0,4},{1,5},{2,6},{3,7},{4,0},{5,1},{6,2},{7,3},{8,12},{9,13},{10,... | collective-permute-start | bytes 1572872 | tf_op jit(solution)/shard_map/ppermute | solution.py:317
  820.5 81.7 %collective-permute-start.61 = (f32[4,352,512]{2,1,0:T(8,128)}, f32[4,352,512]{2,1,0:T(8,128)}, u32[]{:S(2)}, u32[]{:S(2)}) collective-permute-start(f32[4,352,512]{2,1,0:T(8,128)} %get-tuple-element.169), channel_id=1, source_target_pairs={{0,4},{1,5},{2,6},{3,7},{4,0},{5,1},{6,2},{7,3},{8,12},{9,13},{10,... | collective-permute-start | bytes 8650760 | tf_op jit(solution)/shard_map/ppermute | solution.py:317
  822.0 80.8 %collective-permute-start.62 = (f32[4,352,512]{2,1,0:T(8,128)}, f32[4,352,512]{2,1,0:T(8,128)}, u32[]{:S(2)}, u32[]{:S(2)}) collective-permute-start(f32[4,352,512]{2,1,0:T(8,128)} %get-tuple-element.172), channel_id=1, source_target_pairs={{0,2},{1,3},{2,0},{3,1},{4,6},{5,7},{6,4},{7,5},{8,10},{9,11},{10,... | collective-permute-start | bytes 8650760 | tf_op jit(solution)/shard_map/ppermute | solution.py:317
  822.6 158.3 %collective-permute-start.24 = (f32[2,2,2,4,128,256]{5,4,3,2,1,0:T(8,128)}, f32[2,2,2,4,128,256]{5,4,3,2,1,0:T(8,128)}, u32[]{:S(2)}, u32[]{:S(2)}) collective-permute-start(f32[2,2,2,4,128,256]{5,4,3,2,1,0:T(8,128)} %get-tuple-element.115), channel_id=1, source_target_pairs={{0,1},{1,0},{2,3},{3,2},{4,5},{5,4},{6,7},{7,6},{8,9},{9,8},{10,11... | collective-permute-start | bytes 12582920 | tf_op jit(solution)/shard_map/ppermute | solution.py:317
  822.6 159.7 %collective-permute-start.19 = (f32[2,2,2,4,128,256]{5,4,3,2,1,0:T(8,128)}, f32[2,2,2,4,128,256]{5,4,3,2,1,0:T(8,128)}, u32[]{:S(2)}, u32[]{:S(2)}) collective-permute-start(f32[2,2,2,4,128,256]{5,4,3,2,1,0:T(8,128)} %get-tuple-element.109), channel_id=1, source_target_pairs={{0,1},{1,0},{2,3},{3,2},{4,5},{5,4},{6,7},{7,6},{8,9},{9,8},{10,11... | collective-permute-start | bytes 12582920 | tf_op jit(solution)/shard_map/ppermute | solution.py:317
  823.1 205.7 %collective-permute-start.14 = (f32[2,2,2,8,128,256]{5,4,3,2,1,0:T(8,128)}, f32[2,2,2,8,128,256]{5,4,3,2,1,0:T(8,128)}, u32[]{:S(2)}, u32[]{:S(2)}) collective-permute-start(f32[2,2,2,8,128,256]{5,4,3,2,1,0:T(8,128)} %get-tuple-element.103), channel_id=1, source_target_pairs={{0,1},{1,0},{2,3},{3,2},{4,5},{5,4},{6,7},{7,6},{8,9},{9,8},{10,11... | collective-permute-start | bytes 25165832 | tf_op jit(solution)/shard_map/ppermute | solution.py:317
  902.2 70.6 %collective-permute-start.52 = (f32[4,128,1536]{2,1,0:T(8,128)}, f32[4,128,1536]{2,1,0:T(8,128)S(1)}, u32[]{:S(2)}, u32[]{:S(2)}) collective-permute-start(f32[4,128,1536]{2,1,0:T(8,128)} %get-tuple-element.156), channel_id=1, source_target_pairs={{0,4},{1,5},{2,6},{3,7},{4,0},{5,1},{6,2},{7,3},{8,12},{9,13},{10,... | collective-permute-start | bytes 9437192 | tf_op jit(solution)/shard_map/ppermute | solution.py:317
  902.8 77.6 %collective-permute-start.53 = (f32[4,128,1536]{2,1,0:T(8,128)}, f32[4,128,1536]{2,1,0:T(8,128)S(1)}, u32[]{:S(2)}, u32[]{:S(2)}) collective-permute-start(f32[4,128,1536]{2,1,0:T(8,128)} %get-tuple-element.159), channel_id=1, source_target_pairs={{0,2},{1,3},{2,0},{3,1},{4,6},{5,7},{6,4},{7,5},{8,10},{9,11},{10,... | collective-permute-start | bytes 9437192 | tf_op jit(solution)/shard_map/ppermute | solution.py:317
  972.9 271.2 %collective-permute-start.60 = (f32[4,352,1024]{2,1,0:T(8,128)}, f32[4,352,1024]{2,1,0:T(8,128)S(1)}, u32[]{:S(2)}, u32[]{:S(2)}) collective-permute-start(f32[4,352,1024]{2,1,0:T(8,128)} %get-tuple-element.166), channel_id=1, source_target_pairs={{0,8},{8,0},{1,9},{9,1},{2,10},{10,2},{3,11},{11,3},{4,12},{12,4},... | collective-permute-start | bytes 17301512 | tf_op jit(solution)/shard_map/ppermute | solution.py:316
  980.5 262.1 %collective-permute-start.51 = (f32[4,128,2560]{2,1,0:T(8,128)}, f32[4,128,2560]{2,1,0:T(8,128)}, u32[]{:S(2)}, u32[]{:S(2)}) collective-permute-start(f32[4,128,2560]{2,1,0:T(8,128)} %get-tuple-element.153), channel_id=1, source_target_pairs={{0,8},{8,0},{1,9},{9,1},{2,10},{10,2},{3,11},{11,3},{4,12},{12,4},... | collective-permute-start | bytes 15728648 | tf_op jit(solution)/shard_map/ppermute | solution.py:316
  1076.2 165.9 %collective-permute-start.64 = (f32[2,352,512]{2,1,0:T(8,128)}, f32[2,352,512]{2,1,0:T(8,128)S(1)}, u32[]{:S(2)}, u32[]{:S(2)}) collective-permute-start(f32[2,352,512]{2,1,0:T(8,128)} %get-tuple-element.175), channel_id=1, source_target_pairs={{0,8},{8,0},{1,9},{9,1},{2,10},{10,2},{3,11},{11,3},{4,12},{12,4},... | collective-permute-start | bytes 4325384 | tf_op jit(solution)/shard_map/ppermute | solution.py:316
  1099.5 146.0 %collective-permute-start.26 = (f32[4,128,256]{2,1,0:T(8,128)}, f32[4,128,256]{2,1,0:T(8,128)}, u32[]{:S(2)}, u32[]{:S(2)}) collective-permute-start(f32[4,128,256]{2,1,0:T(8,128)} %get-tuple-element.117), channel_id=1, source_target_pairs={{0,4},{1,5},{2,6},{3,7},{4,0},{5,1},{6,2},{7,3},{8,12},{9,13},{10,... | collective-permute-start | bytes 1572872 | tf_op jit(solution)/shard_map/ppermute | solution.py:317
  1118.3 133.8 %collective-permute-start.28 = (f32[4,128,256]{2,1,0:T(8,128)}, f32[4,128,256]{2,1,0:T(8,128)}, u32[]{:S(2)}, u32[]{:S(2)}) collective-permute-start(f32[4,128,256]{2,1,0:T(8,128)} %get-tuple-element.119), channel_id=1, source_target_pairs={{0,2},{1,3},{2,0},{3,1},{4,6},{5,7},{6,4},{7,5},{8,10},{9,11},{10,... | collective-permute-start | bytes 1572872 | tf_op jit(solution)/shard_map/ppermute | solution.py:317
  1252.1 150.6 %collective-permute-start.55 = (f32[2,128,1536]{2,1,0:T(8,128)}, f32[2,128,1536]{2,1,0:T(8,128)}, u32[]{:S(2)}, u32[]{:S(2)}) collective-permute-start(f32[2,128,1536]{2,1,0:T(8,128)} %get-tuple-element.162), channel_id=1, source_target_pairs={{0,8},{8,0},{1,9},{9,1},{2,10},{10,2},{3,11},{11,3},{4,12},{12,4},... | collective-permute-start | bytes 4718600 | tf_op jit(solution)/shard_map/ppermute | solution.py:316
  1257.0 158.4 %collective-permute-start.54 = (f32[2,128,2560]{2,1,0:T(8,128)}, f32[2,128,2560]{2,1,0:T(8,128)}, u32[]{:S(2)}, u32[]{:S(2)}) collective-permute-start(f32[2,128,2560]{2,1,0:T(8,128)} %get-tuple-element.161), channel_id=1, source_target_pairs={{0,2},{1,3},{2,0},{3,1},{4,6},{5,7},{6,4},{7,5},{8,10},{9,11},{10,... | collective-permute-start | bytes 7864328 | tf_op jit(solution)/shard_map/ppermute | solution.py:317
  1262.4 146.5 %collective-permute-start.56 = (f32[2,128,1536]{2,1,0:T(8,128)}, f32[2,128,1536]{2,1,0:T(8,128)}, u32[]{:S(2)}, u32[]{:S(2)}) collective-permute-start(f32[2,128,1536]{2,1,0:T(8,128)} %get-tuple-element.163), channel_id=1, source_target_pairs={{0,4},{1,5},{2,6},{3,7},{4,0},{5,1},{6,2},{7,3},{8,12},{9,13},{10,... | collective-permute-start | bytes 4718600 | tf_op jit(solution)/shard_map/ppermute | solution.py:317
  1279.5 172.4 %collective-permute-start.63 = (f32[2,352,1024]{2,1,0:T(8,128)}, f32[2,352,1024]{2,1,0:T(8,128)}, u32[]{:S(2)}, u32[]{:S(2)}) collective-permute-start(f32[2,352,1024]{2,1,0:T(8,128)} %get-tuple-element.174), channel_id=1, source_target_pairs={{0,2},{1,3},{2,0},{3,1},{4,6},{5,7},{6,4},{7,5},{8,10},{9,11},{10,... | collective-permute-start | bytes 8650760 | tf_op jit(solution)/shard_map/ppermute | solution.py:317
  1282.9 118.1 %collective-permute-start.49 = (f32[128,512]{1,0:T(8,128)}, f32[128,512]{1,0:T(8,128)S(1)}, u32[]{:S(2)}, u32[]{:S(2)}) collective-permute-start(f32[128,512]{1,0:T(8,128)} %fusion.71), channel_id=1, source_target_pairs={{0,2},{1,3},{2,0},{3,1},{4,6},{5,7},{6,4},{7,5},{8,10},{9,11},{10,... | collective-permute-start | bytes 786440 | tf_op jit(solution)/shard_map/ppermute | solution.py:317
  1420.2 75.4 %collective-permute-start.58 = (f32[128,1536]{1,0:T(8,128)S(1)}, f32[128,1536]{1,0:T(8,128)S(1)}, u32[]{:S(2)}, u32[]{:S(2)}) collective-permute-start(f32[128,1536]{1,0:T(8,128)S(1)} %fusion.41), channel_id=1, source_target_pairs={{0,2},{1,3},{2,0},{3,1},{4,6},{5,7},{6,4},{7,5},{8,10},{9,11},{10,... | collective-permute-start | bytes 2359304 | tf_op jit(solution)/shard_map/ppermute | solution.py:317
  1456.7 64.5 %collective-permute-start.66 = (f32[352,1024]{1,0:T(8,128)}, f32[352,1024]{1,0:T(8,128)}, u32[]{:S(2)}, u32[]{:S(2)}) collective-permute-start(f32[352,1024]{1,0:T(8,128)} %fusion.14), channel_id=1, source_target_pairs={{0,4},{1,5},{2,6},{3,7},{4,0},{5,1},{6,2},{7,3},{8,12},{9,13},{10,... | collective-permute-start | bytes 4325384 | tf_op jit(solution)/shard_map/ppermute | solution.py:317
  (86 other events, 3080.0 us)

commit v3 on v2

--- a/solution.py
+++ b/solution.py
@@ -445,19 +445,18 @@
 def pair_kernel(plan, rows, turned, *refs):
     n, steps = pl.program_id(Z), sum(count for _, count in plan)
     count = len(plan)
-    source, left, load_sem = refs[Z], refs[-2], refs[-1]
-    parts, refs = (None, refs[1:-2]) if turned else (refs[-3], refs[1:-3])
+    if turned:
+        left, refs = refs[Z], refs[1:]
+    else:
+        source, refs, (parts, left, load_sem) = refs[Z], refs[1:-3], refs[-3:]
     me = lax.axis_index('cp')
     bits = (lax.axis_index('dp'), me // 4, (me // 2) % 2, me % 2)
 
     def load(place, core):
-        if turned:
-            from_ref, to_ref = source.at[place, core], left.at[place, core]
-        else:
-            flips = (place // 4, place // 2 % 2, place % 2, core)
-            block = sum((1 - bit if flip else bit) * weight for bit, flip, weight in zip(bits, flips, (8, 4, 2, 1)))
-            from_ref, to_ref = source.at[:, pl.ds(pl.multiple_of(block * LANES, LANES), LANES)], parts.at[place, core]
-        return pltpu.make_async_copy(from_ref, to_ref, load_sem.at[place, core])
+        flips = (place // 4, place // 2 % 2, place % 2, core)
+        block = sum((1 - bit if flip else bit) * weight for bit, flip, weight in zip(bits, flips, (8, 4, 2, 1)))
+        columns = pl.ds(pl.multiple_of(block * LANES, LANES), LANES)
+        return pltpu.make_async_copy(source.at[:, columns], parts.at[place, core], load_sem.at[place, core])
 
     right, outs = refs[Z], refs[1:1 + 2 * count]
     mine, sent, came, send_sem, recv_sem, free_sem = refs[1 + 2 * count:]
@@ -471,7 +470,7 @@
 
     @pl.when(n == Z)
     def _():
-        for core in (1, Z):
+        for core in () if turned else (1, Z):
             for place in range(8):
                 load(place, core).start()
         barrier = pltpu.get_barrier_semaphore()
@@ -491,19 +490,18 @@
         for core, dest in ((1, sent), (Z, mine)):
             for place in range(Z, 8, some):
                 group = range(place, place + some)
-                if first:
-                    for k in group:
-                        load(k, core).wait()
-                        if not turned:
-                            left[k, core] = parts[k, core].T
+                for k in group if first else ():
+                    load(k, core).wait()
+                    left[k, core] = parts[k, core].T
                 tile = jnp.concatenate([left[k, core] for k in group], axis=Z)
                 dest[now, place:place + some] = nn(tile, right[...]).reshape(some, rows, -1)
 
-    @pl.when(n == Z)
-    def _():
-        products(True)
-
-    @pl.when((n >= 1) & (n < steps))
+    if not turned:
+        @pl.when(n == Z)
+        def _():
+            products(True)
+
+    @pl.when((n >= (Z if turned else 1)) & (n < steps))
     def _():
         products(False)
 
@@ -536,13 +534,14 @@
         edge += count
     both = pltpu.VMEM((2, 8, rows, tile), F32)
     two = pltpu.SemaphoreType.DMA((2,))
-    staging = [] if turned else [pltpu.VMEM((8, 2, MODEL, LANES), BF)]
+    staging = [] if turned else [pltpu.VMEM((8, 2, MODEL, LANES), BF), pltpu.VMEM((8, 2, rows, MODEL), BF), pltpu.SemaphoreType.DMA((8, 2))]
+    whole = pl.BlockSpec((8, 2, rows, MODEL), lambda n: (Z, Z, Z, Z), pipeline_mode=pl.Buffered(1))
     return pl.pallas_call(
         functools.partial(pair_kernel, plan, rows, turned), grid=(steps + 1,), name='pair',
-        in_specs=[pl.BlockSpec(memory_space=pl.ANY), pl.BlockSpec((MODEL, tile), lambda n: (Z, jnp.minimum(n, steps - 1)))],
+        in_specs=[whole if turned else pl.BlockSpec(memory_space=pl.ANY),
+                  pl.BlockSpec((MODEL, tile), lambda n: (Z, jnp.minimum(n, steps - 1)))],
         out_specs=out_specs, out_shape=out_shape,
-        scratch_shapes=[both, both, both, two, two, pltpu.SemaphoreType.REGULAR, *staging, pltpu.VMEM((8, 2, rows, MODEL), BF),
-                        pltpu.SemaphoreType.DMA((8, 2))],
+        scratch_shapes=[both, both, both, two, two, pltpu.SemaphoreType.REGULAR, *staging],
         cost_estimate=timed(16 * rows * steps * tile * 4096 / 9e8),
         compiler_params=pltpu.CompilerParams(vmem_limit_bytes=63 * 2**20, collective_id=call_id, has_side_effects=True),
     )(left, right)
@@ -598,7 +597,7 @@
 
 def small_grad(bits, left, right):
     def column(core):
-        return lambda k, m: (Z, ((k % 2) ^ m[Z]) * 8 + ((k // 2 % 2) ^ m[1]) * 4 + ((k // 4) ^ m[2]) * 2 + (core ^ m[3]))
+        return lambda k, m: (Z, ((k % 2) ^ m[Z]) * 8 + ((k // 4) ^ m[1]) * 4 + ((k // 2 % 2) ^ m[2]) * 2 + (core ^ m[3]))
 
     out = pl.BlockSpec((1, LANES, WIDE), lambda k, m: (k, Z, Z))
     grid_spec = pltpu.PrefetchScalarGridSpec(
@@ -607,7 +606,7 @@
         out_specs=[out, out])
     keep, send = pl.pallas_call(small_kernel, grid_spec=grid_spec, name='small', out_shape=[jax.ShapeDtypeStruct((8, LANES, WIDE), F32)] * 2,
                                 cost_estimate=timed(8), compiler_params=ALL_VMEM)(bits, left, left, right)
-    for link in 'cxy':
+    for link in 'cyx':
         got, half = swap(send, link), keep.shape[Z] // 2
         send, keep = lax.optimization_barrier((keep[half:] + got[half:], keep[:half] + got[:half]))
     return (keep[Z] + swap(send, 'z')[Z]) / 16
@@ -646,8 +645,9 @@
 
 
 CHUNKS = ((Z, 8), (8, 4), (12, 4))
-PLAN_UP = (('z', 5), ('y', 3), ('x', 3))
+PLAN_UP = (('z', 5), ('y', 4), ('x', 2))
 PLAN_D = (('z', 4), ('y', 2), ('x', 2))
+PLAN_Q = (('z', 3), ('y', 3), ('x', 2))
 
 
 def solution(mesh):
@@ -685,7 +685,7 @@
             if part == Z:
                 grad_w_o = weight_grad(grad_h, o2, PLAN_D, CHUNK, 2, True)
         grad_q2 = grad_q.reshape(tokens, -1)
-        grad_w_q = weight_grad(x2, grad_q2, PLAN_D, CHUNK, 3, True)
+        grad_w_q = weight_grad(x2, grad_q2, PLAN_Q, CHUNK, 3, True)
         grad_kv2 = join(grad_kv).reshape(tokens, -1)
         grad_w_kv = small_grad(bits, x2, grad_kv2).reshape(-1, 4, 2, HALF)
         grad_x = None

time: 1580 us -> 1460 us (0.924)
  waiting for transfers between devices: 585 us -> 484 us
  Pallas kernels: 823 us -> 807 us
    ppermute x13, waiting for transfers between devices: 197 us -> 105 us  [swap(): return lax.ppermute(values, 'dp', [(Z, 1), (1, Z)])]
    pallas_call x4, Pallas kernels: 217 us -> 202 us  [pair_call(): pl.pallas_call(functools.partial(pair_kernel, plan, rows, turned), grid=(...]
  transfers between devices with their start and end apart: 69 -> 69, of which waited for: 21 -> 26; matrix products, arithmetic and copies ran while one was open for 5% -> 5% of each run, Pallas kernels for 34% -> 36%
where the time goes in v3:
time: 1460 us; the launch traced here: 1450 us
  Pallas kernels  807 us (55%)
  waiting for transfers between devices  484 us (33%)
  other arithmetic  83.7 us (6%)
  starting transfers between devices  74.2 us (5%)
    ppermute x56, waiting for transfers between devices, swap(): return lax.ppermute(values, 'cp', [(i, i ^ BITS[link]) for i in range(8)])  379 us
    pallas_call x4, Pallas kernels, pair_call(): pl.pallas_call(functools.partial(pair_kernel, plan, rows, turned), grid=(...  202 us
    pallas_call x5, Pallas kernels, mm(): pl.pallas_call(functools.partial(mm_kernel, nt if flip else nn, added is...  194 us
    pallas_call x3, Pallas kernels, attn_bwd(): pl.pallas_call(functools.partial(bwd_kernel, scale, scale2, aliased), gri...  159 us
    ppermute x13, waiting for transfers between devices, swap(): return lax.ppermute(values, 'dp', [(Z, 1), (1, Z)])  105 us
    pallas_call x2, Pallas kernels, attn_fwd(): pl.pallas_call(functools.partial(fwd_kernel, scale2, aliased), grid_spec=...  90.5 us
    pallas_call x1, Pallas kernels, ff_block(): pl.pallas_call(ff_kernel, grid_spec=grid_spec, name='ff_block', out_shape...  85.5 us
    ppermute x56, starting transfers between devices, swap(): return lax.ppermute(values, 'cp', [(i, i ^ BITS[link]) for i in range(8)])  56.3 us
  transfers between devices with their start and end apart: 69, of which 26 were waited for; matrix products, arithmetic and copies ran while one was open for 5% of the time, Pallas kernels for 36%

profile of v3, /device:TPU:0, one launch (start us, length us, event | category | flops | bytes accessed | tf_op | source)
XLA Modules:
  0.0 1452.5 jit_solution(13755666342621706475)
XLA Ops:
  15.1 22.2 %collective-permute-done.8.refs_2_ = bf16[8,128,512]{2,1,0:T(8,128)(2,1)} collective-permute-done((bf16[8,128,512]{2,1,0:T(8,128)(2,1)}, bf16[8,128,512]{2,1,0:T(8,128)(2,1)}, u32[]{:S(2)}, u32[]{:S(2)}) %collective-permute-start.8) | collective-permute-done | bytes 1048608 | tf_op jit(solution)/shard_map/ppermute | solution.py:317
  39.4 60.9 %mm.7.ga_ref = bf16[2048,5632]{1,0:T(8,128)(2,1)} custom-call(bf16[2048,2048]{1,0:T(8,128)(2,1)} %bitcast.399, bf16[5632,2048]{1,0:T(8,128)(2,1)} %w_ref.3), custom_call_target="tpu_custom_call" | custom-call | flops 47244640256 | bytes 1048576 | tf_op jit(solution)/shard_map/mm/pallas_call | solution.py:340
  102.8 23.7 %mm.5 = bf16[2048,2048]{1,0:T(8,128)(2,1)} custom-call(bf16[2048,2048]{1,0:T(8,128)(2,1)} %bitcast.403, bf16[2048,2048]{1,0:T(8,128)(2,1)} %bitcast.408), custom_call_target="tpu_custom_call" | custom-call | flops 17179869184 | bytes 1048576 | tf_op jit(solution)/shard_map/mm/pallas_call | solution.py:340
  127.6 45.2 %attn_fwd.2 = (bf16[16,128,2048]{2,1,0:T(8,128)(2,1)}, f32[32,2,512]{2,1,0:T(2,128)}) custom-call(s32[1]{0:T(128)} %bitcast.4.me_ref, bf16[16,128,2048]{2,1,0:T(8,128)(2,1)} %bitcast.429, bf16[8,128,512]{2,1,0:T(8,128)(2,1)} %bitcast.426, bf16[8,128,512]{2,1,0:T(8,128)(2,1)} %collective-permute-done.7.refs_1_, ...), custom_call_target="tpu_custom_call" | custom-call | flops 43200000000 | bytes 1048576 | tf_op jit(solution)/shard_map/attn_fwd/pallas_call | solution.py:274
  172.8 45.3 %attn_fwd.3 = (bf16[16,128,2048]{2,1,0:T(8,128)(2,1)}, f32[32,2,512]{2,1,0:T(2,128)}) custom-call(s32[1]{0:T(128)} %bitcast.4.me_ref, bf16[16,128,2048]{2,1,0:T(8,128)(2,1)} %bitcast.430, bf16[8,128,512]{2,1,0:T(8,128)(2,1)} %bitcast.420, bf16[8,128,512]{2,1,0:T(8,128)(2,1)} %collective-permute-done.refs_1_, ...), custom_call_target="tpu_custom_call", output_to_operand_aliasing={{0}: (10, {})} | custom-call | flops 43200000000 | bytes 1048576 | tf_op jit(solution)/shard_map/attn_fwd/pallas_call | solution.py:274
  218.2 24.7 %mm.6.h_ref.refs_0_ = bf16[2048,2048]{1,0:T(8,128)(2,1)} custom-call(bf16[2048,2048]{1,0:T(8,128)(2,1)} %bitcast.438, bf16[2048,2048]{1,0:T(8,128)(2,1)} %bitcast.397, bf16[2048,2048]{1,0:T(8,128)(2,1)} %bitcast.404), custom_call_target="tpu_custom_call" | custom-call | flops 17179869184 | bytes 1048576 | tf_op jit(solution)/shard_map/mm/pallas_call | solution.py:340
  242.8 85.5 %ff_block.1 = (bf16[2,2,2,2,352,2048]{5,4,3,2,1,0:T(8,128)(2,1)}, bf16[2048,5632]{1,0:T(8,128)(2,1)}) custom-call(s32[4]{0:T(128)} %pad_add_fusion.bits_ref, bf16[2048,2048]{1,0:T(8,128)(2,1)} %mm.6.h_ref.refs_0_, bf16[2048,5632]{1,0:T(8,128)(2,1)} %w_ref.5, bf16[2048,5632]{1,0:T(8,128)(2,1)} %mm.7.ga_ref), custom_call_target="tpu_custom_call" | custom-call | flops 54000001024 | bytes 1048576 | tf_op jit(solution)/shard_map/ff_block/pallas_call | solution.py:431
  328.3 61.0 %mm.8.x_ref.h_ref.refs_0_ = bf16[2048,2048]{1,0:T(8,128)(2,1)} custom-call(bf16[2048,5632]{1,0:T(8,128)(2,1)} %get-tuple-element.96.x_ref.refs_1_, bf16[2048,5632]{1,0:T(8,128)(2,1)} %w_ref.5, bf16[2048,2048]{1,0:T(8,128)(2,1)} %bitcast.400), custom_call_target="tpu_custom_call" | custom-call | flops 47244640256 | bytes 1048576 | tf_op jit(solution)/shard_map/mm/pallas_call | solution.py:340
  389.4 33.2 %pair.5 = (f32[4,128,1024]{2,1,0:T(8,128)}, f32[4,128,1024]{2,1,0:T(8,128)}, f32[4,128,512]{2,1,0:T(8,128)}, f32[4,128,512]{2,1,0:T(8,128)}, f32[4,128,512]{2,1,0:T(8,128)}, /*index=5*/f32[4,128,512]{2,1,0:T(8,128)}) custom-call(bf16[2048,2048]{1,0:T(8,128)(2,1)} %mm.8.x_ref.h_ref.refs_0_, bf16[2048,2048]{1,0:T(8,128)(2,1)} %bitcast.439), custom_call_target="tpu_custom_call" | custom-call | flops 17179869184 | bytes 1048576 | tf_op jit(solution)/shard_map/pair/pallas_call | solution.py:539
  422.6 23.7 %mm.9 = bf16[2048,2048]{1,0:T(8,128)(2,1)} custom-call(bf16[2048,2048]{1,0:T(8,128)(2,1)} %mm.8.x_ref.h_ref.refs_0_, bf16[2048,2048]{1,0:T(8,128)(2,1)} %bitcast.398), custom_call_target="tpu_custom_call" | custom-call | flops 17179869184 | bytes 1048576 | tf_op jit(solution)/shard_map/mm/pallas_call | solution.py:340
  447.4 78.2 %attn_bwd.3 = (bf16[16,128,2048]{2,1,0:T(8,128)(2,1)}, f32[2,2,2,8,128,256]{5,4,3,2,1,0:T(8,128)}, f32[2,2,2,8,128,256]{5,4,3,2,1,0:T(8,128)}) custom-call(s32[1]{0:T(128)} %bitcast.4.me_ref, bf16[16,128,2048]{2,1,0:T(8,128)(2,1)} %bitcast.431, bf16[16,128,2048]{2,1,0:T(8,128)(2,1)} %bitcast.434, f32[32,2,512]{2,1,0:T(2,128)} %get-tuple-element.98.lse_ref, ...), custom_call_target="tpu_custom_call" | custom-call | flops 71999995904 | bytes 1048576 | tf_op jit(solution)/shard_map/attn_bwd/pallas_call | solution.py:299
  525.7 40.0 %attn_bwd.4 = (bf16[16,128,2048]{2,1,0:T(8,128)(2,1)}, f32[2,2,2,4,128,256]{5,4,3,2,1,0:T(8,128)}, f32[2,2,2,4,128,256]{5,4,3,2,1,0:T(8,128)}) custom-call(s32[1]{0:T(128)} %bitcast.4.me_ref, bf16[16,128,2048]{2,1,0:T(8,128)(2,1)} %bitcast.432, bf16[16,128,2048]{2,1,0:T(8,128)(2,1)} %bitcast.435, ...), custom_call_target="tpu_custom_call", output_to_operand_aliasing={{0}: (12, {})} | custom-call | flops 35999997952 | bytes 1048576 | tf_op jit(solution)/shard_map/attn_bwd/pallas_call | solution.py:299
  565.7 40.3 %attn_bwd.5 = (bf16[16,128,2048]{2,1,0:T(8,128)(2,1)}, f32[2,2,2,4,128,256]{5,4,3,2,1,0:T(8,128)}, f32[2,2,2,4,128,256]{5,4,3,2,1,0:T(8,128)}) custom-call(s32[1]{0:T(128)} %bitcast.4.me_ref, bf16[16,128,2048]{2,1,0:T(8,128)(2,1)} %bitcast.433, bf16[16,128,2048]{2,1,0:T(8,128)(2,1)} %bitcast.436, ...), custom_call_target="tpu_custom_call", output_to_operand_aliasing={{0}: (12, {})} | custom-call | flops 35999997952 | bytes 1048576 | tf_op jit(solution)/shard_map/attn_bwd/pallas_call | solution.py:299
  606.1 33.2 %pair.4 = (f32[4,128,768]{2,1,0:T(8,128)}, f32[4,128,768]{2,1,0:T(8,128)}, f32[4,128,768]{2,1,0:T(8,128)}, f32[4,128,768]{2,1,0:T(8,128)}, f32[4,128,512]{2,1,0:T(8,128)}, /*index=5*/f32[4,128,512]{2,1,0:T(8,128)}) custom-call(bf16[2048,2048]{1,0:T(8,128)(2,1)} %bitcast.405, bf16[2048,2048]{1,0:T(8,128)(2,1)} %bitcast.440), custom_call_target="tpu_custom_call" | custom-call | flops 17179869184 | bytes 1048576 | tf_op jit(solution)/shard_map/pair/pallas_call | solution.py:539
  648.7 16.0 %collective-permute-done.31 = f32[4,128,512]{2,1,0:T(8,128)S(1)} collective-permute-done((f32[4,128,512]{2,1,0:T(8,128)}, f32[4,128,512]{2,1,0:T(8,128)S(1)}, u32[]{:S(2)}, u32[]{:S(2)}) %collective-permute-start.31) | collective-permute-done | bytes 1048608 | tf_op jit(solution)/shard_map/ppermute | solution.py:317
  667.5 65.9 %pair.6 = (f32[4,128,2560]{2,1,0:T(8,128)}, f32[4,128,2560]{2,1,0:T(8,128)}, f32[4,128,2048]{2,1,0:T(8,128)}, f32[4,128,2048]{2,1,0:T(8,128)}, f32[4,128,1024]{2,1,0:T(8,128)}, /*index=5*/f32[4,128,1024]{2,1,0:T(8,128)}) custom-call(bf16[2048,2048]{1,0:T(8,128)(2,1)} %mm.6.h_ref.refs_0_, bf16[2048,5632]{1,0:T(8,128)(2,1)} %get-tuple-element.96.x_ref.refs_1_), custom_call_target="tpu_custom_call" | custom-call | flops 47244640256 | bytes 1048576 | tf_op jit(solution)/shard_map/pair/pallas_call | solution.py:539
  737.4 69.3 %pair.7 = (f32[4,352,1024]{2,1,0:T(8,128)}, f32[4,352,1024]{2,1,0:T(8,128)}, f32[4,352,512]{2,1,0:T(8,128)}, f32[4,352,512]{2,1,0:T(8,128)}, f32[4,352,512]{2,1,0:T(8,128)}, /*index=5*/f32[4,352,512]{2,1,0:T(8,128)}) custom-call(bf16[8,2,352,2048]{3,2,1,0:T(8,128)(2,1)} %bitcast.428, bf16[2048,2048]{1,0:T(8,128)(2,1)} %bitcast.401), custom_call_target="tpu_custom_call" | custom-call | flops 47244640256 | bytes 1048576 | tf_op jit(solution)/shard_map/pair/pallas_call | solution.py:539
  831.4 15.2 %collective-permute-done.32.refs_3_ = f32[2,128,768]{2,1,0:T(8,128)S(1)} collective-permute-done((f32[2,128,768]{2,1,0:T(8,128)S(1)}, f32[2,128,768]{2,1,0:T(8,128)S(1)}, u32[]{:S(2)}, u32[]{:S(2)}) %collective-permute-start.32) | collective-permute-done | bytes 786464 | tf_op jit(solution)/shard_map/ppermute | solution.py:317
  850.9 30.0 %collective-permute-done.61 = f32[4,352,512]{2,1,0:T(8,128)S(1)} collective-permute-done((f32[4,352,512]{2,1,0:T(8,128)}, f32[4,352,512]{2,1,0:T(8,128)S(1)}, u32[]{:S(2)}, u32[]{:S(2)}) %collective-permute-start.61) | collective-permute-done | bytes 2883616 | tf_op jit(solution)/shard_map/ppermute | solution.py:317
  880.9 29.9 %collective-permute-done.62 = f32[4,352,512]{2,1,0:T(8,128)S(1)} collective-permute-done((f32[4,352,512]{2,1,0:T(8,128)}, f32[4,352,512]{2,1,0:T(8,128)S(1)}, u32[]{:S(2)}, u32[]{:S(2)}) %collective-permute-start.62) | collective-permute-done | bytes 2883616 | tf_op jit(solution)/shard_map/ppermute | solution.py:317
  921.7 47.6 %collective-permute-done.52 = f32[4,128,2048]{2,1,0:T(8,128)S(1)} collective-permute-done((f32[4,128,2048]{2,1,0:T(8,128)}, f32[4,128,2048]{2,1,0:T(8,128)S(1)}, u32[]{:S(2)}, u32[]{:S(2)}) %collective-permute-start.52) | collective-permute-done | bytes 4194336 | tf_op jit(solution)/shard_map/ppermute | solution.py:317
  982.6 13.1 collective-permute-done.27
  1001.2 17.0 %collective-permute-done.22 = f32[2,4,128,256]{3,2,1,0:T(8,128)} collective-permute-done((f32[2,4,128,256]{3,2,1,0:T(8,128)}, f32[2,4,128,256]{3,2,1,0:T(8,128)}, u32[]{:S(2)}, u32[]{:S(2)}) %collective-permute-start.22) | collective-permute-done | bytes 1048608 | tf_op jit(solution)/shard_map/ppermute | solution.py:317
  1029.9 36.2 %collective-permute-done.20 = f32[2,4,128,256]{3,2,1,0:T(8,128)S(1)} collective-permute-done((f32[2,4,128,256]{3,2,1,0:T(8,128)}, f32[2,4,128,256]{3,2,1,0:T(8,128)S(1)}, u32[]{:S(2)}, u32[]{:S(2)}) %collective-permute-start.20) | collective-permute-done | bytes 1048608 | tf_op jit(solution)/shard_map/ppermute | solution.py:317
  1082.6 71.6 %collective-permute-done.50.refs_8_ = f32[128,512]{1,0:T(8,128)} collective-permute-done((f32[128,512]{1,0:T(8,128)}, f32[128,512]{1,0:T(8,128)}, u32[]{:S(2)}, u32[]{:S(2)}) %collective-permute-start.50) | collective-permute-done | bytes 262176 | tf_op jit(solution)/shard_map/ppermute | solution.py:316
  1210.4 11.7 small.1
  1223.6 20.9 %collective-permute-done.64.refs_4_ = f32[2,352,512]{2,1,0:T(8,128)} collective-permute-done((f32[2,352,512]{2,1,0:T(8,128)}, f32[2,352,512]{2,1,0:T(8,128)}, u32[]{:S(2)}, u32[]{:S(2)}) %collective-permute-start.64) | collective-permute-done | bytes 1441824 | tf_op jit(solution)/shard_map/ppermute | solution.py:316
  1268.0 52.7 %collective-permute-done.63.refs_3_ = f32[2,352,1024]{2,1,0:T(8,128)} collective-permute-done((f32[2,352,1024]{2,1,0:T(8,128)}, f32[2,352,1024]{2,1,0:T(8,128)}, u32[]{:S(2)}, u32[]{:S(2)}) %collective-permute-start.63) | collective-permute-done | bytes 2883616 | tf_op jit(solution)/shard_map/ppermute | solution.py:317
  1335.5 28.3 %collective-permute-done.48.refs_6_ = f32[128,1024]{1,0:T(8,128)S(1)} collective-permute-done((f32[128,1024]{1,0:T(8,128)S(1)}, f32[128,1024]{1,0:T(8,128)S(1)}, u32[]{:S(2)}, u32[]{:S(2)}) %collective-permute-start.48) | collective-permute-done | bytes 524320 | tf_op jit(solution)/shard_map/ppermute | solution.py:317
  1379.9 14.9 %collective-permute-done.66.refs_6_ = f32[352,1024]{1,0:T(8,128)} collective-permute-done((f32[352,1024]{1,0:T(8,128)}, f32[352,1024]{1,0:T(8,128)}, u32[]{:S(2)}, u32[]{:S(2)}) %collective-permute-start.66) | collective-permute-done | bytes 1441824 | tf_op jit(solution)/shard_map/ppermute | solution.py:317
  1414.4 16.7 %gx.2.refs_0_ = bf16[2048,2048]{1,0:T(8,128)(2,1)} custom-call(bf16[2048,2048]{1,0:T(8,128)(2,1)} %mm.8.x_ref.h_ref.refs_0_, bf16[2048,2048]{1,0:T(8,128)(2,1)} %bitcast.441, bf16[2048,512]{1,0:T(8,128)(2,1)} %bitcast.444, bf16[2048,2048]{1,0:T(8,128)(2,1)} %bitcast.409, bf16[256,2048]{1,0:T(8,128)(2,1)} %bitcast.412, bf16[256,2048]{1,0:T(8,128)(2,1)} %bitcast.415), custom_call_target="tpu_custom_call" | custom-call | flops 12600000512 | bytes 1048576 | tf_op jit(solution)/shard_map/gx/pallas_call | solution.py:389
  1434.4 16.9 %gx.3 = bf16[2048,2048]{1,0:T(8,128)(2,1)} custom-call(bf16[2048,2048]{1,0:T(8,128)(2,1)} %mm.8.x_ref.h_ref.refs_0_, bf16[2048,2048]{1,0:T(8,128)(2,1)} %bitcast.442, bf16[2048,512]{1,0:T(8,128)(2,1)} %bitcast.445, bf16[2048,2048]{1,0:T(8,128)(2,1)} %bitcast.410, bf16[256,2048]{1,0:T(8,128)(2,1)} %bitcast.413, ...), custom_call_target="tpu_custom_call", output_to_operand_aliasing={{}: (6, {})} | custom-call | flops 12600000512 | bytes 1048576 | tf_op jit(solution)/shard_map/gx/pallas_call | solution.py:389
  (270 shorter events, 260.1 us)
Async XLA Ops:
  13.0 87.8 %collective-permute-start.10 = (bf16[8,128,512]{2,1,0:T(8,128)(2,1)}, bf16[8,128,512]{2,1,0:T(8,128)(2,1)}, u32[]{:S(2)}, u32[]{:S(2)}) collective-permute-start(bf16[8,128,512]{2,1,0:T(8,128)(2,1)} %bitcast.424), channel_id=1, source_target_pairs={{0,4},{1,5},{2,6},{3,7},{4,0},{5,1},{6,2},{7,3},{8,12},{9,13},{10,... | collective-permute-start | bytes 3145736 | tf_op jit(solution)/shard_map/ppermute | solution.py:317
  14.5 86.3 %collective-permute-start.7 = (bf16[8,128,512]{2,1,0:T(8,128)(2,1)}, bf16[8,128,512]{2,1,0:T(8,128)(2,1)}, u32[]{:S(2)}, u32[]{:S(2)}) collective-permute-start(bf16[8,128,512]{2,1,0:T(8,128)(2,1)} %bitcast.425), channel_id=1, source_target_pairs={{0,1},{1,0},{2,3},{3,2},{4,5},{5,4},{6,7},{7,6},{8,9},{9,8},{10,11... | collective-permute-start | bytes 3145736 | tf_op jit(solution)/shard_map/ppermute | solution.py:317
  14.5 86.8 %collective-permute-start.3 = (bf16[8,128,512]{2,1,0:T(8,128)(2,1)}, bf16[8,128,512]{2,1,0:T(8,128)(2,1)}, u32[]{:S(2)}, u32[]{:S(2)}) collective-permute-start(bf16[8,128,512]{2,1,0:T(8,128)(2,1)} %bitcast.417), channel_id=1, source_target_pairs={{0,4},{1,5},{2,6},{3,7},{4,0},{5,1},{6,2},{7,3},{8,12},{9,13},{10,... | collective-permute-start | bytes 3145736 | tf_op jit(solution)/shard_map/ppermute | solution.py:317
  15.0 111.5 %collective-permute-start.1 = (bf16[8,128,512]{2,1,0:T(8,128)(2,1)}, bf16[8,128,512]{2,1,0:T(8,128)(2,1)}, u32[]{:S(2)}, u32[]{:S(2)}) collective-permute-start(bf16[8,128,512]{2,1,0:T(8,128)(2,1)} %bitcast.418), channel_id=1, source_target_pairs={{0,2},{1,3},{2,0},{3,1},{4,6},{5,7},{6,4},{7,5},{8,10},{9,11},{10,... | collective-permute-start | bytes 3145736 | tf_op jit(solution)/shard_map/ppermute | solution.py:317
  446.3 194.4 %collective-permute-start.43 = (f32[4,128,512]{2,1,0:T(8,128)}, f32[4,128,512]{2,1,0:T(8,128)}, u32[]{:S(2)}, u32[]{:S(2)}) collective-permute-start(f32[4,128,512]{2,1,0:T(8,128)} %get-tuple-element.144), channel_id=1, source_target_pairs={{0,4},{1,5},{2,6},{3,7},{4,0},{5,1},{6,2},{7,3},{8,12},{9,13},{10,... | collective-permute-start | bytes 3145736 | tf_op jit(solution)/shard_map/ppermute | solution.py:317
  446.9 198.0 %collective-permute-start.44 = (f32[4,128,512]{2,1,0:T(8,128)}, f32[4,128,512]{2,1,0:T(8,128)}, u32[]{:S(2)}, u32[]{:S(2)}) collective-permute-start(f32[4,128,512]{2,1,0:T(8,128)} %get-tuple-element.147), channel_id=1, source_target_pairs={{0,2},{1,3},{2,0},{3,1},{4,6},{5,7},{6,4},{7,5},{8,10},{9,11},{10,... | collective-permute-start | bytes 3145736 | tf_op jit(solution)/shard_map/ppermute | solution.py:317
  643.4 92.9 %collective-permute-start.46 = (f32[2,128,512]{2,1,0:T(8,128)}, f32[2,128,512]{2,1,0:T(8,128)}, u32[]{:S(2)}, u32[]{:S(2)}) collective-permute-start(f32[2,128,512]{2,1,0:T(8,128)} %get-tuple-element.150), channel_id=1, source_target_pairs={{0,8},{8,0},{1,9},{9,1},{2,10},{10,2},{3,11},{11,3},{4,12},{12,4},... | collective-permute-start | bytes 1572872 | tf_op jit(solution)/shard_map/ppermute | solution.py:316
  647.2 89.6 %collective-permute-start.47 = (f32[2,128,512]{2,1,0:T(8,128)}, f32[2,128,512]{2,1,0:T(8,128)}, u32[]{:S(2)}, u32[]{:S(2)}) collective-permute-start(f32[2,128,512]{2,1,0:T(8,128)} %get-tuple-element.151), channel_id=1, source_target_pairs={{0,4},{1,5},{2,6},{3,7},{4,0},{5,1},{6,2},{7,3},{8,12},{9,13},{10,... | collective-permute-start | bytes 1572872 | tf_op jit(solution)/shard_map/ppermute | solution.py:317
  665.9 71.4 %collective-permute-start.34 = (f32[2,128,512]{2,1,0:T(8,128)}, f32[2,128,512]{2,1,0:T(8,128)}, u32[]{:S(2)}, u32[]{:S(2)}) collective-permute-start(f32[2,128,512]{2,1,0:T(8,128)} %get-tuple-element.131), channel_id=1, source_target_pairs={{0,4},{1,5},{2,6},{3,7},{4,0},{5,1},{6,2},{7,3},{8,12},{9,13},{10,... | collective-permute-start | bytes 1572872 | tf_op jit(solution)/shard_map/ppermute | solution.py:317
  733.4 93.2 %collective-permute-start.42 = (f32[4,128,1024]{2,1,0:T(8,128)}, f32[4,128,1024]{2,1,0:T(8,128)}, u32[]{:S(2)}, u32[]{:S(2)}) collective-permute-start(f32[4,128,1024]{2,1,0:T(8,128)} %get-tuple-element.141), channel_id=1, source_target_pairs={{0,8},{8,0},{1,9},{9,1},{2,10},{10,2},{3,11},{11,3},{4,12},{12,4},... | collective-permute-start | bytes 6291464 | tf_op jit(solution)/shard_map/ppermute | solution.py:316
  734.9 95.0 %collective-permute-start.53 = (f32[4,128,1024]{2,1,0:T(8,128)}, f32[4,128,1024]{2,1,0:T(8,128)}, u32[]{:S(2)}, u32[]{:S(2)}) collective-permute-start(f32[4,128,1024]{2,1,0:T(8,128)} %get-tuple-element.159), channel_id=1, source_target_pairs={{0,2},{1,3},{2,0},{3,1},{4,6},{5,7},{6,4},{7,5},{8,10},{9,11},{10,... | collective-permute-start | bytes 6291464 | tf_op jit(solution)/shard_map/ppermute | solution.py:317
  736.3 79.1 %collective-permute-start.29 = (f32[4,128,768]{2,1,0:T(8,128)}, f32[4,128,768]{2,1,0:T(8,128)}, u32[]{:S(2)}, u32[]{:S(2)}) collective-permute-start(f32[4,128,768]{2,1,0:T(8,128)} %get-tuple-element.121), channel_id=1, source_target_pairs={{0,8},{8,0},{1,9},{9,1},{2,10},{10,2},{3,11},{11,3},{4,12},{12,4},... | collective-permute-start | bytes 4718600 | tf_op jit(solution)/shard_map/ppermute | solution.py:316
  736.8 80.0 %collective-permute-start.30 = (f32[4,128,768]{2,1,0:T(8,128)}, f32[4,128,768]{2,1,0:T(8,128)}, u32[]{:S(2)}, u32[]{:S(2)}) collective-permute-start(f32[4,128,768]{2,1,0:T(8,128)} %get-tuple-element.124), channel_id=1, source_target_pairs={{0,4},{1,5},{2,6},{3,7},{4,0},{5,1},{6,2},{7,3},{8,12},{9,13},{10,... | collective-permute-start | bytes 4718600 | tf_op jit(solution)/shard_map/ppermute | solution.py:317
  737.4 235.5 %collective-permute-start.14 = (f32[2,2,2,8,128,256]{5,4,3,2,1,0:T(8,128)}, f32[2,2,2,8,128,256]{5,4,3,2,1,0:T(8,128)}, u32[]{:S(2)}, u32[]{:S(2)}) collective-permute-start(f32[2,2,2,8,128,256]{5,4,3,2,1,0:T(8,128)} %get-tuple-element.103), channel_id=1, source_target_pairs={{0,1},{1,0},{2,3},{3,2},{4,5},{5,4},{6,7},{7,6},{8,9},{9,8},{10,11... | collective-permute-start | bytes 25165832 | tf_op jit(solution)/shard_map/ppermute | solution.py:317
  815.4 65.6 %collective-permute-start.61 = (f32[4,352,512]{2,1,0:T(8,128)}, f32[4,352,512]{2,1,0:T(8,128)S(1)}, u32[]{:S(2)}, u32[]{:S(2)}) collective-permute-start(f32[4,352,512]{2,1,0:T(8,128)} %get-tuple-element.169), channel_id=1, source_target_pairs={{0,4},{1,5},{2,6},{3,7},{4,0},{5,1},{6,2},{7,3},{8,12},{9,13},{10,... | collective-permute-start | bytes 8650760 | tf_op jit(solution)/shard_map/ppermute | solution.py:317
  824.4 88.1 %collective-permute-start.24 = (f32[2,2,2,4,128,256]{5,4,3,2,1,0:T(8,128)}, f32[2,2,2,4,128,256]{5,4,3,2,1,0:T(8,128)S(1)}, u32[]{:S(2)}, u32[]{:S(2)}) collective-permute-start(f32[2,2,2,4,128,256]{5,4,3,2,1,0:T(8,128)} %get-tuple-element.115), channel_id=1, source_target_pairs={{0,1},{1,0},{2,3},{3,2},{4,5},{5,4},{6,7},{7,6},{8,9},{9,8},{10,11... | collective-permute-start | bytes 12582920 | tf_op jit(solution)/shard_map/ppermute | solution.py:317
  849.6 119.7 %collective-permute-start.52 = (f32[4,128,2048]{2,1,0:T(8,128)}, f32[4,128,2048]{2,1,0:T(8,128)S(1)}, u32[]{:S(2)}, u32[]{:S(2)}) collective-permute-start(f32[4,128,2048]{2,1,0:T(8,128)} %get-tuple-element.156), channel_id=1, source_target_pairs={{0,4},{1,5},{2,6},{3,7},{4,0},{5,1},{6,2},{7,3},{8,12},{9,13},{10,... | collective-permute-start | bytes 12582920 | tf_op jit(solution)/shard_map/ppermute | solution.py:317
  880.9 88.9 %collective-permute-start.19 = (f32[2,2,2,4,128,256]{5,4,3,2,1,0:T(8,128)S(1)}, f32[2,2,2,4,128,256]{5,4,3,2,1,0:T(8,128)S(1)}, u32[]{:S(2)}, u32[]{:S(2)}) collective-permute-start(f32[2,2,2,4,128,256]{5,4,3,2,1,0:T(8,128)S(1)} %copy-done.35), channel_id=1, source_target_pairs={{0,1},{1,0},{2,3},{3,2},{4,5},{5,4},{6,7},{7,6},{8,9},{9,8},{10,11... | collective-permute-start | bytes 12582920 | tf_op jit(solution)/shard_map/ppermute | solution.py:317
  910.8 246.8 %collective-permute-start.60 = (f32[4,352,1024]{2,1,0:T(8,128)}, f32[4,352,1024]{2,1,0:T(8,128)S(1)}, u32[]{:S(2)}, u32[]{:S(2)}) collective-permute-start(f32[4,352,1024]{2,1,0:T(8,128)} %get-tuple-element.166), channel_id=1, source_target_pairs={{0,8},{8,0},{1,9},{9,1},{2,10},{10,2},{3,11},{11,3},{4,12},{12,4},... | collective-permute-start | bytes 17301512 | tf_op jit(solution)/shard_map/ppermute | solution.py:316
  912.5 244.4 %collective-permute-start.51 = (f32[4,128,2560]{2,1,0:T(8,128)}, f32[4,128,2560]{2,1,0:T(8,128)}, u32[]{:S(2)}, u32[]{:S(2)}) collective-permute-start(f32[4,128,2560]{2,1,0:T(8,128)} %get-tuple-element.153), channel_id=1, source_target_pairs={{0,8},{8,0},{1,9},{9,1},{2,10},{10,2},{3,11},{11,3},{4,12},{12,4},... | collective-permute-start | bytes 15728648 | tf_op jit(solution)/shard_map/ppermute | solution.py:316
  995.7 75.4 %collective-permute-start.17 = (f32[2,8,128,256]{3,2,1,0:T(8,128)}, f32[2,8,128,256]{3,2,1,0:T(8,128)}, u32[]{:S(2)}, u32[]{:S(2)}) collective-permute-start(f32[2,8,128,256]{3,2,1,0:T(8,128)} %get-tuple-element.183), channel_id=1, source_target_pairs={{0,4},{1,5},{2,6},{3,7},{4,0},{5,1},{6,2},{7,3},{8,12},{9,13},{10,... | collective-permute-start | bytes 6291464 | tf_op jit(solution)/shard_map/ppermute | solution.py:317
  997.9 77.3 %collective-permute-start.15 = (f32[2,8,128,256]{3,2,1,0:T(8,128)}, f32[2,8,128,256]{3,2,1,0:T(8,128)}, u32[]{:S(2)}, u32[]{:S(2)}) collective-permute-start(f32[2,8,128,256]{3,2,1,0:T(8,128)} %get-tuple-element.184), channel_id=1, source_target_pairs={{0,2},{1,3},{2,0},{3,1},{4,6},{5,7},{6,4},{7,5},{8,10},{9,11},{10,... | collective-permute-start | bytes 6291464 | tf_op jit(solution)/shard_map/ppermute | solution.py:317
  1066.1 89.5 %collective-permute-start.45 = (f32[2,128,1024]{2,1,0:T(8,128)}, f32[2,128,1024]{2,1,0:T(8,128)}, u32[]{:S(2)}, u32[]{:S(2)}) collective-permute-start(f32[2,128,1024]{2,1,0:T(8,128)} %get-tuple-element.149), channel_id=1, source_target_pairs={{0,2},{1,3},{2,0},{3,1},{4,6},{5,7},{6,4},{7,5},{8,10},{9,11},{10,... | collective-permute-start | bytes 3145736 | tf_op jit(solution)/shard_map/ppermute | solution.py:317
  1071.1 87.1 %collective-permute-start.26 = (f32[4,128,256]{2,1,0:T(8,128)}, f32[4,128,256]{2,1,0:T(8,128)}, u32[]{:S(2)}, u32[]{:S(2)}) collective-permute-start(f32[4,128,256]{2,1,0:T(8,128)} %get-tuple-element.117), channel_id=1, source_target_pairs={{0,4},{1,5},{2,6},{3,7},{4,0},{5,1},{6,2},{7,3},{8,12},{9,13},{10,... | collective-permute-start | bytes 1572872 | tf_op jit(solution)/shard_map/ppermute | solution.py:317
  1075.3 78.8 %collective-permute-start.50 = (f32[128,512]{1,0:T(8,128)}, f32[128,512]{1,0:T(8,128)}, u32[]{:S(2)}, u32[]{:S(2)}) collective-permute-start(f32[128,512]{1,0:T(8,128)} %fusion.71), channel_id=1, source_target_pairs={{0,8},{8,0},{1,9},{9,1},{2,10},{10,2},{3,11},{11,3},{4,12},{12,4},... | collective-permute-start | bytes 786440 | tf_op jit(solution)/shard_map/ppermute | solution.py:316
  1168.9 83.7 %collective-permute-start.55 = (f32[2,128,2048]{2,1,0:T(8,128)}, f32[2,128,2048]{2,1,0:T(8,128)}, u32[]{:S(2)}, u32[]{:S(2)}) collective-permute-start(f32[2,128,2048]{2,1,0:T(8,128)} %get-tuple-element.162), channel_id=1, source_target_pairs={{0,8},{8,0},{1,9},{9,1},{2,10},{10,2},{3,11},{11,3},{4,12},{12,4},... | collective-permute-start | bytes 6291464 | tf_op jit(solution)/shard_map/ppermute | solution.py:316
  1170.7 94.0 %collective-permute-start.54 = (f32[2,128,2560]{2,1,0:T(8,128)}, f32[2,128,2560]{2,1,0:T(8,128)}, u32[]{:S(2)}, u32[]{:S(2)}) collective-permute-start(f32[2,128,2560]{2,1,0:T(8,128)} %get-tuple-element.161), channel_id=1, source_target_pairs={{0,2},{1,3},{2,0},{3,1},{4,6},{5,7},{6,4},{7,5},{8,10},{9,11},{10,... | collective-permute-start | bytes 7864328 | tf_op jit(solution)/shard_map/ppermute | solution.py:317
  1202.7 118.0 %collective-permute-start.63 = (f32[2,352,1024]{2,1,0:T(8,128)}, f32[2,352,1024]{2,1,0:T(8,128)}, u32[]{:S(2)}, u32[]{:S(2)}) collective-permute-start(f32[2,352,1024]{2,1,0:T(8,128)} %get-tuple-element.174), channel_id=1, source_target_pairs={{0,2},{1,3},{2,0},{3,1},{4,6},{5,7},{6,4},{7,5},{8,10},{9,11},{10,... | collective-permute-start | bytes 8650760 | tf_op jit(solution)/shard_map/ppermute | solution.py:317
  1222.1 109.9 %collective-permute-start.38 = (f32[8,128,512]{2,1,0:T(8,128)}, f32[8,128,512]{2,1,0:T(8,128)S(1)}, u32[]{:S(2)}, u32[]{:S(2)}) collective-permute-start(f32[8,128,512]{2,1,0:T(8,128)} %get-tuple-element.133), channel_id=1, source_target_pairs={{0,1},{1,0},{2,3},{3,2},{4,5},{5,4},{6,7},{7,6},{8,9},{9,8},{10,11... | collective-permute-start | bytes 6291464 | tf_op jit(solution)/shard_map/ppermute | solution.py:317
  1252.6 77.9 %collective-permute-start.65 = (f32[2,352,512]{2,1,0:T(8,128)S(1)}, f32[2,352,512]{2,1,0:T(8,128)S(1)}, u32[]{:S(2)}, u32[]{:S(2)}) collective-permute-start(f32[2,352,512]{2,1,0:T(8,128)S(1)} %copy-done.23), channel_id=1, source_target_pairs={{0,4},{1,5},{2,6},{3,7},{4,0},{5,1},{6,2},{7,3},{8,12},{9,13},{10,... | collective-permute-start | bytes 4325384 | tf_op jit(solution)/shard_map/ppermute | solution.py:317
  1263.1 65.9 %collective-permute-start.36 = (f32[128,768]{1,0:T(8,128)S(1)}, f32[128,768]{1,0:T(8,128)S(1)}, u32[]{:S(2)}, u32[]{:S(2)}) collective-permute-start(f32[128,768]{1,0:T(8,128)S(1)} %copy-done.31), channel_id=1, source_target_pairs={{0,2},{1,3},{2,0},{3,1},{4,6},{5,7},{6,4},{7,5},{8,10},{9,11},{10,... | collective-permute-start | bytes 1179656 | tf_op jit(solution)/shard_map/ppermute | solution.py:317
  1264.6 102.1 %collective-permute-start.58 = (f32[128,2048]{1,0:T(8,128)S(1)}, f32[128,2048]{1,0:T(8,128)}, u32[]{:S(2)}, u32[]{:S(2)}) collective-permute-start(f32[128,2048]{1,0:T(8,128)S(1)} %fusion.16), channel_id=1, source_target_pairs={{0,2},{1,3},{2,0},{3,1},{4,6},{5,7},{6,4},{7,5},{8,10},{9,11},{10,... | collective-permute-start | bytes 3145736 | tf_op jit(solution)/shard_map/ppermute | solution.py:317
  (87 other events, 3154.3 us)

commit v4 on v3

--- a/solution.py
+++ b/solution.py
@@ -645,9 +645,8 @@
 
 
 CHUNKS = ((Z, 8), (8, 4), (12, 4))
-PLAN_UP = (('z', 5), ('y', 4), ('x', 2))
-PLAN_D = (('z', 4), ('y', 2), ('x', 2))
-PLAN_Q = (('z', 3), ('y', 3), ('x', 2))
+PLAN_UP = (('z', 5), ('y', 3), ('x', 3))
+PLAN_D = (('z', 3), ('y', 3), ('x', 2))
 
 
 def solution(mesh):
@@ -685,7 +684,7 @@
             if part == Z:
                 grad_w_o = weight_grad(grad_h, o2, PLAN_D, CHUNK, 2, True)
         grad_q2 = grad_q.reshape(tokens, -1)
-        grad_w_q = weight_grad(x2, grad_q2, PLAN_Q, CHUNK, 3, True)
+        grad_w_q = weight_grad(x2, grad_q2, PLAN_D, CHUNK, 3, True)
         grad_kv2 = join(grad_kv).reshape(tokens, -1)
         grad_w_kv = small_grad(bits, x2, grad_kv2).reshape(-1, 4, 2, HALF)
         grad_x = None

time: 1460 us -> 1450 us (level)
  starting transfers between devices: 74.2 us -> 55.6 us
    ppermute x56, waiting for transfers between devices: 379 us -> 453 us  [swap(): return lax.ppermute(values, 'cp', [(i, i ^ BITS[link]) for i in range(8)])]
    ppermute x13, waiting for transfers between devices: 105 us -> 31.8 us  [swap(): return lax.ppermute(values, 'dp', [(Z, 1), (1, Z)])]
  transfers between devices with their start and end apart: 69 -> 69, of which waited for: 26 -> 24; matrix products, arithmetic and copies ran while one was open for 5% -> 6% of each run, Pallas kernels for 36% -> 36%
where the time goes in v4:
time: 1450 us; the launch traced here: 1440 us
  Pallas kernels  808 us (56%)
  waiting for transfers between devices  485 us (33%)
  other arithmetic  85.2 us (6%)
  starting transfers between devices  55.6 us (4%)
    ppermute x56, waiting for transfers between devices, swap(): return lax.ppermute(values, 'cp', [(i, i ^ BITS[link]) for i in range(8)])  453 us
    pallas_call x4, Pallas kernels, pair_call(): pl.pallas_call(functools.partial(pair_kernel, plan, rows, turned), grid=(...  203 us
    pallas_call x5, Pallas kernels, mm(): pl.pallas_call(functools.partial(mm_kernel, nt if flip else nn, added is...  194 us
    pallas_call x3, Pallas kernels, attn_bwd(): pl.pallas_call(functools.partial(bwd_kernel, scale, scale2, aliased), gri...  159 us
    pallas_call x2, Pallas kernels, attn_fwd(): pl.pallas_call(functools.partial(fwd_kernel, scale2, aliased), grid_spec=...  90.5 us
    pallas_call x1, Pallas kernels, ff_block(): pl.pallas_call(ff_kernel, grid_spec=grid_spec, name='ff_block', out_shape...  85.5 us
    ppermute x56, starting transfers between devices, swap(): return lax.ppermute(values, 'cp', [(i, i ^ BITS[link]) for i in range(8)])  47.4 us
    pallas_call x2, Pallas kernels, gx_call(): pl.pallas_call(gx_kernel, grid=(total // rows,), name='gx', in_specs=[til...  33.7 us
  transfers between devices with their start and end apart: 69, of which 24 were waited for; matrix products, arithmetic and copies ran while one was open for 6% of the time, Pallas kernels for 36%

profile of v4, /device:TPU:0, one launch (start us, length us, event | category | flops | bytes accessed | tf_op | source)
XLA Modules:
  0.0 1440.5 jit_solution(3131516727627555581)
XLA Ops:
  0.6 9.2 kv.1
  15.1 22.2 %collective-permute-done.8.refs_2_ = bf16[8,128,512]{2,1,0:T(8,128)(2,1)} collective-permute-done((bf16[8,128,512]{2,1,0:T(8,128)(2,1)}, bf16[8,128,512]{2,1,0:T(8,128)(2,1)}, u32[]{:S(2)}, u32[]{:S(2)}) %collective-permute-start.8) | collective-permute-done | bytes 1048608 | tf_op jit(solution)/shard_map/ppermute | solution.py:317
  39.4 60.8 %mm.7.ga_ref = bf16[2048,5632]{1,0:T(8,128)(2,1)} custom-call(bf16[2048,2048]{1,0:T(8,128)(2,1)} %bitcast.403, bf16[5632,2048]{1,0:T(8,128)(2,1)} %w_ref.3), custom_call_target="tpu_custom_call" | custom-call | flops 47244640256 | bytes 1048576 | tf_op jit(solution)/shard_map/mm/pallas_call | solution.py:340
  102.8 23.7 %mm.5 = bf16[2048,2048]{1,0:T(8,128)(2,1)} custom-call(bf16[2048,2048]{1,0:T(8,128)(2,1)} %bitcast.407, bf16[2048,2048]{1,0:T(8,128)(2,1)} %bitcast.412), custom_call_target="tpu_custom_call" | custom-call | flops 17179869184 | bytes 1048576 | tf_op jit(solution)/shard_map/mm/pallas_call | solution.py:340
  127.6 45.2 %attn_fwd.2 = (bf16[16,128,2048]{2,1,0:T(8,128)(2,1)}, f32[32,2,512]{2,1,0:T(2,128)}) custom-call(s32[1]{0:T(128)} %bitcast.4.me_ref, bf16[16,128,2048]{2,1,0:T(8,128)(2,1)} %bitcast.433, bf16[8,128,512]{2,1,0:T(8,128)(2,1)} %bitcast.430, bf16[8,128,512]{2,1,0:T(8,128)(2,1)} %collective-permute-done.7.refs_1_, ...), custom_call_target="tpu_custom_call" | custom-call | flops 43200000000 | bytes 1048576 | tf_op jit(solution)/shard_map/attn_fwd/pallas_call | solution.py:274
  172.8 45.3 %attn_fwd.3 = (bf16[16,128,2048]{2,1,0:T(8,128)(2,1)}, f32[32,2,512]{2,1,0:T(2,128)}) custom-call(s32[1]{0:T(128)} %bitcast.4.me_ref, bf16[16,128,2048]{2,1,0:T(8,128)(2,1)} %bitcast.434, bf16[8,128,512]{2,1,0:T(8,128)(2,1)} %bitcast.424, bf16[8,128,512]{2,1,0:T(8,128)(2,1)} %collective-permute-done.refs_1_, ...), custom_call_target="tpu_custom_call", output_to_operand_aliasing={{0}: (10, {})} | custom-call | flops 43200000000 | bytes 1048576 | tf_op jit(solution)/shard_map/attn_fwd/pallas_call | solution.py:274
  218.2 24.7 %mm.6.h_ref.refs_0_ = bf16[2048,2048]{1,0:T(8,128)(2,1)} custom-call(bf16[2048,2048]{1,0:T(8,128)(2,1)} %bitcast.442, bf16[2048,2048]{1,0:T(8,128)(2,1)} %bitcast.401, bf16[2048,2048]{1,0:T(8,128)(2,1)} %bitcast.408), custom_call_target="tpu_custom_call" | custom-call | flops 17179869184 | bytes 1048576 | tf_op jit(solution)/shard_map/mm/pallas_call | solution.py:340
  242.9 85.5 %ff_block.1 = (bf16[2,2,2,2,352,2048]{5,4,3,2,1,0:T(8,128)(2,1)}, bf16[2048,5632]{1,0:T(8,128)(2,1)}) custom-call(s32[4]{0:T(128)} %pad_add_fusion.bits_ref, bf16[2048,2048]{1,0:T(8,128)(2,1)} %mm.6.h_ref.refs_0_, bf16[2048,5632]{1,0:T(8,128)(2,1)} %w_ref.5, bf16[2048,5632]{1,0:T(8,128)(2,1)} %mm.7.ga_ref), custom_call_target="tpu_custom_call" | custom-call | flops 54000001024 | bytes 1048576 | tf_op jit(solution)/shard_map/ff_block/pallas_call | solution.py:431
  328.3 61.1 %mm.8.x_ref.h_ref.refs_0_ = bf16[2048,2048]{1,0:T(8,128)(2,1)} custom-call(bf16[2048,5632]{1,0:T(8,128)(2,1)} %get-tuple-element.96.x_ref.refs_1_, bf16[2048,5632]{1,0:T(8,128)(2,1)} %w_ref.5, bf16[2048,2048]{1,0:T(8,128)(2,1)} %bitcast.404), custom_call_target="tpu_custom_call" | custom-call | flops 47244640256 | bytes 1048576 | tf_op jit(solution)/shard_map/mm/pallas_call | solution.py:340
  389.4 33.1 %pair.5 = (f32[4,128,768]{2,1,0:T(8,128)}, f32[4,128,768]{2,1,0:T(8,128)}, f32[4,128,768]{2,1,0:T(8,128)}, f32[4,128,768]{2,1,0:T(8,128)}, f32[4,128,512]{2,1,0:T(8,128)}, /*index=5*/f32[4,128,512]{2,1,0:T(8,128)}) custom-call(bf16[2048,2048]{1,0:T(8,128)(2,1)} %mm.8.x_ref.h_ref.refs_0_, bf16[2048,2048]{1,0:T(8,128)(2,1)} %bitcast.443), custom_call_target="tpu_custom_call" | custom-call | flops 17179869184 | bytes 1048576 | tf_op jit(solution)/shard_map/pair/pallas_call | solution.py:539
  422.6 23.8 %mm.9 = bf16[2048,2048]{1,0:T(8,128)(2,1)} custom-call(bf16[2048,2048]{1,0:T(8,128)(2,1)} %mm.8.x_ref.h_ref.refs_0_, bf16[2048,2048]{1,0:T(8,128)(2,1)} %bitcast.402), custom_call_target="tpu_custom_call" | custom-call | flops 17179869184 | bytes 1048576 | tf_op jit(solution)/shard_map/mm/pallas_call | solution.py:340
  448.8 78.2 %attn_bwd.3 = (bf16[16,128,2048]{2,1,0:T(8,128)(2,1)}, f32[2,2,2,8,128,256]{5,4,3,2,1,0:T(8,128)}, f32[2,2,2,8,128,256]{5,4,3,2,1,0:T(8,128)}) custom-call(s32[1]{0:T(128)} %bitcast.4.me_ref, bf16[16,128,2048]{2,1,0:T(8,128)(2,1)} %bitcast.435, bf16[16,128,2048]{2,1,0:T(8,128)(2,1)} %bitcast.438, f32[32,2,512]{2,1,0:T(2,128)} %get-tuple-element.98.lse_ref, ...), custom_call_target="tpu_custom_call" | custom-call | flops 71999995904 | bytes 1048576 | tf_op jit(solution)/shard_map/attn_bwd/pallas_call | solution.py:299
  527.0 40.0 %attn_bwd.4 = (bf16[16,128,2048]{2,1,0:T(8,128)(2,1)}, f32[2,2,2,4,128,256]{5,4,3,2,1,0:T(8,128)}, f32[2,2,2,4,128,256]{5,4,3,2,1,0:T(8,128)}) custom-call(s32[1]{0:T(128)} %bitcast.4.me_ref, bf16[16,128,2048]{2,1,0:T(8,128)(2,1)} %bitcast.436, bf16[16,128,2048]{2,1,0:T(8,128)(2,1)} %bitcast.439, ...), custom_call_target="tpu_custom_call", output_to_operand_aliasing={{0}: (12, {})} | custom-call | flops 35999997952 | bytes 1048576 | tf_op jit(solution)/shard_map/attn_bwd/pallas_call | solution.py:299
  567.0 40.3 %attn_bwd.5 = (bf16[16,128,2048]{2,1,0:T(8,128)(2,1)}, f32[2,2,2,4,128,256]{5,4,3,2,1,0:T(8,128)}, f32[2,2,2,4,128,256]{5,4,3,2,1,0:T(8,128)}) custom-call(s32[1]{0:T(128)} %bitcast.4.me_ref, bf16[16,128,2048]{2,1,0:T(8,128)(2,1)} %bitcast.437, bf16[16,128,2048]{2,1,0:T(8,128)(2,1)} %bitcast.440, ...), custom_call_target="tpu_custom_call", output_to_operand_aliasing={{0}: (12, {})} | custom-call | flops 35999997952 | bytes 1048576 | tf_op jit(solution)/shard_map/attn_bwd/pallas_call | solution.py:299
  607.3 33.0 %pair.4 = (f32[4,128,768]{2,1,0:T(8,128)}, f32[4,128,768]{2,1,0:T(8,128)}, f32[4,128,768]{2,1,0:T(8,128)}, f32[4,128,768]{2,1,0:T(8,128)}, f32[4,128,512]{2,1,0:T(8,128)}, /*index=5*/f32[4,128,512]{2,1,0:T(8,128)}) custom-call(bf16[2048,2048]{1,0:T(8,128)(2,1)} %bitcast.409, bf16[2048,2048]{1,0:T(8,128)(2,1)} %bitcast.444), custom_call_target="tpu_custom_call" | custom-call | flops 17179869184 | bytes 1048576 | tf_op jit(solution)/shard_map/pair/pallas_call | solution.py:539
  646.5 19.3 %collective-permute-done.31 = f32[4,128,512]{2,1,0:T(8,128)S(1)} collective-permute-done((f32[4,128,512]{2,1,0:T(8,128)}, f32[4,128,512]{2,1,0:T(8,128)S(1)}, u32[]{:S(2)}, u32[]{:S(2)}) %collective-permute-start.31) | collective-permute-done | bytes 1048608 | tf_op jit(solution)/shard_map/ppermute | solution.py:317
  683.1 40.8 %collective-permute-done.47.refs_5_ = f32[2,128,512]{2,1,0:T(8,128)S(1)} collective-permute-done((f32[2,128,512]{2,1,0:T(8,128)S(1)}, f32[2,128,512]{2,1,0:T(8,128)S(1)}, u32[]{:S(2)}, u32[]{:S(2)}) %collective-permute-start.47) | collective-permute-done | bytes 524320 | tf_op jit(solution)/shard_map/ppermute | solution.py:317
  725.6 68.9 %pair.7 = (f32[4,352,768]{2,1,0:T(8,128)}, f32[4,352,768]{2,1,0:T(8,128)}, f32[4,352,768]{2,1,0:T(8,128)}, f32[4,352,768]{2,1,0:T(8,128)}, f32[4,352,512]{2,1,0:T(8,128)}, /*index=5*/f32[4,352,512]{2,1,0:T(8,128)}) custom-call(bf16[8,2,352,2048]{3,2,1,0:T(8,128)(2,1)} %bitcast.432, bf16[2048,2048]{1,0:T(8,128)(2,1)} %bitcast.405), custom_call_target="tpu_custom_call" | custom-call | flops 47244640256 | bytes 1048576 | tf_op jit(solution)/shard_map/pair/pallas_call | solution.py:539
  807.2 68.0 %pair.6 = (f32[4,128,2560]{2,1,0:T(8,128)}, f32[4,128,2560]{2,1,0:T(8,128)}, f32[4,128,1536]{2,1,0:T(8,128)}, f32[4,128,1536]{2,1,0:T(8,128)}, f32[4,128,1536]{2,1,0:T(8,128)}, /*index=5*/f32[4,128,1536]{2,1,0:T(8,128)}) custom-call(bf16[2048,2048]{1,0:T(8,128)(2,1)} %mm.6.h_ref.refs_0_, bf16[2048,5632]{1,0:T(8,128)(2,1)} %get-tuple-element.96.x_ref.refs_1_), custom_call_target="tpu_custom_call" | custom-call | flops 47244640256 | bytes 1048576 | tf_op jit(solution)/shard_map/pair/pallas_call | solution.py:539
  884.0 62.4 %collective-permute-done.52 = f32[4,128,1536]{2,1,0:T(8,128)S(1)} collective-permute-done((f32[4,128,1536]{2,1,0:T(8,128)}, f32[4,128,1536]{2,1,0:T(8,128)S(1)}, u32[]{:S(2)}, u32[]{:S(2)}) %collective-permute-start.52) | collective-permute-done | bytes 3145760 | tf_op jit(solution)/shard_map/ppermute | solution.py:317
  948.8 28.6 %collective-permute-done.65.refs_5_ = f32[2,352,512]{2,1,0:T(8,128)S(1)} collective-permute-done((f32[2,352,512]{2,1,0:T(8,128)S(1)}, f32[2,352,512]{2,1,0:T(8,128)S(1)}, u32[]{:S(2)}, u32[]{:S(2)}) %collective-permute-start.65) | collective-permute-done | bytes 1441824 | tf_op jit(solution)/shard_map/ppermute | solution.py:317
  983.7 16.1 %collective-permute-done.27 = f32[2,4,128,256]{3,2,1,0:T(8,128)S(1)} collective-permute-done((f32[2,4,128,256]{3,2,1,0:T(8,128)S(1)}, f32[2,4,128,256]{3,2,1,0:T(8,128)S(1)}, u32[]{:S(2)}, u32[]{:S(2)}) %collective-permute-start.27) | collective-permute-done | bytes 1048608 | tf_op jit(solution)/shard_map/ppermute | solution.py:317
  1017.4 119.5 %collective-permute-done.17 = f32[2,8,128,256]{3,2,1,0:T(8,128)S(1)} collective-permute-done((f32[2,8,128,256]{3,2,1,0:T(8,128)}, f32[2,8,128,256]{3,2,1,0:T(8,128)S(1)}, u32[]{:S(2)}, u32[]{:S(2)}) %collective-permute-start.17) | collective-permute-done | bytes 2097184 | tf_op jit(solution)/shard_map/ppermute | solution.py:317
  1183.3 25.0 %collective-permute-done.21.refs_5_ = f32[4,128,256]{2,1,0:T(8,128)} collective-permute-done((f32[4,128,256]{2,1,0:T(8,128)S(1)}, f32[4,128,256]{2,1,0:T(8,128)}, u32[]{:S(2)}, u32[]{:S(2)}) %collective-permute-start.21) | collective-permute-done | bytes 524320 | tf_op jit(solution)/shard_map/ppermute | solution.py:317
  1223.8 11.7 small.1
  1245.3 20.5 %collective-permute-done.37.refs_8_ = f32[128,512]{1,0:T(8,128)S(1)} collective-permute-done((f32[128,512]{1,0:T(8,128)S(1)}, f32[128,512]{1,0:T(8,128)S(1)}, u32[]{:S(2)}, u32[]{:S(2)}) %collective-permute-start.37) | collective-permute-done | bytes 262176 | tf_op jit(solution)/shard_map/ppermute | solution.py:316
  1278.1 49.4 %collective-permute-done.49.refs_7_ = f32[128,768]{1,0:T(8,128)S(1)} collective-permute-done((f32[128,768]{1,0:T(8,128)S(1)}, f32[128,768]{1,0:T(8,128)S(1)}, u32[]{:S(2)}, u32[]{:S(2)}) %collective-permute-start.49) | collective-permute-done | bytes 393248 | tf_op jit(solution)/shard_map/ppermute | solution.py:317
  1344.0 10.9 collective-permute-done.66.refs_6_
  1373.1 9.8 collective-permute-done.57.refs_6_
  1388.4 10.1 collective-permute-done.39
  1402.3 16.8 %gx.2.refs_0_ = bf16[2048,2048]{1,0:T(8,128)(2,1)} custom-call(bf16[2048,2048]{1,0:T(8,128)(2,1)} %mm.8.x_ref.h_ref.refs_0_, bf16[2048,2048]{1,0:T(8,128)(2,1)} %bitcast.445, bf16[2048,512]{1,0:T(8,128)(2,1)} %bitcast.448, bf16[2048,2048]{1,0:T(8,128)(2,1)} %bitcast.413, bf16[256,2048]{1,0:T(8,128)(2,1)} %bitcast.416, bf16[256,2048]{1,0:T(8,128)(2,1)} %bitcast.419), custom_call_target="tpu_custom_call" | custom-call | flops 12600000512 | bytes 1048576 | tf_op jit(solution)/shard_map/gx/pallas_call | solution.py:389
  1422.5 16.9 %gx.3 = bf16[2048,2048]{1,0:T(8,128)(2,1)} custom-call(bf16[2048,2048]{1,0:T(8,128)(2,1)} %mm.8.x_ref.h_ref.refs_0_, bf16[2048,2048]{1,0:T(8,128)(2,1)} %bitcast.446, bf16[2048,512]{1,0:T(8,128)(2,1)} %bitcast.449, bf16[2048,2048]{1,0:T(8,128)(2,1)} %bitcast.414, bf16[256,2048]{1,0:T(8,128)(2,1)} %bitcast.417, ...), custom_call_target="tpu_custom_call", output_to_operand_aliasing={{}: (6, {})} | custom-call | flops 12600000512 | bytes 1048576 | tf_op jit(solution)/shard_map/gx/pallas_call | solution.py:389
  (277 shorter events, 218.4 us)
Async XLA Ops:
  13.0 87.8 %collective-permute-start.10 = (bf16[8,128,512]{2,1,0:T(8,128)(2,1)}, bf16[8,128,512]{2,1,0:T(8,128)(2,1)}, u32[]{:S(2)}, u32[]{:S(2)}) collective-permute-start(bf16[8,128,512]{2,1,0:T(8,128)(2,1)} %bitcast.428), channel_id=1, source_target_pairs={{0,4},{1,5},{2,6},{3,7},{4,0},{5,1},{6,2},{7,3},{8,12},{9,13},{10,... | collective-permute-start | bytes 3145736 | tf_op jit(solution)/shard_map/ppermute | solution.py:317
  14.5 86.3 %collective-permute-start.7 = (bf16[8,128,512]{2,1,0:T(8,128)(2,1)}, bf16[8,128,512]{2,1,0:T(8,128)(2,1)}, u32[]{:S(2)}, u32[]{:S(2)}) collective-permute-start(bf16[8,128,512]{2,1,0:T(8,128)(2,1)} %bitcast.429), channel_id=1, source_target_pairs={{0,1},{1,0},{2,3},{3,2},{4,5},{5,4},{6,7},{7,6},{8,9},{9,8},{10,11... | collective-permute-start | bytes 3145736 | tf_op jit(solution)/shard_map/ppermute | solution.py:317
  14.5 86.8 %collective-permute-start.3 = (bf16[8,128,512]{2,1,0:T(8,128)(2,1)}, bf16[8,128,512]{2,1,0:T(8,128)(2,1)}, u32[]{:S(2)}, u32[]{:S(2)}) collective-permute-start(bf16[8,128,512]{2,1,0:T(8,128)(2,1)} %bitcast.421), channel_id=1, source_target_pairs={{0,4},{1,5},{2,6},{3,7},{4,0},{5,1},{6,2},{7,3},{8,12},{9,13},{10,... | collective-permute-start | bytes 3145736 | tf_op jit(solution)/shard_map/ppermute | solution.py:317
  15.0 111.5 %collective-permute-start.1 = (bf16[8,128,512]{2,1,0:T(8,128)(2,1)}, bf16[8,128,512]{2,1,0:T(8,128)(2,1)}, u32[]{:S(2)}, u32[]{:S(2)}) collective-permute-start(bf16[8,128,512]{2,1,0:T(8,128)(2,1)} %bitcast.422), channel_id=1, source_target_pairs={{0,2},{1,3},{2,0},{3,1},{4,6},{5,7},{6,4},{7,5},{8,10},{9,11},{10,... | collective-permute-start | bytes 3145736 | tf_op jit(solution)/shard_map/ppermute | solution.py:317
  37.3 65.5 %collective-permute-start.12 = (bf16[8,128,512]{2,1,0:T(8,128)(2,1)}, bf16[8,128,512]{2,1,0:T(8,128)(2,1)}, u32[]{:S(2)}, u32[]{:S(2)}) collective-permute-start(bf16[8,128,512]{2,1,0:T(8,128)(2,1)} %collective-permute-done.8.refs_2_), channel_id=1, source_target_pairs={{0,4},{1,5},{2,6},{3,7},{4,0},{5,1},{6,2},{7,3},{8,12},{9,13},{10,... | collective-permute-start | bytes 3145736 | tf_op jit(solution)/shard_map/ppermute | solution.py:317
  446.3 196.3 %collective-permute-start.44 = (f32[4,128,512]{2,1,0:T(8,128)}, f32[4,128,512]{2,1,0:T(8,128)}, u32[]{:S(2)}, u32[]{:S(2)}) collective-permute-start(f32[4,128,512]{2,1,0:T(8,128)} %get-tuple-element.147), channel_id=1, source_target_pairs={{0,2},{1,3},{2,0},{3,1},{4,6},{5,7},{6,4},{7,5},{8,10},{9,11},{10,... | collective-permute-start | bytes 3145736 | tf_op jit(solution)/shard_map/ppermute | solution.py:317
  447.2 220.2 %collective-permute-start.42 = (f32[4,128,768]{2,1,0:T(8,128)}, f32[4,128,768]{2,1,0:T(8,128)}, u32[]{:S(2)}, u32[]{:S(2)}) collective-permute-start(f32[4,128,768]{2,1,0:T(8,128)} %get-tuple-element.141), channel_id=1, source_target_pairs={{0,8},{8,0},{1,9},{9,1},{2,10},{10,2},{3,11},{11,3},{4,12},{12,4},... | collective-permute-start | bytes 4718600 | tf_op jit(solution)/shard_map/ppermute | solution.py:316
  642.6 153.2 %collective-permute-start.30 = (f32[4,128,768]{2,1,0:T(8,128)}, f32[4,128,768]{2,1,0:T(8,128)}, u32[]{:S(2)}, u32[]{:S(2)}) collective-permute-start(f32[4,128,768]{2,1,0:T(8,128)} %get-tuple-element.124), channel_id=1, source_target_pairs={{0,4},{1,5},{2,6},{3,7},{4,0},{5,1},{6,2},{7,3},{8,12},{9,13},{10,... | collective-permute-start | bytes 4718600 | tf_op jit(solution)/shard_map/ppermute | solution.py:317
  665.8 58.1 %collective-permute-start.47 = (f32[2,128,512]{2,1,0:T(8,128)S(1)}, f32[2,128,512]{2,1,0:T(8,128)S(1)}, u32[]{:S(2)}, u32[]{:S(2)}) collective-permute-start(f32[2,128,512]{2,1,0:T(8,128)S(1)} %get-tuple-element.151), channel_id=1, source_target_pairs={{0,4},{1,5},{2,6},{3,7},{4,0},{5,1},{6,2},{7,3},{8,12},{9,13},{10,... | collective-permute-start | bytes 1572872 | tf_op jit(solution)/shard_map/ppermute | solution.py:317
  667.3 128.3 %collective-permute-start.34 = (f32[2,128,512]{2,1,0:T(8,128)}, f32[2,128,512]{2,1,0:T(8,128)}, u32[]{:S(2)}, u32[]{:S(2)}) collective-permute-start(f32[2,128,512]{2,1,0:T(8,128)} %get-tuple-element.131), channel_id=1, source_target_pairs={{0,4},{1,5},{2,6},{3,7},{4,0},{5,1},{6,2},{7,3},{8,12},{9,13},{10,... | collective-permute-start | bytes 1572872 | tf_op jit(solution)/shard_map/ppermute | solution.py:317
  679.0 127.3 %collective-permute-start.45 = (f32[2,128,768]{2,1,0:T(8,128)}, f32[2,128,768]{2,1,0:T(8,128)}, u32[]{:S(2)}, u32[]{:S(2)}) collective-permute-start(f32[2,128,768]{2,1,0:T(8,128)} %get-tuple-element.149), channel_id=1, source_target_pairs={{0,2},{1,3},{2,0},{3,1},{4,6},{5,7},{6,4},{7,5},{8,10},{9,11},{10,... | collective-permute-start | bytes 2359304 | tf_op jit(solution)/shard_map/ppermute | solution.py:317
  681.2 125.1 %collective-permute-start.46 = (f32[2,128,768]{2,1,0:T(8,128)}, f32[2,128,768]{2,1,0:T(8,128)}, u32[]{:S(2)}, u32[]{:S(2)}) collective-permute-start(f32[2,128,768]{2,1,0:T(8,128)} %get-tuple-element.150), channel_id=1, source_target_pairs={{0,8},{8,0},{1,9},{9,1},{2,10},{10,2},{3,11},{11,3},{4,12},{12,4},... | collective-permute-start | bytes 2359304 | tf_op jit(solution)/shard_map/ppermute | solution.py:316
  724.8 82.0 %collective-permute-start.32 = (f32[2,128,768]{2,1,0:T(8,128)}, f32[2,128,768]{2,1,0:T(8,128)}, u32[]{:S(2)}, u32[]{:S(2)}) collective-permute-start(f32[2,128,768]{2,1,0:T(8,128)} %get-tuple-element.129), channel_id=1, source_target_pairs={{0,2},{1,3},{2,0},{3,1},{4,6},{5,7},{6,4},{7,5},{8,10},{9,11},{10,... | collective-permute-start | bytes 2359304 | tf_op jit(solution)/shard_map/ppermute | solution.py:317
  795.6 182.2 %collective-permute-start.14 = (f32[2,2,2,8,128,256]{5,4,3,2,1,0:T(8,128)}, f32[2,2,2,8,128,256]{5,4,3,2,1,0:T(8,128)}, u32[]{:S(2)}, u32[]{:S(2)}) collective-permute-start(f32[2,2,2,8,128,256]{5,4,3,2,1,0:T(8,128)} %get-tuple-element.103), channel_id=1, source_target_pairs={{0,1},{1,0},{2,3},{3,2},{4,5},{5,4},{6,7},{7,6},{8,9},{9,8},{10,11... | collective-permute-start | bytes 25165832 | tf_op jit(solution)/shard_map/ppermute | solution.py:317
  805.1 70.6 %collective-permute-start.62 = (f32[4,352,512]{2,1,0:T(8,128)}, f32[4,352,512]{2,1,0:T(8,128)}, u32[]{:S(2)}, u32[]{:S(2)}) collective-permute-start(f32[4,352,512]{2,1,0:T(8,128)} %get-tuple-element.172), channel_id=1, source_target_pairs={{0,2},{1,3},{2,0},{3,1},{4,6},{5,7},{6,4},{7,5},{8,10},{9,11},{10,... | collective-permute-start | bytes 8650760 | tf_op jit(solution)/shard_map/ppermute | solution.py:317
  806.3 74.4 %collective-permute-start.24 = (f32[2,2,2,4,128,256]{5,4,3,2,1,0:T(8,128)}, f32[2,2,2,4,128,256]{5,4,3,2,1,0:T(8,128)}, u32[]{:S(2)}, u32[]{:S(2)}) collective-permute-start(f32[2,2,2,4,128,256]{5,4,3,2,1,0:T(8,128)} %get-tuple-element.115), channel_id=1, source_target_pairs={{0,1},{1,0},{2,3},{3,2},{4,5},{5,4},{6,7},{7,6},{8,9},{9,8},{10,11... | collective-permute-start | bytes 12582920 | tf_op jit(solution)/shard_map/ppermute | solution.py:317
  806.3 142.0 %collective-permute-start.19 = (f32[2,2,2,4,128,256]{5,4,3,2,1,0:T(8,128)}, f32[2,2,2,4,128,256]{5,4,3,2,1,0:T(8,128)}, u32[]{:S(2)}, u32[]{:S(2)}) collective-permute-start(f32[2,2,2,4,128,256]{5,4,3,2,1,0:T(8,128)} %get-tuple-element.109), channel_id=1, source_target_pairs={{0,1},{1,0},{2,3},{3,2},{4,5},{5,4},{6,7},{7,6},{8,9},{9,8},{10,11... | collective-permute-start | bytes 12582920 | tf_op jit(solution)/shard_map/ppermute | solution.py:317
  806.8 68.5 %collective-permute-start.33 = (f32[2,128,768]{2,1,0:T(8,128)}, f32[2,128,768]{2,1,0:T(8,128)}, u32[]{:S(2)}, u32[]{:S(2)}) collective-permute-start(f32[2,128,768]{2,1,0:T(8,128)} %get-tuple-element.130), channel_id=1, source_target_pairs={{0,8},{8,0},{1,9},{9,1},{2,10},{10,2},{3,11},{11,3},{4,12},{12,4},... | collective-permute-start | bytes 2359304 | tf_op jit(solution)/shard_map/ppermute | solution.py:316
  875.3 71.2 %collective-permute-start.52 = (f32[4,128,1536]{2,1,0:T(8,128)}, f32[4,128,1536]{2,1,0:T(8,128)S(1)}, u32[]{:S(2)}, u32[]{:S(2)}) collective-permute-start(f32[4,128,1536]{2,1,0:T(8,128)} %get-tuple-element.156), channel_id=1, source_target_pairs={{0,4},{1,5},{2,6},{3,7},{4,0},{5,1},{6,2},{7,3},{8,12},{9,13},{10,... | collective-permute-start | bytes 9437192 | tf_op jit(solution)/shard_map/ppermute | solution.py:317
  875.6 71.2 %collective-permute-start.53 = (f32[4,128,1536]{2,1,0:T(8,128)}, f32[4,128,1536]{2,1,0:T(8,128)S(1)}, u32[]{:S(2)}, u32[]{:S(2)}) collective-permute-start(f32[4,128,1536]{2,1,0:T(8,128)} %get-tuple-element.159), channel_id=1, source_target_pairs={{0,2},{1,3},{2,0},{3,1},{4,6},{5,7},{6,4},{7,5},{8,10},{9,11},{10,... | collective-permute-start | bytes 9437192 | tf_op jit(solution)/shard_map/ppermute | solution.py:317
  880.7 96.7 %collective-permute-start.65 = (f32[2,352,512]{2,1,0:T(8,128)S(1)}, f32[2,352,512]{2,1,0:T(8,128)S(1)}, u32[]{:S(2)}, u32[]{:S(2)}) collective-permute-start(f32[2,352,512]{2,1,0:T(8,128)S(1)} %get-tuple-element.176), channel_id=1, source_target_pairs={{0,4},{1,5},{2,6},{3,7},{4,0},{5,1},{6,2},{7,3},{8,12},{9,13},{10,... | collective-permute-start | bytes 4325384 | tf_op jit(solution)/shard_map/ppermute | solution.py:317
  948.3 221.6 %collective-permute-start.51 = (f32[4,128,2560]{2,1,0:T(8,128)}, f32[4,128,2560]{2,1,0:T(8,128)S(1)}, u32[]{:S(2)}, u32[]{:S(2)}) collective-permute-start(f32[4,128,2560]{2,1,0:T(8,128)} %get-tuple-element.153), channel_id=1, source_target_pairs={{0,8},{8,0},{1,9},{9,1},{2,10},{10,2},{3,11},{11,3},{4,12},{12,4},... | collective-permute-start | bytes 15728648 | tf_op jit(solution)/shard_map/ppermute | solution.py:316
  977.4 190.7 %collective-permute-start.60 = (f32[4,352,768]{2,1,0:T(8,128)}, f32[4,352,768]{2,1,0:T(8,128)S(1)}, u32[]{:S(2)}, u32[]{:S(2)}) collective-permute-start(f32[4,352,768]{2,1,0:T(8,128)} %get-tuple-element.166), channel_id=1, source_target_pairs={{0,8},{8,0},{1,9},{9,1},{2,10},{10,2},{3,11},{11,3},{4,12},{12,4},... | collective-permute-start | bytes 12976136 | tf_op jit(solution)/shard_map/ppermute | solution.py:316
  977.9 191.4 %collective-permute-start.61 = (f32[4,352,768]{2,1,0:T(8,128)}, f32[4,352,768]{2,1,0:T(8,128)S(1)}, u32[]{:S(2)}, u32[]{:S(2)}) collective-permute-start(f32[4,352,768]{2,1,0:T(8,128)} %get-tuple-element.169), channel_id=1, source_target_pairs={{0,4},{1,5},{2,6},{3,7},{4,0},{5,1},{6,2},{7,3},{8,12},{9,13},{10,... | collective-permute-start | bytes 12976136 | tf_op jit(solution)/shard_map/ppermute | solution.py:317
  999.9 137.0 %collective-permute-start.17 = (f32[2,8,128,256]{3,2,1,0:T(8,128)}, f32[2,8,128,256]{3,2,1,0:T(8,128)S(1)}, u32[]{:S(2)}, u32[]{:S(2)}) collective-permute-start(f32[2,8,128,256]{3,2,1,0:T(8,128)} %get-tuple-element.183), channel_id=1, source_target_pairs={{0,4},{1,5},{2,6},{3,7},{4,0},{5,1},{6,2},{7,3},{8,12},{9,13},{10,... | collective-permute-start | bytes 6291464 | tf_op jit(solution)/shard_map/ppermute | solution.py:317
  1000.2 137.0 %collective-permute-start.15 = (f32[2,8,128,256]{3,2,1,0:T(8,128)S(1)}, f32[2,8,128,256]{3,2,1,0:T(8,128)}, u32[]{:S(2)}, u32[]{:S(2)}) collective-permute-start(f32[2,8,128,256]{3,2,1,0:T(8,128)S(1)} %get-tuple-element.184), channel_id=1, source_target_pairs={{0,2},{1,3},{2,0},{3,1},{4,6},{5,7},{6,4},{7,5},{8,10},{9,11},{10,... | collective-permute-start | bytes 6291464 | tf_op jit(solution)/shard_map/ppermute | solution.py:317
  1210.1 57.4 %collective-permute-start.64 = (f32[2,352,768]{2,1,0:T(8,128)}, f32[2,352,768]{2,1,0:T(8,128)}, u32[]{:S(2)}, u32[]{:S(2)}) collective-permute-start(f32[2,352,768]{2,1,0:T(8,128)} %get-tuple-element.175), channel_id=1, source_target_pairs={{0,8},{8,0},{1,9},{9,1},{2,10},{10,2},{3,11},{11,3},{4,12},{12,4},... | collective-permute-start | bytes 6488072 | tf_op jit(solution)/shard_map/ppermute | solution.py:316
  1217.6 110.8 %collective-permute-start.54 = (f32[2,128,2560]{2,1,0:T(8,128)}, f32[2,128,2560]{2,1,0:T(8,128)}, u32[]{:S(2)}, u32[]{:S(2)}) collective-permute-start(f32[2,128,2560]{2,1,0:T(8,128)} %get-tuple-element.161), channel_id=1, source_target_pairs={{0,2},{1,3},{2,0},{3,1},{4,6},{5,7},{6,4},{7,5},{8,10},{9,11},{10,... | collective-permute-start | bytes 7864328 | tf_op jit(solution)/shard_map/ppermute | solution.py:317
  1235.5 96.9 %collective-permute-start.38 = (f32[8,128,512]{2,1,0:T(8,128)}, f32[8,128,512]{2,1,0:T(8,128)S(1)}, u32[]{:S(2)}, u32[]{:S(2)}) collective-permute-start(f32[8,128,512]{2,1,0:T(8,128)} %get-tuple-element.133), channel_id=1, source_target_pairs={{0,1},{1,0},{2,3},{3,2},{4,5},{5,4},{6,7},{7,6},{8,9},{9,8},{10,11... | collective-permute-start | bytes 6291464 | tf_op jit(solution)/shard_map/ppermute | solution.py:317
  1266.1 61.5 %collective-permute-start.49 = (f32[128,768]{1,0:T(8,128)S(1)}, f32[128,768]{1,0:T(8,128)S(1)}, u32[]{:S(2)}, u32[]{:S(2)}) collective-permute-start(f32[128,768]{1,0:T(8,128)S(1)} %copy-done.31), channel_id=1, source_target_pairs={{0,2},{1,3},{2,0},{3,1},{4,6},{5,7},{6,4},{7,5},{8,10},{9,11},{10,... | collective-permute-start | bytes 1179656 | tf_op jit(solution)/shard_map/ppermute | solution.py:317
  1267.5 60.5 %collective-permute-start.35 = (f32[128,768]{1,0:T(8,128)S(1)}, f32[128,768]{1,0:T(8,128)S(1)}, u32[]{:S(2)}, u32[]{:S(2)}) collective-permute-start(f32[128,768]{1,0:T(8,128)S(1)} %copy-done.30), channel_id=1, source_target_pairs={{0,4},{1,5},{2,6},{3,7},{4,0},{5,1},{6,2},{7,3},{8,12},{9,13},{10,... | collective-permute-start | bytes 1179656 | tf_op jit(solution)/shard_map/ppermute | solution.py:317
  1277.6 58.4 %collective-permute-start.36 = (f32[128,768]{1,0:T(8,128)S(1)}, f32[128,768]{1,0:T(8,128)S(1)}, u32[]{:S(2)}, u32[]{:S(2)}) collective-permute-start(f32[128,768]{1,0:T(8,128)S(1)} %copy-done.29), channel_id=1, source_target_pairs={{0,2},{1,3},{2,0},{3,1},{4,6},{5,7},{6,4},{7,5},{8,10},{9,11},{10,... | collective-permute-start | bytes 1179656 | tf_op jit(solution)/shard_map/ppermute | solution.py:317
  (90 other events, 2989.8 us)
